TPU v7x, 32 devices: a whole 2x2x4 slice. The times are simulated.
32 devices in a mesh: groups: 2 (over y), det: 4 (over z), tm: 4 (over x, core).
Axes of the slice: x: 2, y: 2, z: 4, core: 2. Of those that a mesh axis runs over, the one named last changes fastest.
Arguments:
- tod: float32 [2048, 16384], P(('groups', 'det'), 'tm'), parts along dimension 0, may hold values from -8 to 8
- gain_knots: float32 [2048, 64], P(('groups', 'det')), parts along dimension 0, may hold values from 0.25 to 1.75
- intervals: int32 [32768], P(('groups', 'tm')), parts along dimension 0, may hold values from 0 to 62, never falling along the last dimension, each value on 1 to 1040 neighbouring positions
- fraction: float32 [32768], P(('groups', 'tm')), parts along dimension 0, may hold values from 0 to 1
- azimuth: int32 [32768], P(('groups', 'tm')), parts along dimension 0, may hold values from 0 to 447
- mode_index: int32 [32], P(('groups', 'tm')), parts along dimension 0, may hold values from 0 to 1
- mode_bank: float32 [2, 1024, 512], P(None, 'det'), may hold values from -0.1875 to 0.1875
- mode_mix: float32 [2, 512, 512], replicated, may hold values from -0.2 to 0.2
Outputs:
- filtered: float32 [2048, 16384], P(('groups', 'det'), 'tm'), parts along dimension 0
There are 2 independent parts, one for each index of `groups`. A program takes and returns all parts, laid end to end along the dimension named above; an argument that names none is the same for every part. Nothing has to cross between parts.
Inputs may be any that keep to these rules, and one draw needn't show every extreme that they name: `intervals`: never falls along time; every interval from 0 to 62 holds at least one sample.
All inputs are finite; a program needn't handle non-finite values.
Results may differ from a plain program's by a relative error of at most 0.000068.
Values sent between devices are 32-bit elements; how exact they have to be, the bound alone decides.
No kernel may reach another device: no remote copies, remote signals or barrier semaphores. Data moves between devices by JAX's collectives and lax.ppermute only.
A program may use at most 128 MiB of HBM per device.

v0:
```python
import jax
import jax.numpy as jnp
from jax import lax
from jax.sharding import PartitionSpec as P

BLOCK = 1024
NBIN = 512


def on_device(tod, gain_knots, intervals, fraction, azimuth, mode_index, mode_bank, mode_mix):
    precise = lax.Precision.HIGHEST
    det_rows, samples = tod.shape
    knot_row = lax.broadcasted_iota(jnp.int32, (gain_knots.shape[1], samples), 0)
    spread = jnp.where(knot_row == intervals[None, :], 1.0 - fraction[None, :], 0.0)
    spread = spread + jnp.where(knot_row == intervals[None, :] + 1, fraction[None, :], 0.0)
    calibrated = tod * jnp.dot(gain_knots, spread, precision=precise)
    nblocks = samples // BLOCK
    blocks = calibrated.reshape(det_rows, nblocks, BLOCK)
    selected = jnp.take(mode_bank, mode_index, axis=0)
    mixing = jnp.take(mode_mix, mode_index, axis=0)
    partial_amps = jnp.einsum("kdm,dkt->kmt", selected, blocks, precision=precise)
    share = lax.psum_scatter(partial_amps, "det", scatter_dimension=2, tiled=True)
    coef_share = share + jnp.einsum("kmn,knt->kmt", mixing, share, precision=precise)
    coef = lax.all_gather(coef_share, "det", axis=2, tiled=True)
    removed = jnp.einsum("kdm,kmt->dkt", selected, coef, precision=precise)
    cleaned = (blocks - removed).reshape(det_rows, samples)
    onehot = (lax.broadcasted_iota(jnp.int32, (NBIN, samples), 0) == azimuth[None, :]).astype(
        tod.dtype
    )
    fit_part = lax.dot_general(cleaned, onehot, (((1,), (1,)), ((), ())), precision=precise)
    count_part = jnp.sum(onehot, axis=1)
    fit, counts = lax.psum((fit_part, count_part), "tm")
    template = fit / jnp.maximum(counts, 1.0)[None, :]
    return cleaned - jnp.dot(template, onehot, precision=precise)


def solution(mesh):
    placed = (
        P(("groups", "det"), "tm"),
        P(("groups", "det"), None),
        P(("groups", "tm")),
        P(("groups", "tm")),
        P(("groups", "tm")),
        P(("groups", "tm")),
        P(None, "det", None),
        P(),
    )
    return jax.shard_map(
        on_device, mesh=mesh, in_specs=placed, out_specs=P(("groups", "det"), "tm"), check_vma=False
    )
```

profile of v0, /device:TPU:0, one launch (start us, length us, event | category | flops | bytes accessed | tf_op | source)
XLA Modules:
  0.0 418.7 jit_solution(13190840496527715943)
XLA Ops:
  6.5 0.0 copy-start
  6.5 0.0 reduce-scatter.2.cloned.1.call-start
  6.5 0.8 compare_select_fusion
  7.3 0.7 compare_and_fusion
  8.0 0.0 copy-start.7
  8.0 0.0 copy-start.6
  8.0 0.0 copy-start.4
  8.1 5.7 %copy.14 = f32[256,4096]{0,1:T(8,128)} copy(f32[256,4096]{1,0:T(8,128)} %param.8) | data formatting | bytes 8388608 | tf_op args[0]
  13.7 0.0 copy-done.7
  13.7 0.0 copy-start.5
  13.8 0.0 copy-done.6
  13.8 0.0 copy-done.4
  13.8 2.0 gather_fusion
  15.8 0.0 copy-done.5
  15.8 0.0 copy-start.2
  15.8 5.6 %fusion.3 = f32[256,4096]{0,1:T(8,128)S(1)} fusion(f32[256,4096]{0,1:T(8,128)} %copy.14, f32[256,64]{0,1:T(8,128)S(1)} %copy-done.5, f32[4096]{0:T(1024)S(1)} %copy-done.6, s32[4096]{0:T(1024)S(1)} %broadcast_add_fusion, f32[4096]{0:T(1024)S(1)} %broadcast_subtract_fusion, s32[4096]{0:T(1024)S(1)} %copy-done.7), kind=kOutput, calls=%fused_computation.8 | convolution fusion | flops 807665664 | bytes 8519680 | tf_op jit(solution)/shard_map/dot_general | solution.py:16
  21.4 0.0 copy-start.1
  21.4 2.0 copy-done.1
  23.4 0.0 copy-done.2
  23.4 15.6 %fusion.11 = f32[4,512,1024]{2,1,0:T(8,128)} fusion(f32[256,4,1024]{0,2,1:T(8,128)S(1)} %bitcast.13, f32[4,256,512]{2,1,0:T(8,128)S(1)} %copy-done.2, pred[4]{0:T(512)(128)(4,1)S(1)} %compare_and_fusion), kind=kOutput, calls=%fused_computation.17 | convolution fusion | flops 6442975232 | bytes 14680068 | tf_op jit(solution)/shard_map/kdm,dkt->kmt/dot_general | solution.py:21
  39.1 0.0 reduce-scatter.2.cloned.1.call-update
  39.1 0.2 all-gather.2.cloned.1.call-start
  39.3 0.0 copy-done
  39.3 2.8 gather_fusion.1
  42.1 144.5 %reduce-scatter.2.cloned.1.call-done = f32[4,512,256]{2,1,0:T(8,128)} async-done(((f32[4,512,1024]{2,1,0:T(8,128)}), f32[4,512,256]{2,1,0:T(8,128)}) %reduce-scatter.2.cloned.1.call-update) | async-done | bytes 2097168 | tf_op jit(solution)/shard_map/reduce_scatter | solution.py:22
  186.6 8.7 %fusion.13 = f32[4,512,256]{2,1,0:T(8,128)} fusion(f32[4,512,256]{2,1,0:T(8,128)} %reduce-scatter.2.cloned.1.call-done, f32[4,512,512]{2,1,0:T(8,128)} %gather_fusion.1, pred[4]{0:T(512)(128)(4,1)S(1)} %compare_and_fusion), kind=kOutput, calls=%fused_computation.19 | convolution fusion | flops 3222798336 | bytes 8388612 | tf_op jit(solution)/shard_map/kmn,knt->kmt/dot_general | solution.py:23
  195.3 0.0 all-gather.2.cloned.1.call-update
  195.3 0.0 copy-start.8
  195.3 0.0 all-reduce.2.cloned.1.call-start
  195.4 150.3 %all-gather.2.cloned.1.call-done = f32[4,512,1024]{2,1,0:T(8,128)} async-done(((f32[4,512,256]{2,1,0:T(8,128)}), f32[4,512,1024]{2,1,0:T(8,128)}) %all-gather.2.cloned.1.call-update) | async-done | bytes 8388624 | tf_op jit(solution)/shard_map/all_gather | solution.py:24
  345.7 17.4 %bitcast_subtract_fusion = f32[256,4,1024]{0,2,1:T(8,128)S(1)} fusion(f32[256,4,1024]{0,2,1:T(8,128)} %bitcast.14, f32[4,512,1024]{2,1,0:T(8,128)} %all-gather.2.cloned.1.call-done, f32[4,256,512]{2,1,0:T(8,128)} %gather_fusion, pred[4]{0:T(512)(128)(4,1)S(1)} %compare_and_fusion), kind=kOutput, calls=%fused_computation.9 | convolution fusion | flops 6444023808 | bytes 18874372 | tf_op jit(solution)/shard_map/kdm,kmt->dkt/dot_general | solution.py:25
  363.1 0.0 copy-start.3
  363.1 2.0 copy-done.3
  365.1 0.0 copy-done.8
  365.1 8.2 %fusion.1 = f32[256,512]{1,0:T(8,128)} fusion(f32[256,4096]{0,1:T(8,128)S(1)} %bitcast.15, s32[4096]{0:T(1024)S(1)} %copy-done.8), kind=kOutput, calls=%fused_computation.5 | convolution fusion | flops 6444548096 | bytes 4734976 | tf_op jit(solution)/shard_map/dot_general | solution.py:30
  373.2 0.0 all-reduce.2.cloned.1.call-update
  373.2 0.9 convert_reduce_fusion
  374.2 7.1 %psum.15 = f32[512]{0:T(512)S(1)} all-reduce(f32[512]{0:T(512)S(1)} %convert_reduce_fusion), channel_id=1, replica_groups=mesh['groups'=2,'det'=4,'tm'=4] {'tm'}, use_global_device_ids=true, to_apply=%region_3.4 | all-reduce | flops 512 | bytes 4096 | tf_op jit(solution)/shard_map/psum | solution.py:32
  381.3 5.6 %copy.18 = f32[256,4096]{1,0:T(8,128)} copy(f32[256,4096]{0,1:T(8,128)} %bitcast.16) | data formatting | bytes 8388608 | tf_op jit(solution)/shard_map/reshape | solution.py:26
  386.9 18.0 %all-reduce.2.cloned.1.call-done = f32[256,512]{1,0:T(8,128)} async-done(((f32[256,512]{1,0:T(8,128)}), f32[256,512]{1,0:T(8,128)}) %all-reduce.2.cloned.1.call-update) | async-done | bytes 524304 | tf_op jit(solution)/shard_map/psum | solution.py:32
  405.0 7.2 %fusion.2 = f32[256,4096]{1,0:T(8,128)} fusion(f32[256,4096]{1,0:T(8,128)} %copy.18, s32[4096]{0:T(1024)S(1)} %copy-done.8, f32[256,512]{1,0:T(8,128)} %all-reduce.2.cloned.1.call-done, f32[512]{0:T(512)S(1)} %broadcast_maximum_fusion), kind=kOutput, calls=%fused_computation.6 | convolution fusion | flops 6445727744 | bytes 8931328 | tf_op jit(solution)/shard_map/dot_general | solution.py:34
  (4 shorter events, 0.0 us)
Async XLA Ops:
  6.5 32.8 %copy-start = (f32[2,512,512]{2,1,0:T(8,128)S(1)}, f32[2,512,512]{2,1,0:T(8,128)}, u32[]{:S(2)}) copy-start(f32[2,512,512]{2,1,0:T(8,128)} %param.15) | copy-start | bytes 6291460
  6.5 180.0 %reduce-scatter.2.cloned.1.call-start = ((), (), s32[]{:S(2)}) async-start(), calls=%async_computation.1 | async-start | bytes 10485760 | tf_op jit(solution)/shard_map/reduce_scatter | solution.py:22
  8.0 5.7 %copy-start.7 = (s32[4096]{0:T(1024)S(1)}, s32[4096]{0:T(1024)}, u32[]{:S(2)}) copy-start(s32[4096]{0:T(1024)} %param.10) | copy-start | bytes 49156
  8.0 5.7 %copy-start.6 = (f32[4096]{0:T(1024)S(1)}, f32[4096]{0:T(1024)}, u32[]{:S(2)}) copy-start(f32[4096]{0:T(1024)} %param.11) | copy-start | bytes 49156
  8.0 5.7 %copy-start.4 = (f32[2,256,512]{2,1,0:T(8,128)S(1)}, f32[2,256,512]{2,1,0:T(8,128)}, u32[]{:S(2)}) copy-start(f32[2,256,512]{2,1,0:T(8,128)} %param.14) | copy-start | bytes 3145732
  13.7 2.1 copy-start.5
  15.8 7.6 %copy-start.2 = (f32[4,256,512]{2,1,0:T(8,128)S(1)}, f32[4,256,512]{2,1,0:T(8,128)}, u32[]{:S(2)}) copy-start(f32[4,256,512]{2,1,0:T(8,128)} %gather_fusion) | copy-start | bytes 6291460
  21.4 2.0 copy-start.1
  39.1 306.6 %all-gather.2.cloned.1.call-start = ((), (), s32[]{:S(2)}) async-start(), calls=%async_computation.2 | async-start | bytes 10485760 | tf_op jit(solution)/shard_map/all_gather | solution.py:24
  195.3 169.8 %copy-start.8 = (s32[4096]{0:T(1024)S(1)}, s32[4096]{0:T(1024)}, u32[]{:S(2)}) copy-start(s32[4096]{0:T(1024)} %param.12) | copy-start | bytes 49156
  195.3 209.7 %all-reduce.2.cloned.1.call-start = ((), (), s32[]{:S(2)}) async-start(), calls=%async_computation.3 | async-start | bytes 1048576 | tf_op jit(solution)/shard_map/psum | solution.py:32
  363.1 2.0 copy-start.3
Sparse Core Ops, SparseCore 0:
  39.2 147.3 reduce-scatter.1
  195.4 150.2 all-gather.1
  373.4 31.5 all-reduce.1
where the time goes:
time: 419 us
  waiting for transfers between devices  313 us (75%)
  matrix products  62.7 us (15%)
  local copies, waits for them, and re-layouts  20.2 us (5%)
  between operations  13.2 us (3%)
  blocking collectives  7.13 us (2%)
    all_gather x1, waiting for transfers between devices, on_device(): coef = lax.all_gather(coef_share, 'det', axis=2, tiled=True)  150 us
    reduce_scatter x1, waiting for transfers between devices, on_device(): lax.psum_scatter(partial_amps, 'det', scatter_dimension=2, tiled=True)  144 us
    psum x1, waiting for transfers between devices, on_device(): fit, counts = lax.psum((fit_part, count_part), 'tm')  18 us
    dot_general x1, matrix products, on_device(): removed = jnp.einsum('kdm,kmt->dkt', selected, coef, precision=precise)  17.4 us
    dot_general x1, matrix products, on_device(): jnp.einsum('kdm,dkt->kmt', selected, blocks, precision=precise)  15.6 us
    unnamed x19, local copies, waits for them, and re-layouts  9.74 us
    dot_general x1, matrix products, on_device(): jnp.einsum('kmn,knt->kmt', mixing, share, precision=precise)  8.69 us
  transfers between devices with their start and end apart: 3, of which 3 were waited for; matrix products, arithmetic and copies ran while one was open for 2% of the time, Pallas kernels for 0%

commit v1 on v0

--- a/solution.py
+++ b/solution.py
@@ -1,13 +1,17 @@
+import functools
 import jax
 import jax.numpy as jnp
 from jax import lax
+from jax.experimental import pallas as pl
+from jax.experimental.pallas import tpu as pltpu
 from jax.sharding import PartitionSpec as P
 
 BLOCK = 1024
 NBIN = 512
-
-
-def on_device(tod, gain_knots, intervals, fraction, azimuth, mode_index, mode_bank, mode_mix):
+PIECES = ((0, 256), (512, 512), (256, 256))
+
+
+def gathered_sums(tod, gain_knots, intervals, fraction, azimuth, mode_index, mode_bank, mode_mix):
     precise = lax.Precision.HIGHEST
     det_rows, samples = tod.shape
     knot_row = lax.broadcasted_iota(jnp.int32, (gain_knots.shape[1], samples), 0)
@@ -34,6 +38,286 @@
     return cleaned - jnp.dot(template, onehot, precision=precise)
 
 
+def halves(x):
+    high = x.astype(jnp.bfloat16)
+    return high, (x - high.astype(jnp.float32)).astype(jnp.bfloat16)
+
+
+def dot(a, b, contract=((1,), (0,))):
+    return lax.dot_general(a, b, (contract, ((), ())), preferred_element_type=jnp.float32)
+
+
+def dot3(a, b):
+    return dot(a[0], b[0]) + (dot(a[0], b[1]) + dot(a[1], b[0]))
+
+
+def calibrate_kernel(count, me_ref, gain_ref, *refs):
+    gain_high, gain_low = halves(gain_ref[...])
+    gains = jnp.concatenate([gain_high, gain_high, gain_low, gain_low], axis=0)
+    knots = gain_ref.shape[0]
+    for n in range(count):
+        tod_ref, where_ref, share_ref = refs[3 * n : 3 * n + 3]
+        knot_row = lax.broadcasted_iota(jnp.int32, (knots, tod_ref.shape[1]), 0)
+        where, share = where_ref[...], share_ref[...]
+        spread = jnp.where(knot_row == where, 1.0 - share, 0.0)
+        spread = spread + jnp.where(knot_row == where + 1, share, 0.0)
+        high, low = halves(spread)
+        spreads = jnp.concatenate([high, low, high, low], axis=0)
+        refs[3 * count + n][...] = tod_ref[...] * dot(gains, spreads, ((0,), (0,)))
+
+
+def calibrate(ring, me, tod, gains, where, share, pieces):
+    rows = tod.shape[0]
+    specs, operands = [], []
+    for shift, start, width in pieces:
+        per_block, offset = BLOCK // width, start // width
+
+        def at(i, me_ref, shift=shift, per_block=per_block, offset=offset):
+            return 0, lax.rem(me_ref[0] + shift, ring) * per_block + offset
+
+        specs += [pl.BlockSpec((rows, width), at)] + [pl.BlockSpec((1, width), at)] * 2
+        operands += [tod, where, share]
+    return pl.pallas_call(
+        functools.partial(calibrate_kernel, len(pieces)),
+        out_shape=[jax.ShapeDtypeStruct((rows, width), jnp.float32) for _, _, width in pieces],
+        grid_spec=pltpu.PrefetchScalarGridSpec(
+            num_scalar_prefetch=1,
+            grid=(1,),
+            in_specs=[pl.BlockSpec(gains.shape, lambda i, me_ref: (0, 0))] + specs,
+            out_specs=[pl.BlockSpec((rows, width), lambda i, me_ref: (0, 0)) for _, _, width in pieces],
+        ),
+        cost_estimate=pl.CostEstimate(
+            flops=2 * rows * 256 * sum(w for _, _, w in pieces),
+            bytes_accessed=8 * rows * sum(w for _, _, w in pieces),
+            transcendentals=0,
+        ),
+    )(me, gains, *operands)
+
+
+def modes_kernel(ring, shares, at_ref, bank_ref, mix_ref, first_high, first_low, second_high, second_low, modes):
+    rows = bank_ref.shape[2]
+    me, part = at_ref[0], at_ref[2]
+    other = jnp.bitwise_xor(me, lax.rem(me - pl.program_id(0) + ring, ring))
+    z_slot = (other // 2) + 2 * lax.rem(other, 2)
+    for share in range(shares):
+        flip = jnp.bitwise_xor(part, share)
+        slot = z_slot + ring * (lax.rem(flip // 2, 2) + 2 * (flip // 4) + 4 * lax.rem(flip, 2))
+        modes[pl.ds(share * rows, rows), :] = bank_ref[slot, 0]
+    u = modes[...]
+    mixed = u + dot3(halves(u), halves(mix_ref[0]))
+    first_high[...], first_low[...] = halves(u.T)
+    second_high[...], second_low[...] = halves(mixed)
+
+
+def prepare_modes(ring, shares, at, banks, mode_mix):
+    _, _, rows, m = banks.shape
+    det_rows = rows * shares
+    first = pl.BlockSpec((m, det_rows), lambda s, at_ref: (0, s))
+    second = pl.BlockSpec((det_rows, m), lambda s, at_ref: (s, 0))
+    total = ring * det_rows
+    return pl.pallas_call(
+        functools.partial(modes_kernel, ring, shares),
+        out_shape=[jax.ShapeDtypeStruct((m, total), jnp.bfloat16)] * 2
+        + [jax.ShapeDtypeStruct((total, m), jnp.bfloat16)] * 2,
+        grid_spec=pltpu.PrefetchScalarGridSpec(
+            num_scalar_prefetch=1,
+            grid=(ring,),
+            in_specs=[
+                pl.BlockSpec((banks.shape[0], 1, rows, m), lambda s, at_ref: (0, at_ref[1], 0, 0)),
+                pl.BlockSpec((1, m, m), lambda s, at_ref: (at_ref[1], 0, 0)),
+            ],
+            out_specs=[first, first, second, second],
+            scratch_shapes=[pltpu.VMEM((det_rows, m), jnp.float32)],
+        ),
+        cost_estimate=pl.CostEstimate(
+            flops=6 * total * m * m, bytes_accessed=12 * total * m, transcendentals=0
+        ),
+    )(at, banks, mode_mix)
+
+
+def filter_kernel(ring, first_high, first_low, second_high, second_low, *refs):
+    rows = refs[0].shape[0]
+    data = halves(jnp.concatenate([refs[s][...] for s in range(ring)], axis=0))
+    amps = dot3((first_high[...], first_low[...]), data)
+    amps = halves(amps)
+    for s in range(ring):
+        block = pl.ds(s * rows, rows)
+        refs[ring + s][...] = dot3((second_high[block, :], second_low[block, :]), amps)
+
+
+def common_mode(ring, modes, arrived):
+    rows, width = arrived[0].shape
+    m, total = modes[0].shape
+    tile = min(width, 256)
+    whole = [pl.BlockSpec((m, total), lambda i: (0, 0))] * 2 + [pl.BlockSpec((total, m), lambda i: (0, 0))] * 2
+    column = pl.BlockSpec((rows, tile), lambda i: (0, i))
+    return pl.pallas_call(
+        functools.partial(filter_kernel, ring),
+        out_shape=[jax.ShapeDtypeStruct((rows, width), jnp.float32)] * ring,
+        grid=(width // tile,),
+        in_specs=whole + [column] * ring,
+        out_specs=[column] * ring,
+        cost_estimate=pl.CostEstimate(
+            flops=12 * total * m * width, bytes_accessed=8 * total * width, transcendentals=0
+        ),
+    )(*modes, *arrived)
+
+
+def fit_kernel(ring, more, at_ref, *refs):
+    data, back, azimuth_ref = refs[:ring], refs[ring : 2 * ring], refs[2 * ring]
+    old = refs[2 * ring + 1 : 2 * ring + 3] if more else ()
+    cleaned_ref, fit_ref = refs[-2:]
+    step = pl.program_id(0)
+
+    @pl.when(step == 0)
+    def _():
+        fit_ref[...] = old[1][...] if more else jnp.zeros_like(fit_ref)
+
+    for s in range(ring):
+
+        @pl.when(step == s)
+        def _():
+            cleaned_ref[...] = data[s][...] - back[s][...]
+
+    rows = cleaned_ref.shape[0]
+    cleaned = jnp.concatenate(halves(cleaned_ref[...]), axis=0)
+    bins = lax.broadcasted_iota(jnp.int32, (fit_ref.shape[1], cleaned_ref.shape[1]), 0)
+    onehot = (bins == azimuth_ref[...]).astype(jnp.float32).astype(jnp.bfloat16)
+    sums = dot(cleaned, onehot, ((1,), (1,)))
+    fit_ref[...] += sums[:rows] + sums[rows:]
+
+
+def fit_piece(ring, at, start, data, back, azimuth, old):
+    rows, width = data[0].shape
+    samples = azimuth.shape[1]
+    per_block, offset = BLOCK // width, start // width
+
+    def where(s, at_ref):
+        return 0, lax.rem(at_ref[0] + s, ring) * per_block + offset
+
+    full = pl.BlockSpec((rows, width), lambda s, at_ref: (0, 0))
+    sums = pl.BlockSpec((rows, NBIN), lambda s, at_ref: (0, 0))
+    more = old is not None
+    return pl.pallas_call(
+        functools.partial(fit_kernel, ring, more),
+        out_shape=[
+            jax.ShapeDtypeStruct((rows, samples), jnp.float32),
+            jax.ShapeDtypeStruct((rows, NBIN), jnp.float32),
+        ],
+        grid_spec=pltpu.PrefetchScalarGridSpec(
+            num_scalar_prefetch=1,
+            grid=(ring,),
+            in_specs=[full] * (2 * ring)
+            + [pl.BlockSpec((1, width), where)]
+            + ([pl.BlockSpec(memory_space=pl.ANY), sums] if more else []),
+            out_specs=[pl.BlockSpec((rows, width), where), sums],
+        ),
+        input_output_aliases={2 * ring + 2: 0} if more else {},
+        cost_estimate=pl.CostEstimate(
+            flops=4 * ring * rows * width * NBIN, bytes_accessed=12 * ring * rows * width, transcendentals=0
+        ),
+    )(at, *data, *back, azimuth, *(old if more else ()))
+
+
+def template_kernel(at_ref, cleaned_ref, azimuth_ref, own_ref, mate_ref, counts_ref, out_ref, both_ref):
+    half = own_ref.shape[0]
+    core = at_ref[3]
+
+    @pl.when(pl.program_id(0) == 0)
+    def _():
+        counts = jnp.maximum(counts_ref[...], 1.0)
+        for ref, side in ((own_ref, core), (mate_ref, 1 - core)):
+            first = pl.multiple_of(side * half, half)
+            high, low = halves(ref[...] / counts)
+            both_ref[pl.ds(first, half), :] = high
+            both_ref[pl.ds(2 * half + first, half), :] = low
+
+    bins = lax.broadcasted_iota(jnp.int32, (both_ref.shape[1], cleaned_ref.shape[1]), 0)
+    onehot = (bins == azimuth_ref[...]).astype(jnp.float32).astype(jnp.bfloat16)
+    template = dot(both_ref[...], onehot)
+    out_ref[...] = cleaned_ref[...] - (template[: 2 * half] + template[2 * half :])
+
+
+def remove_template(at, cleaned, azimuth, own, mate, counts):
+    rows, samples = cleaned.shape
+    tile = 512
+    column = pl.BlockSpec((rows, tile), lambda i, at_ref: (0, i))
+    whole = pl.BlockSpec(own.shape, lambda i, at_ref: (0, 0))
+    return pl.pallas_call(
+        template_kernel,
+        out_shape=jax.ShapeDtypeStruct((rows, samples), jnp.float32),
+        grid_spec=pltpu.PrefetchScalarGridSpec(
+            num_scalar_prefetch=1,
+            grid=(samples // tile,),
+            in_specs=[
+                column,
+                pl.BlockSpec((1, tile), lambda i, at_ref: (0, i)),
+                whole,
+                whole,
+                pl.BlockSpec(counts.shape, lambda i, at_ref: (0, 0)),
+            ],
+            out_specs=column,
+            scratch_shapes=[pltpu.VMEM((2 * rows, own.shape[1]), jnp.bfloat16)],
+        ),
+        cost_estimate=pl.CostEstimate(
+            flops=4 * rows * samples * NBIN, bytes_accessed=8 * rows * samples, transcendentals=0
+        ),
+    )(at, cleaned, azimuth, own, mate, counts)
+
+
+def exchanged_blocks(ring, shares, tod, gain_knots, intervals, fraction, azimuth, mode_index, mode_bank, mode_mix):
+    det_rows, samples = tod.shape
+    me = lax.axis_index("det")
+    tm = lax.axis_index("tm")
+    part_of = lax.axis_index("groups") * lax.axis_size("tm") + tm
+    core = lax.rem(tm, 2)
+    which = lax.dynamic_index_in_dim(mode_index, me, 0, False)
+    me_only = jnp.full((1,), me, jnp.int32)
+    at = jnp.stack([me, which, part_of, core])
+
+    def send(array, shift):
+        return lax.ppermute(array, "det", [(i, (i + shift) % ring) for i in range(ring)])
+
+    def swap(array, axis, bit):
+        return lax.ppermute(array, axis, [(i, i ^ bit) for i in range(lax.axis_size(axis))])
+
+    gains = gain_knots.T
+    where, share = intervals[None, :], fraction[None, :]
+    azimuth = azimuth[None, :]
+    data, arrived = {}, {}
+    order = [[(s, start, width) for s in (1, 2, 3)] for start, width in PIECES]
+    order[-1] += [(0, start, width) for start, width in PIECES]
+    for pieces in order:
+        blocks = calibrate(ring, me_only, tod, gains, where, share, pieces)
+        for (s, start, width), block in zip(pieces, blocks):
+            data[s, start] = block
+            arrived[s, start] = send(block, s) if s else block
+
+    rows = det_rows // shares
+    banks = lax.dynamic_slice_in_dim(mode_bank, part_of * rows, rows, 1)[None]
+    for axis, bit in (("det", 2), ("det", 1), ("tm", 2), ("groups", 1), ("tm", 1)):
+        banks = jnp.concatenate([banks, swap(banks, axis, bit)], axis=0)
+    modes = prepare_modes(ring, shares, at, banks, mode_mix)
+
+    counts = jnp.sum((lax.broadcasted_iota(jnp.int32, (NBIN, samples), 0) == azimuth).astype(jnp.float32), axis=1)
+    counts = jnp.broadcast_to(counts[None, :], (8, NBIN))
+    for bit in (1, 2):
+        counts = counts + swap(counts, "tm", bit)
+
+    state = None
+    for start, width in PIECES:
+        removed = common_mode(ring, modes, [arrived[s, start] for s in range(ring)])
+        back = [send(removed[s], -s) if s else removed[s] for s in range(ring)]
+        state = fit_piece(ring, at, start, [data[s, start] for s in range(ring)], back, azimuth, state)
+    cleaned, fit = state
+    half = det_rows // 2
+    own = lax.dynamic_slice_in_dim(fit, core * half, half, 0)
+    own = own + swap(lax.dynamic_slice_in_dim(fit, (1 - core) * half, half, 0), "tm", 1)
+    own = own + swap(own, "tm", 2)
+    mate = swap(own, "tm", 1)
+    return remove_template(at, cleaned, azimuth, own, mate, counts[:1])
+
+
 def solution(mesh):
     placed = (
         P(("groups", "det"), "tm"),
@@ -45,6 +329,15 @@
         P(None, "det", None),
         P(),
     )
+    ring = mesh.shape["det"]
+    shares = mesh.shape["groups"] * mesh.shape["tm"]
+
+    def on_device(tod, gain_knots, intervals, fraction, azimuth, mode_index, mode_bank, mode_mix):
+        args = (tod, gain_knots, intervals, fraction, azimuth, mode_index, mode_bank, mode_mix)
+        if ring == 4 and mode_index.shape[0] == ring and shares == 8 and tod.shape[0] % (16 * shares) == 0:
+            return exchanged_blocks(ring, shares, *args)
+        return gathered_sums(*args)
+
     return jax.shard_map(
         on_device, mesh=mesh, in_specs=placed, out_specs=P(("groups", "det"), "tm"), check_vma=False
     )

time: 419 us -> 282 us (0.67)
  waiting for transfers between devices: 313 us -> 134 us
  starting transfers between devices: 0.27 us -> 66.7 us
  Pallas kernels: 0 us -> 63.9 us
  matrix products: 62.7 us -> 0 us
  between operations: 13.2 us -> 0.28 us
  local copies, waits for them, and re-layouts: 20.2 us -> 12.9 us
  blocking collectives: 7.13 us -> 0 us
    all_gather x1 -> x0, waiting for transfers between devices: 150 us -> none  [on_device(): coef = lax.all_gather(coef_share, 'det', axis=2, tiled=True)]
    reduce_scatter x1 -> x0, waiting for transfers between devices: 144 us -> none  [on_device(): lax.psum_scatter(partial_amps, 'det', scatter_dimension=2, tiled=True)]
    ppermute x0 -> x28, waiting for transfers between devices: none -> 134 us  [the longest x18 82.1 us: send(): lax.ppermute(array, 'det', [(i, (i + shift) % ring) for i in range(ring)])]
    ppermute x0 -> x28, starting transfers between devices: none -> 66.7 us  [the longest x18 55.8 us: send(): lax.ppermute(array, 'det', [(i, (i + shift) % ring) for i in range(ring)])]
    pallas_call x0 -> x11, Pallas kernels: none -> 63.9 us  [the longest x3 23.5 us: common_mode(): pl.pallas_call(functools.partial(filter_kernel, ring), out_shape=[jax.Sha...]
    dot_general x6 -> x0, matrix products: 62.7 us -> none  [the longest x1 17.4 us: on_device(): removed = jnp.einsum('kdm,kmt->dkt', selected, coef, precision=precise)]
    psum x1 -> x0, waiting for transfers between devices: 18 us -> none  [on_device(): fit, counts = lax.psum((fit_part, count_part), 'tm')]
    psum x1 -> x0, blocking collectives: 7.13 us -> none  [on_device(): fit, counts = lax.psum((fit_part, count_part), 'tm')]
  transfers between devices with their start and end apart: 3 -> 28, of which waited for: 3 -> 10; matrix products, arithmetic and copies ran while one was open for 2% -> 3% of each run, Pallas kernels for 0% -> 18%
where the time goes in v1:
time: 282 us; the launch traced here: 281 us
  waiting for transfers between devices  134 us (48%)
  starting transfers between devices  66.7 us (24%)
  Pallas kernels  63.9 us (23%)
  local copies, waits for them, and re-layouts  12.9 us (5%)
  other arithmetic  3.89 us (1%)
    ppermute x18, waiting for transfers between devices, send(): lax.ppermute(array, 'det', [(i, (i + shift) % ring) for i in range(ring)])  82.1 us
    ppermute x18, starting transfers between devices, send(): lax.ppermute(array, 'det', [(i, (i + shift) % ring) for i in range(ring)])  55.8 us
    ppermute x10, waiting for transfers between devices, swap(): lax.ppermute(array, axis, [(i, i ^ bit) for i in range(lax.axis_size(axis...  51.6 us
    pallas_call x3, Pallas kernels, common_mode(): pl.pallas_call(functools.partial(filter_kernel, ring), out_shape=[jax.Sha...  23.5 us
    pallas_call x3, Pallas kernels, fit_piece(): pl.pallas_call(functools.partial(fit_kernel, ring, more), out_shape=[jax....  16.5 us
    ppermute x10, starting transfers between devices, swap(): lax.ppermute(array, axis, [(i, i ^ bit) for i in range(lax.axis_size(axis...  10.9 us
    pallas_call x1, Pallas kernels, remove_template(): pl.pallas_call(template_kernel, out_shape=jax.ShapeDtypeStruct((rows, sam...  8.98 us
    pallas_call x3, Pallas kernels, calibrate(): pl.pallas_call(functools.partial(calibrate_kernel, len(pieces)), out_shap...  8.41 us
  transfers between devices with their start and end apart: 28, of which 10 were waited for; matrix products, arithmetic and copies ran while one was open for 3% of the time, Pallas kernels for 18%

profile of v1, /device:TPU:0, one launch (start us, length us, event | category | flops | bytes accessed | tf_op | source)
XLA Modules:
  0.0 281.3 jit_solution(2588049630227076978)
XLA Ops:
  0.0 1.6 constant_dynamic-update-slice_fusion.4
  1.6 4.1 %collective-permute-start = (f32[1,2,32,512]{3,2,1,0:T(8,128)S(1)}, f32[1,2,32,512]{3,2,1,0:T(8,128)S(1)}, u32[]{:S(2)}, u32[]{:S(2)}) collective-permute-start(f32[1,2,32,512]{3,2,1,0:T(8,128)S(1)} %get-tuple-element.74), channel_id=1, source_target_pairs={{0,8},{4,12},{8,0},{12,4},{1,9},{5,13},{9,1},{13,5},{2,10},{6,14},... | collective-permute-start | bytes 393224 | tf_op jit(solution)/shard_map/ppermute | solution.py:282
  5.6 6.3 %collective-permute-done = f32[1,2,32,512]{3,2,1,0:T(8,128)S(1)} collective-permute-done((f32[1,2,32,512]{3,2,1,0:T(8,128)S(1)}, f32[1,2,32,512]{3,2,1,0:T(8,128)S(1)}, u32[]{:S(2)}, u32[]{:S(2)}) %collective-permute-start) | collective-permute-done | bytes 131104 | tf_op jit(solution)/shard_map/ppermute | solution.py:282
  12.0 0.8 collective-permute-start.1
  12.8 6.7 %collective-permute-done.1 = f32[2,2,32,512]{3,2,1,0:T(8,128)S(1)} collective-permute-done((f32[2,2,32,512]{3,2,1,0:T(8,128)S(1)}, f32[2,2,32,512]{3,2,1,0:T(8,128)S(1)}, u32[]{:S(2)}, u32[]{:S(2)}) %collective-permute-start.1) | collective-permute-done | bytes 262176 | tf_op jit(solution)/shard_map/ppermute | solution.py:282
  19.5 1.4 collective-permute-start.2
  20.9 10.9 %collective-permute-done.2 = f32[4,2,32,512]{3,2,1,0:T(8,128)S(1)} collective-permute-done((f32[4,2,32,512]{3,2,1,0:T(8,128)S(1)}, f32[4,2,32,512]{3,2,1,0:T(8,128)S(1)}, u32[]{:S(2)}, u32[]{:S(2)}) %collective-permute-start.2) | collective-permute-done | bytes 524320 | tf_op jit(solution)/shard_map/ppermute | solution.py:282
  31.8 0.1 pad_maximum_fusion
  31.9 1.3 collective-permute-start.3
  33.3 0.7 constant_dynamic-update-slice_fusion.10
  33.9 0.7 constant_dynamic-update-slice_fusion.3
  34.7 0.9 constant_dynamic-update-slice_fusion.2
  35.5 1.1 constant_dynamic-update-slice_fusion.1
  36.6 18.0 %collective-permute-done.3 = f32[8,2,32,512]{3,2,1,0:T(8,128)S(1)} collective-permute-done((f32[8,2,32,512]{3,2,1,0:T(8,128)S(1)}, f32[8,2,32,512]{3,2,1,0:T(8,128)S(1)}, u32[]{:S(2)}, u32[]{:S(2)}) %collective-permute-start.3) | collective-permute-done | bytes 1048608 | tf_op jit(solution)/shard_map/ppermute | solution.py:282
  54.6 1.6 constant_dynamic-update-slice_fusion
  56.2 2.3 shard_map.87
  58.5 3.0 %collective-permute-start.17 = (f32[256,256]{1,0:T(8,128)}, f32[256,256]{1,0:T(8,128)S(1)}, u32[]{:S(2)}, u32[]{:S(2)}) collective-permute-start(f32[256,256]{1,0:T(8,128)} %get-tuple-element.60.refs_1_), channel_id=1, source_target_pairs={{0,4},{4,8},{8,12},{12,0},{1,5},{5,9},{9,13},{13,1},{2,6},{6,10},{... | collective-permute-start | bytes 786440 | tf_op jit(solution)/shard_map/ppermute | solution.py:279
  61.5 2.9 %shard_map.85 = (f32[256,512]{1,0:T(8,128)}, f32[256,512]{1,0:T(8,128)}, f32[256,512]{1,0:T(8,128)}) custom-call(s32[1]{0:T(128)} %bitcast.me_ref, f32[64,256]{1,0:T(8,128)} %bitcast.35, f32[256,4096]{1,0:T(8,128)} %refs_6_.5, s32[1,4096]{1,0:T(1,128)} %bitcast.13, f32[1,4096]{1,0:T(1,128)} %bitcast.25, f32[256,4096]{1,0:T(8,128)} %refs_6_.5, ...), custom_call_target="tpu_custom_call" | custom-call | flops 201326592 | bytes 3145728 | tf_op jit(solution)/shard_map/pallas_call | solution.py:80
  64.5 2.8 collective-permute-start.11
  67.2 0.6 collective-permute-start.12
  67.9 2.9 %collective-permute-start.13 = (f32[256,512]{1,0:T(8,128)}, f32[256,512]{1,0:T(8,128)}, u32[]{:S(2)}, u32[]{:S(2)}) collective-permute-start(f32[256,512]{1,0:T(8,128)} %get-tuple-element.54.refs_3_), channel_id=1, source_target_pairs={{0,12},{4,0},{8,4},{12,8},{1,13},{5,1},{9,5},{13,9},{2,14},{6,2},{... | collective-permute-start | bytes 1572872 | tf_op jit(solution)/shard_map/ppermute | solution.py:279
  70.8 0.6 dynamic_slice.13
  71.4 1.2 pad_add_fusion.at_ref
  72.6 3.1 %shard_map.82 = (f32[256,256]{1,0:T(8,128)}, f32[256,256]{1,0:T(8,128)}, f32[256,256]{1,0:T(8,128)}, f32[256,256]{1,0:T(8,128)}, f32[256,512]{1,0:T(8,128)}, /*index=5*/f32[256,256]{1,0:T(8,128)}) custom-call(s32[1]{0:T(128)} %bitcast.me_ref, f32[64,256]{1,0:T(8,128)} %bitcast.36, f32[256,4096]{1,0:T(8,128)} %refs_6_.5, s32[1,4096]{1,0:T(1,128)} %bitcast.16, ...), custom_call_target="tpu_custom_call" | custom-call | flops 234881024 | bytes 3670016 | tf_op jit(solution)/shard_map/pallas_call | solution.py:80
  75.8 0.1 collective-permute-start.18
  75.9 1.5 collective-permute-start.19
  77.3 1.5 constant_dynamic-update-slice_fusion.5.bank_ref
  78.9 6.5 %shard_map.83 = (bf16[512,1024]{1,0:T(8,128)(2,1)}, bf16[512,1024]{1,0:T(8,128)(2,1)}, bf16[1024,512]{1,0:T(8,128)(2,1)}, bf16[1024,512]{1,0:T(8,128)(2,1)}) custom-call(s32[4]{0:T(128)} %pad_add_fusion.at_ref, f32[32,2,32,512]{3,2,1,0:T(8,128)} %constant_dynamic-update-slice_fusion.5.bank_ref, f32[2,512,512]{2,1,0:T(8,128)} %mix_ref.1), custom_call_target="tpu_custom_call" | custom-call | flops 1610612736 | bytes 6291456 | tf_op jit(solution)/shard_map/pallas_call | solution.py:118
  85.4 42.6 %collective-permute-done.18.refs_2_ = f32[256,256]{1,0:T(8,128)} collective-permute-done((f32[256,256]{1,0:T(8,128)S(1)}, f32[256,256]{1,0:T(8,128)}, u32[]{:S(2)}, u32[]{:S(2)}) %collective-permute-start.18) | collective-permute-done | bytes 262176 | tf_op jit(solution)/shard_map/ppermute | solution.py:279
  128.0 4.5 %collective-permute-start.5 = (f32[256,256]{1,0:T(8,128)S(1)}, f32[256,256]{1,0:T(8,128)S(1)}, u32[]{:S(2)}, u32[]{:S(2)}) collective-permute-start(f32[256,256]{1,0:T(8,128)S(1)} %copy-done.7), channel_id=1, source_target_pairs={{0,4},{4,8},{8,12},{12,0},{1,5},{5,9},{9,13},{13,1},{2,6},{6,10},{... | collective-permute-start | bytes 786440 | tf_op jit(solution)/shard_map/ppermute | solution.py:279
  132.5 3.5 %collective-permute-start.6 = (f32[256,256]{1,0:T(8,128)S(1)}, f32[256,256]{1,0:T(8,128)S(1)}, u32[]{:S(2)}, u32[]{:S(2)}) collective-permute-start(f32[256,256]{1,0:T(8,128)S(1)} %copy-done.8), channel_id=1, source_target_pairs={{0,8},{4,12},{8,0},{12,4},{1,9},{5,13},{9,1},{13,5},{2,10},{6,14},... | collective-permute-start | bytes 786440 | tf_op jit(solution)/shard_map/ppermute | solution.py:279
  136.0 6.6 %shard_map.88 = (f32[256,256]{1,0:T(8,128)}, f32[256,256]{1,0:T(8,128)}, f32[256,256]{1,0:T(8,128)}, f32[256,256]{1,0:T(8,128)}) custom-call(bf16[512,1024]{1,0:T(8,128)(2,1)} %get-tuple-element.43.first_high, bf16[512,1024]{1,0:T(8,128)(2,1)} %get-tuple-element.44.first_low, bf16[1024,512]{1,0:T(8,128)(2,1)} %get-tuple-element.45.second_high, ...), custom_call_target="tpu_custom_call" | custom-call | flops 1610612736 | bytes 2097152 | tf_op jit(solution)/shard_map/pallas_call | solution.py:154
  142.6 0.5 collective-permute-start.7
  143.1 1.1 collective-permute-start.20
  144.2 10.3 %shard_map.86 = (f32[256,512]{1,0:T(8,128)}, f32[256,512]{1,0:T(8,128)}, f32[256,512]{1,0:T(8,128)}, f32[256,512]{1,0:T(8,128)}) custom-call(bf16[512,1024]{1,0:T(8,128)(2,1)} %get-tuple-element.43.first_high, bf16[512,1024]{1,0:T(8,128)(2,1)} %get-tuple-element.44.first_low, bf16[1024,512]{1,0:T(8,128)(2,1)} %get-tuple-element.45.second_high, ...), custom_call_target="tpu_custom_call" | custom-call | flops 3221225472 | bytes 4194304 | tf_op jit(solution)/shard_map/pallas_call | solution.py:154
  154.5 1.5 collective-permute-start.14
  156.0 0.9 collective-permute-start.15
  156.9 27.3 %collective-permute-start.16 = (f32[256,512]{1,0:T(8,128)}, f32[256,512]{1,0:T(8,128)S(1)}, u32[]{:S(2)}, u32[]{:S(2)}) collective-permute-start(f32[256,512]{1,0:T(8,128)} %get-tuple-element.58), channel_id=1, source_target_pairs={{0,4},{4,8},{8,12},{12,0},{1,5},{5,9},{9,13},{13,1},{2,6},{6,10},{... | collective-permute-start | bytes 1572872 | tf_op jit(solution)/shard_map/ppermute | solution.py:279
  184.2 0.7 copy-done.22
  184.9 3.4 %collective-permute-start.21 = (f32[256,256]{1,0:T(8,128)}, f32[256,256]{1,0:T(8,128)S(1)}, u32[]{:S(2)}, u32[]{:S(2)}) collective-permute-start(f32[256,256]{1,0:T(8,128)} %get-tuple-element.65), channel_id=1, source_target_pairs={{0,8},{4,12},{8,0},{12,4},{1,9},{5,13},{9,1},{13,5},{2,10},{6,14},... | collective-permute-start | bytes 786440 | tf_op jit(solution)/shard_map/ppermute | solution.py:279
  188.3 0.1 collective-permute-start.22
  188.4 6.6 %shard_map.84 = (f32[256,256]{1,0:T(8,128)}, f32[256,256]{1,0:T(8,128)}, f32[256,256]{1,0:T(8,128)}, f32[256,256]{1,0:T(8,128)}) custom-call(bf16[512,1024]{1,0:T(8,128)(2,1)} %get-tuple-element.43.first_high, bf16[512,1024]{1,0:T(8,128)(2,1)} %get-tuple-element.44.first_low, bf16[1024,512]{1,0:T(8,128)(2,1)} %get-tuple-element.45.second_high, ...), custom_call_target="tpu_custom_call" | custom-call | flops 1610612736 | bytes 2097152 | tf_op jit(solution)/shard_map/pallas_call | solution.py:154
  195.0 30.9 %collective-permute-done.21.refs_6_ = f32[256,256]{1,0:T(8,128)S(1)} collective-permute-done((f32[256,256]{1,0:T(8,128)}, f32[256,256]{1,0:T(8,128)S(1)}, u32[]{:S(2)}, u32[]{:S(2)}) %collective-permute-start.21) | collective-permute-done | bytes 262176 | tf_op jit(solution)/shard_map/ppermute | solution.py:279
  226.0 2.2 collective-permute-start.10
  228.2 5.0 %shard_map.89 = (f32[256,4096]{1,0:T(8,128)}, f32[256,512]{1,0:T(8,128)}) custom-call(s32[4]{0:T(128)} %pad_add_fusion.at_ref, f32[256,256]{1,0:T(8,128)} %get-tuple-element.59.refs_0_, f32[256,256]{1,0:T(8,128)} %get-tuple-element.60.refs_1_, f32[256,256]{1,0:T(8,128)} %get-tuple-element.61.refs_2_, f32[256,256]{1,0:T(8,128)} %get-tuple-element.62.refs_3_, ...), custom_call_target="tpu_custom_call" | custom-call | flops 536870912 | bytes 3145728 | tf_op jit(solution)/shard_map/pallas_call | solution.py:201
  233.3 0.8 copy-done.2
  234.1 0.1 copy-done.3
  234.2 6.3 %shard_map.90 = (f32[256,4096]{1,0:T(8,128)}, f32[256,512]{1,0:T(8,128)}) custom-call(s32[4]{0:T(128)} %pad_add_fusion.at_ref, f32[256,512]{1,0:T(8,128)} %get-tuple-element.51.refs_0_, f32[256,512]{1,0:T(8,128)} %get-tuple-element.52.refs_1_, f32[256,512]{1,0:T(8,128)} %get-tuple-element.53.refs_2_, ...), custom_call_target="tpu_custom_call", output_to_operand_aliasing={{0}: (10, {})} | custom-call | flops 1073741824 | bytes 6291456 | tf_op jit(solution)/shard_map/pallas_call | solution.py:201
  240.5 8.6 %collective-permute-done.9.refs_6_ = f32[256,256]{1,0:T(8,128)S(1)} collective-permute-done((f32[256,256]{1,0:T(8,128)}, f32[256,256]{1,0:T(8,128)S(1)}, u32[]{:S(2)}, u32[]{:S(2)}) %collective-permute-start.9) | collective-permute-done | bytes 262176 | tf_op jit(solution)/shard_map/ppermute | solution.py:279
  249.1 0.7 copy-done.12
  249.8 0.1 copy-done.13
  249.9 5.2 %shard_map.91 = (f32[256,4096]{1,0:T(8,128)}, f32[256,512]{1,0:T(8,128)}) custom-call(s32[4]{0:T(128)} %pad_add_fusion.at_ref, f32[256,256]{1,0:T(8,128)} %get-tuple-element.39.refs_0_, f32[256,256]{1,0:T(8,128)} %get-tuple-element.40.refs_1_, f32[256,256]{1,0:T(8,128)} %get-tuple-element.41.refs_2_, ...), custom_call_target="tpu_custom_call", output_to_operand_aliasing={{0}: (10, {})} | custom-call | flops 536870912 | bytes 3145728 | tf_op jit(solution)/shard_map/pallas_call | solution.py:201
  255.1 1.0 constant_dynamic-slice_fusion
  256.0 0.1 collective-permute-start.23
  256.1 1.5 collective-permute-done.23
  257.6 1.0 dynamic-slice_add_fusion
  258.6 1.5 collective-permute-start.24
  260.2 0.9 convert_reduce_fusion
  261.2 5.9 %collective-permute-done.24 = f32[128,512]{1,0:T(8,128)S(1)} collective-permute-done((f32[128,512]{1,0:T(8,128)S(1)}, f32[128,512]{1,0:T(8,128)S(1)}, u32[]{:S(2)}, u32[]{:S(2)}) %collective-permute-start.24) | collective-permute-done | bytes 262176 | tf_op jit(solution)/shard_map/ppermute | solution.py:282
  267.2 1.5 collective-permute-start.27
  268.8 2.3 collective-permute-done.27
  271.0 0.6 slice_add_fusion.counts_ref
  271.6 0.7 copy-done.16
  272.3 9.0 %shard_map.92 = f32[256,4096]{1,0:T(8,128)} custom-call(s32[4]{0:T(128)} %pad_add_fusion.at_ref, f32[256,4096]{1,0:T(8,128)} %get-tuple-element.71.cleaned_ref, s32[1,4096]{1,0:T(1,128)} %bitcast.40, f32[128,512]{1,0:T(8,128)} %copy-done, f32[128,512]{1,0:T(8,128)} %copy-done.16, f32[1,512]{1,0:T(1,128)} %slice_add_fusion.counts_ref), custom_call_target="tpu_custom_call" | custom-call | flops 2147483648 | bytes 8388608 | tf_op jit(solution)/shard_map/pallas_call | solution.py:246
  (70 shorter events, 0.5 us)
Async XLA Ops:
  1.6 10.4 %collective-permute-start = (f32[1,2,32,512]{3,2,1,0:T(8,128)S(1)}, f32[1,2,32,512]{3,2,1,0:T(8,128)S(1)}, u32[]{:S(2)}, u32[]{:S(2)}) collective-permute-start(f32[1,2,32,512]{3,2,1,0:T(8,128)S(1)} %get-tuple-element.74), channel_id=1, source_target_pairs={{0,8},{4,12},{8,0},{12,4},{1,9},{5,13},{9,1},{13,5},{2,10},{6,14},... | collective-permute-start | bytes 393224 | tf_op jit(solution)/shard_map/ppermute | solution.py:282
  12.0 7.5 %collective-permute-start.1 = (f32[2,2,32,512]{3,2,1,0:T(8,128)S(1)}, f32[2,2,32,512]{3,2,1,0:T(8,128)S(1)}, u32[]{:S(2)}, u32[]{:S(2)}) collective-permute-start(f32[2,2,32,512]{3,2,1,0:T(8,128)S(1)} %pad_maximum_fusion.2), channel_id=1, source_target_pairs={{0,4},{4,0},{8,12},{12,8},{1,5},{5,1},{9,13},{13,9},{2,6},{6,2},{1... | collective-permute-start | bytes 786440 | tf_op jit(solution)/shard_map/ppermute | solution.py:282
  19.5 12.3 %collective-permute-start.2 = (f32[4,2,32,512]{3,2,1,0:T(8,128)S(1)}, f32[4,2,32,512]{3,2,1,0:T(8,128)S(1)}, u32[]{:S(2)}, u32[]{:S(2)}) collective-permute-start(f32[4,2,32,512]{3,2,1,0:T(8,128)S(1)} %pad_maximum_fusion.1), channel_id=1, source_target_pairs={{0,2},{1,3},{2,0},{3,1},{4,6},{5,7},{6,4},{7,5},{8,10},{9,11},{10,... | collective-permute-start | bytes 1572872 | tf_op jit(solution)/shard_map/ppermute | solution.py:282
  31.9 22.7 %collective-permute-start.3 = (f32[8,2,32,512]{3,2,1,0:T(8,128)S(1)}, f32[8,2,32,512]{3,2,1,0:T(8,128)S(1)}, u32[]{:S(2)}, u32[]{:S(2)}) collective-permute-start(f32[8,2,32,512]{3,2,1,0:T(8,128)S(1)} %pad_maximum_fusion), channel_id=1, source_target_pairs={{0,16},{16,0},{1,17},{17,1},{2,18},{18,2},{3,19},{19,3},{4,20},{20... | collective-permute-start | bytes 3145736 | tf_op jit(solution)/shard_map/ppermute | solution.py:282
  56.2 19.6 %collective-permute-start.4 = (f32[16,2,32,512]{3,2,1,0:T(8,128)}, f32[16,2,32,512]{3,2,1,0:T(8,128)S(1)}, u32[]{:S(2)}, u32[]{:S(2)}) collective-permute-start(f32[16,2,32,512]{3,2,1,0:T(8,128)} %get-tuple-element.75), channel_id=1, source_target_pairs={{0,1},{1,0},{2,3},{3,2},{4,5},{5,4},{6,7},{7,6},{8,9},{9,8},{10,11... | collective-permute-start | bytes 6291464 | tf_op jit(solution)/shard_map/ppermute | solution.py:282
  58.5 12.3 %copy-start.23 = (s32[4]{0:T(128)S(1)}, s32[4]{0:T(128)}, u32[]{:S(2)}) copy-start(s32[4]{0:T(128)} %param.13) | copy-start | bytes 52
  58.5 17.2 %collective-permute-start.17 = (f32[256,256]{1,0:T(8,128)}, f32[256,256]{1,0:T(8,128)S(1)}, u32[]{:S(2)}, u32[]{:S(2)}) collective-permute-start(f32[256,256]{1,0:T(8,128)} %get-tuple-element.60.refs_1_), channel_id=1, source_target_pairs={{0,4},{4,8},{8,12},{12,0},{1,5},{5,9},{9,13},{13,1},{2,6},{6,10},{... | collective-permute-start | bytes 786440 | tf_op jit(solution)/shard_map/ppermute | solution.py:279
  64.5 78.2 %collective-permute-start.11 = (f32[256,512]{1,0:T(8,128)}, f32[256,512]{1,0:T(8,128)S(1)}, u32[]{:S(2)}, u32[]{:S(2)}) collective-permute-start(f32[256,512]{1,0:T(8,128)} %get-tuple-element.52.refs_1_), channel_id=1, source_target_pairs={{0,4},{4,8},{8,12},{12,0},{1,5},{5,9},{9,13},{13,1},{2,6},{6,10},{... | collective-permute-start | bytes 1572872 | tf_op jit(solution)/shard_map/ppermute | solution.py:279
  67.2 75.9 %collective-permute-start.12 = (f32[256,512]{1,0:T(8,128)}, f32[256,512]{1,0:T(8,128)}, u32[]{:S(2)}, u32[]{:S(2)}) collective-permute-start(f32[256,512]{1,0:T(8,128)} %get-tuple-element.53.refs_2_), channel_id=1, source_target_pairs={{0,8},{4,12},{8,0},{12,4},{1,9},{5,13},{9,1},{13,5},{2,10},{6,14},... | collective-permute-start | bytes 1572872 | tf_op jit(solution)/shard_map/ppermute | solution.py:279
  67.9 76.3 %collective-permute-start.13 = (f32[256,512]{1,0:T(8,128)}, f32[256,512]{1,0:T(8,128)}, u32[]{:S(2)}, u32[]{:S(2)}) collective-permute-start(f32[256,512]{1,0:T(8,128)} %get-tuple-element.54.refs_3_), channel_id=1, source_target_pairs={{0,12},{4,0},{8,4},{12,8},{1,13},{5,1},{9,5},{13,9},{2,14},{6,2},{... | collective-permute-start | bytes 1572872 | tf_op jit(solution)/shard_map/ppermute | solution.py:279
  72.6 3.2 %copy-start.5 = (f32[256,256]{1,0:T(8,128)S(1)}, f32[256,256]{1,0:T(8,128)}, u32[]{:S(2)}) copy-start(f32[256,256]{1,0:T(8,128)} %get-tuple-element.61.refs_2_) | copy-start | bytes 786436
  72.6 3.3 %copy-start.6 = (f32[256,256]{1,0:T(8,128)S(1)}, f32[256,256]{1,0:T(8,128)}, u32[]{:S(2)}) copy-start(f32[256,256]{1,0:T(8,128)} %get-tuple-element.62.refs_3_) | copy-start | bytes 786436
  75.7 9.6 %copy-start.18 = (f32[256,256]{1,0:T(8,128)}, f32[256,256]{1,0:T(8,128)S(1)}, u32[]{:S(2)}) copy-start(f32[256,256]{1,0:T(8,128)S(1)} %collective-permute-done.17.refs_1_) | copy-start | bytes 786436
  75.8 52.2 %collective-permute-start.18 = (f32[256,256]{1,0:T(8,128)S(1)}, f32[256,256]{1,0:T(8,128)}, u32[]{:S(2)}, u32[]{:S(2)}) collective-permute-start(f32[256,256]{1,0:T(8,128)S(1)} %copy-done.5), channel_id=1, source_target_pairs={{0,8},{4,12},{8,0},{12,4},{1,9},{5,13},{9,1},{13,5},{2,10},{6,14},... | collective-permute-start | bytes 786440 | tf_op jit(solution)/shard_map/ppermute | solution.py:279
  75.9 56.7 %collective-permute-start.19 = (f32[256,256]{1,0:T(8,128)S(1)}, f32[256,256]{1,0:T(8,128)}, u32[]{:S(2)}, u32[]{:S(2)}) collective-permute-start(f32[256,256]{1,0:T(8,128)S(1)} %copy-done.6), channel_id=1, source_target_pairs={{0,12},{4,0},{8,4},{12,8},{1,13},{5,1},{9,5},{13,9},{2,14},{6,2},{... | collective-permute-start | bytes 786440 | tf_op jit(solution)/shard_map/ppermute | solution.py:279
  78.9 49.1 %copy-start.7 = (f32[256,256]{1,0:T(8,128)S(1)}, f32[256,256]{1,0:T(8,128)}, u32[]{:S(2)}) copy-start(f32[256,256]{1,0:T(8,128)} %get-tuple-element.40.refs_1_) | copy-start | bytes 786436
  78.9 53.7 %copy-start.8 = (f32[256,256]{1,0:T(8,128)S(1)}, f32[256,256]{1,0:T(8,128)}, u32[]{:S(2)}) copy-start(f32[256,256]{1,0:T(8,128)} %get-tuple-element.41.refs_2_) | copy-start | bytes 786436
  85.4 57.3 %copy-start.9 = (f32[256,256]{1,0:T(8,128)S(1)}, f32[256,256]{1,0:T(8,128)}, u32[]{:S(2)}) copy-start(f32[256,256]{1,0:T(8,128)} %get-tuple-element.42.refs_3_) | copy-start | bytes 786436
  128.0 28.0 %collective-permute-start.5 = (f32[256,256]{1,0:T(8,128)S(1)}, f32[256,256]{1,0:T(8,128)S(1)}, u32[]{:S(2)}, u32[]{:S(2)}) collective-permute-start(f32[256,256]{1,0:T(8,128)S(1)} %copy-done.7), channel_id=1, source_target_pairs={{0,4},{4,8},{8,12},{12,0},{1,5},{5,9},{9,13},{13,1},{2,6},{6,10},{... | collective-permute-start | bytes 786440 | tf_op jit(solution)/shard_map/ppermute | solution.py:279
  132.5 24.4 %collective-permute-start.6 = (f32[256,256]{1,0:T(8,128)S(1)}, f32[256,256]{1,0:T(8,128)S(1)}, u32[]{:S(2)}, u32[]{:S(2)}) collective-permute-start(f32[256,256]{1,0:T(8,128)S(1)} %copy-done.8), channel_id=1, source_target_pairs={{0,8},{4,12},{8,0},{12,4},{1,9},{5,13},{9,1},{13,5},{2,10},{6,14},... | collective-permute-start | bytes 786440 | tf_op jit(solution)/shard_map/ppermute | solution.py:279
  142.6 1.5 copy-start.17
  142.6 41.5 %collective-permute-start.7 = (f32[256,256]{1,0:T(8,128)S(1)}, f32[256,256]{1,0:T(8,128)S(1)}, u32[]{:S(2)}, u32[]{:S(2)}) collective-permute-start(f32[256,256]{1,0:T(8,128)S(1)} %copy-done.9), channel_id=1, source_target_pairs={{0,12},{4,0},{8,4},{12,8},{1,13},{5,1},{9,5},{13,9},{2,14},{6,2},{... | collective-permute-start | bytes 786440 | tf_op jit(solution)/shard_map/ppermute | solution.py:279
  143.1 45.2 %collective-permute-start.20 = (f32[256,256]{1,0:T(8,128)}, f32[256,256]{1,0:T(8,128)S(1)}, u32[]{:S(2)}, u32[]{:S(2)}) collective-permute-start(f32[256,256]{1,0:T(8,128)} %get-tuple-element.64), channel_id=1, source_target_pairs={{0,12},{4,0},{8,4},{12,8},{1,13},{5,1},{9,5},{13,9},{2,14},{6,2},{... | collective-permute-start | bytes 786440 | tf_op jit(solution)/shard_map/ppermute | solution.py:279
  144.2 44.1 %copy-start.20 = (f32[256,256]{1,0:T(8,128)S(1)}, f32[256,256]{1,0:T(8,128)}, u32[]{:S(2)}) copy-start(f32[256,256]{1,0:T(8,128)} %get-tuple-element.66) | copy-start | bytes 786436
  154.5 71.5 %collective-permute-start.14 = (f32[256,512]{1,0:T(8,128)}, f32[256,512]{1,0:T(8,128)S(1)}, u32[]{:S(2)}, u32[]{:S(2)}) collective-permute-start(f32[256,512]{1,0:T(8,128)} %get-tuple-element.56), channel_id=1, source_target_pairs={{0,12},{4,0},{8,4},{12,8},{1,13},{5,1},{9,5},{13,9},{2,14},{6,2},{... | collective-permute-start | bytes 1572872 | tf_op jit(solution)/shard_map/ppermute | solution.py:279
  156.0 32.4 %copy-start.19 = (f32[256,256]{1,0:T(8,128)}, f32[256,256]{1,0:T(8,128)S(1)}, u32[]{:S(2)}) copy-start(f32[256,256]{1,0:T(8,128)S(1)} %collective-permute-done.5.refs_1_) | copy-start | bytes 786436
  156.0 77.2 %collective-permute-start.15 = (f32[256,512]{1,0:T(8,128)}, f32[256,512]{1,0:T(8,128)S(1)}, u32[]{:S(2)}, u32[]{:S(2)}) collective-permute-start(f32[256,512]{1,0:T(8,128)} %get-tuple-element.57), channel_id=1, source_target_pairs={{0,8},{4,12},{8,0},{12,4},{1,9},{5,13},{9,1},{13,5},{2,10},{6,14},... | collective-permute-start | bytes 1572872 | tf_op jit(solution)/shard_map/ppermute | solution.py:279
  156.9 31.5 %copy-start.21 = (f32[256,256]{1,0:T(8,128)}, f32[256,256]{1,0:T(8,128)S(1)}, u32[]{:S(2)}) copy-start(f32[256,256]{1,0:T(8,128)S(1)} %collective-permute-done.6.refs_2_) | copy-start | bytes 786436
  156.9 76.3 %collective-permute-start.16 = (f32[256,512]{1,0:T(8,128)}, f32[256,512]{1,0:T(8,128)S(1)}, u32[]{:S(2)}, u32[]{:S(2)}) collective-permute-start(f32[256,512]{1,0:T(8,128)} %get-tuple-element.58), channel_id=1, source_target_pairs={{0,4},{4,8},{8,12},{12,0},{1,5},{5,9},{9,13},{13,1},{2,6},{6,10},{... | collective-permute-start | bytes 1572872 | tf_op jit(solution)/shard_map/ppermute | solution.py:279
  184.2 0.7 copy-start.22
  184.9 41.0 %collective-permute-start.21 = (f32[256,256]{1,0:T(8,128)}, f32[256,256]{1,0:T(8,128)S(1)}, u32[]{:S(2)}, u32[]{:S(2)}) collective-permute-start(f32[256,256]{1,0:T(8,128)} %get-tuple-element.65), channel_id=1, source_target_pairs={{0,8},{4,12},{8,0},{12,4},{1,9},{5,13},{9,1},{13,5},{2,10},{6,14},... | collective-permute-start | bytes 786440 | tf_op jit(solution)/shard_map/ppermute | solution.py:279
  188.3 39.9 %copy-start.10 = (f32[256,256]{1,0:T(8,128)}, f32[256,256]{1,0:T(8,128)S(1)}, u32[]{:S(2)}) copy-start(f32[256,256]{1,0:T(8,128)S(1)} %collective-permute-done.20.refs_5_) | copy-start | bytes 786436
  188.3 37.6 %collective-permute-start.22 = (f32[256,256]{1,0:T(8,128)S(1)}, f32[256,256]{1,0:T(8,128)S(1)}, u32[]{:S(2)}, u32[]{:S(2)}) collective-permute-start(f32[256,256]{1,0:T(8,128)S(1)} %copy-done.20), channel_id=1, source_target_pairs={{0,4},{4,8},{8,12},{12,0},{1,5},{5,9},{9,13},{13,1},{2,6},{6,10},{... | collective-permute-start | bytes 786440 | tf_op jit(solution)/shard_map/ppermute | solution.py:279
  225.9 2.3 copy-start.14
  225.9 14.6 %collective-permute-start.8 = (f32[256,256]{1,0:T(8,128)}, f32[256,256]{1,0:T(8,128)S(1)}, u32[]{:S(2)}, u32[]{:S(2)}) collective-permute-start(f32[256,256]{1,0:T(8,128)} %get-tuple-element.48), channel_id=1, source_target_pairs={{0,12},{4,0},{8,4},{12,8},{1,13},{5,1},{9,5},{13,9},{2,14},{6,2},{... | collective-permute-start | bytes 786440 | tf_op jit(solution)/shard_map/ppermute | solution.py:279
  225.9 2.3 copy-start.15
  225.9 23.2 %collective-permute-start.9 = (f32[256,256]{1,0:T(8,128)}, f32[256,256]{1,0:T(8,128)S(1)}, u32[]{:S(2)}, u32[]{:S(2)}) collective-permute-start(f32[256,256]{1,0:T(8,128)} %get-tuple-element.49), channel_id=1, source_target_pairs={{0,8},{4,12},{8,0},{12,4},{1,9},{5,13},{9,1},{13,5},{2,10},{6,14},... | collective-permute-start | bytes 786440 | tf_op jit(solution)/shard_map/ppermute | solution.py:279
  226.0 7.3 %copy-start.1 = (f32[256,512]{1,0:T(8,128)}, f32[256,512]{1,0:T(8,128)S(1)}, u32[]{:S(2)}) copy-start(f32[256,512]{1,0:T(8,128)S(1)} %collective-permute-done.14.refs_5_) | copy-start | bytes 1572868
  226.0 23.1 %collective-permute-start.10 = (f32[256,256]{1,0:T(8,128)}, f32[256,256]{1,0:T(8,128)S(1)}, u32[]{:S(2)}, u32[]{:S(2)}) collective-permute-start(f32[256,256]{1,0:T(8,128)} %get-tuple-element.50), channel_id=1, source_target_pairs={{0,4},{4,8},{8,12},{12,0},{1,5},{5,9},{9,13},{13,1},{2,6},{6,10},{... | collective-permute-start | bytes 786440 | tf_op jit(solution)/shard_map/ppermute | solution.py:279
  233.2 0.8 copy-start.2
  233.3 1.0 copy-start.3
  240.5 19.7 %copy-start.4 = (s32[4096]{0:T(1024)S(1)}, s32[4096]{0:T(1024)}, u32[]{:S(2)}) copy-start(s32[4096]{0:T(1024)} %param.12) | copy-start | bytes 49156
  240.5 8.6 %copy-start.11 = (f32[256,256]{1,0:T(8,128)}, f32[256,256]{1,0:T(8,128)S(1)}, u32[]{:S(2)}) copy-start(f32[256,256]{1,0:T(8,128)S(1)} %collective-permute-done.8.refs_5_) | copy-start | bytes 786436
  249.1 0.7 copy-start.12
  249.1 0.8 copy-start.13
  256.0 1.6 collective-permute-start.23
  258.6 8.4 %collective-permute-start.24 = (f32[128,512]{1,0:T(8,128)S(1)}, f32[128,512]{1,0:T(8,128)S(1)}, u32[]{:S(2)}, u32[]{:S(2)}) collective-permute-start(f32[128,512]{1,0:T(8,128)S(1)} %dynamic-slice_add_fusion), channel_id=1, source_target_pairs={{0,2},{1,3},{2,0},{3,1},{4,6},{5,7},{6,4},{7,5},{8,10},{9,11},{10,... | collective-permute-start | bytes 786440 | tf_op jit(solution)/shard_map/ppermute | solution.py:282
  261.1 6.1 %collective-permute-start.26 = (f32[8,512]{1,0:T(8,128)S(1)}, f32[8,512]{1,0:T(8,128)S(1)}, u32[]{:S(2)}, u32[]{:S(2)}) collective-permute-start(f32[8,512]{1,0:T(8,128)S(1)} %broadcast_in_dim.23), channel_id=1, source_target_pairs={{0,1},{1,0},{2,3},{3,2},{4,5},{5,4},{6,7},{7,6},{8,9},{9,8},{10,11... | collective-permute-start | bytes 49160 | tf_op jit(solution)/shard_map/ppermute | solution.py:282
  267.1 4.5 %copy-start = (f32[128,512]{1,0:T(8,128)}, f32[128,512]{1,0:T(8,128)S(1)}, u32[]{:S(2)}) copy-start(f32[128,512]{1,0:T(8,128)S(1)} %add.34.own_ref) | copy-start | bytes 786436
  267.1 4.5 %collective-permute-start.25 = (f32[128,512]{1,0:T(8,128)S(1)}, f32[128,512]{1,0:T(8,128)S(1)}, u32[]{:S(2)}, u32[]{:S(2)}) collective-permute-start(f32[128,512]{1,0:T(8,128)S(1)} %add.34.own_ref), channel_id=1, source_target_pairs={{0,1},{1,0},{2,3},{3,2},{4,5},{5,4},{6,7},{7,6},{8,9},{9,8},{10,11... | collective-permute-start | bytes 786440 | tf_op jit(solution)/shard_map/ppermute | solution.py:282
  267.2 3.8 %collective-permute-start.27 = (f32[8,512]{1,0:T(8,128)S(1)}, f32[8,512]{1,0:T(8,128)S(1)}, u32[]{:S(2)}, u32[]{:S(2)}) collective-permute-start(f32[8,512]{1,0:T(8,128)S(1)} %broadcast_add_fusion), channel_id=1, source_target_pairs={{0,2},{1,3},{2,0},{3,1},{4,6},{5,7},{6,4},{7,5},{8,10},{9,11},{10,... | collective-permute-start | bytes 49160 | tf_op jit(solution)/shard_map/ppermute | solution.py:282
  271.6 0.7 copy-start.16

commit v2 on v1

--- a/solution.py
+++ b/solution.py
@@ -163,31 +163,149 @@
     )(*modes, *arrived)
 
 
-def fit_kernel(ring, more, at_ref, *refs):
-    data, back, azimuth_ref = refs[:ring], refs[ring : 2 * ring], refs[2 * ring]
-    old = refs[2 * ring + 1 : 2 * ring + 3] if more else ()
-    cleaned_ref, fit_ref = refs[-2:]
+def onehot_of(azimuth, bins):
+    row = lax.broadcasted_iota(jnp.int32, (bins, azimuth.shape[1]), 0)
+    return (row == azimuth).astype(jnp.float32).astype(jnp.bfloat16)
+
+
+def block_start(ring, me, shift, start):
+    return pl.multiple_of(lax.rem(me + shift, ring) * BLOCK + start, 128)
+
+
+def bin_kernel(ring, pieces, at_ref, index_ref, azimuth_ref, *refs):
+    data, (keep_ref, send_ref, sums) = refs[: len(pieces)], refs[len(pieces) :]
+    me, tm = at_ref[0], at_ref[4]
+    rows = keep_ref.shape[0]
+    sums[...] = jnp.zeros_like(sums)
+    for (shift, start, width), ref in zip(pieces, data):
+        both = jnp.concatenate(halves(ref[...]), axis=0)
+        onehot = onehot_of(azimuth_ref[:, pl.ds(block_start(ring, me, shift, start), width)], sums.shape[2])
+        part = dot(both, onehot, ((1,), (1,)))
+        sums[index_ref[lax.rem(me + shift, ring)]] += part[:rows] + part[rows:]
+    share = sums.shape[2] // 4
+    for x in range(2):
+        for bank in range(2):
+            column = slice((2 * x + bank) * share, (2 * x + bank + 1) * share)
+            for flip, ref in ((0, keep_ref), (1, send_ref)):
+                first = pl.multiple_of(jnp.bitwise_xor(tm, 2 * x + flip) * share, share)
+                ref[:, column] = sums[bank, :, pl.ds(first, share)]
+
+
+def bin_data(ring, at, mode_index, azimuth, pieces, data):
+    rows = data[0].shape[0]
+    work = sum(width for _, _, width in pieces)
+    return pl.pallas_call(
+        functools.partial(bin_kernel, ring, pieces),
+        out_shape=[jax.ShapeDtypeStruct((rows, NBIN), jnp.float32)] * 2,
+        in_specs=[pl.BlockSpec(memory_space=pltpu.SMEM)] * 2 + [pl.BlockSpec(memory_space=pltpu.VMEM)] * (1 + len(data)),
+        out_specs=[pl.BlockSpec(memory_space=pltpu.VMEM)] * 2,
+        scratch_shapes=[pltpu.VMEM((2, rows, NBIN), jnp.float32)],
+        cost_estimate=pl.CostEstimate(
+            flops=4 * rows * work * NBIN, bytes_accessed=4 * rows * work, transcendentals=0
+        ),
+    )(at, mode_index, azimuth, *data)
+
+
+def pool_kernel(ring, shares, at_ref, bank_ref, own_ref, mix_ref, sums_ref, mine_ref, cross_ref, near_ref, total):
     step = pl.program_id(0)
+    slots, _, rows, m = bank_ref.shape
+    sums = halves(sums_ref[...])
+    amps = [halves(own_ref[0].T)[n] for n in range(2)]
+    amps = dot3(amps, sums)
+    coef = halves(amps + dot3(halves(mix_ref[0]), halves(amps)))
+    removed = dot3(halves(bank_ref[:, 0].reshape(slots * rows, m)), coef)
 
     @pl.when(step == 0)
     def _():
-        fit_ref[...] = old[1][...] if more else jnp.zeros_like(fit_ref)
-
+        total[...] = removed
+        mine_ref[...] = sums_ref[...]
+
+    @pl.when(step == 1)
+    def _():
+        total[...] += removed
+        mine_ref[...] += sums_ref[...]
+        part = at_ref[2]
+        for p in range(shares):
+            flip = jnp.bitwise_xor(part, p)
+            slot = ring * (lax.rem(flip // 2, 2) + 2 * (flip // 4) + 4 * lax.rem(flip, 2))
+            block = slice(p * rows, (p + 1) * rows)
+
+            def rows_of(z):
+                return total[pl.ds(pl.multiple_of((slot + z) * rows, rows), rows), :]
+
+            mine_ref[block, :] -= rows_of(0)
+            cross_ref[block, :] = rows_of(1)
+            near_ref[block, :] = rows_of(2)
+            near_ref[p * rows + shares * rows : (p + 1) * rows + shares * rows, :] = rows_of(3)
+
+
+def pool(ring, shares, at, banks, mode_bank, mode_mix, sums):
+    slots, _, rows, m = banks.shape
+    det_rows, share = rows * shares, sums.shape[1] // 2
+    shapes = [(det_rows, share), (det_rows, share), (2 * det_rows, share)]
+    return pl.pallas_call(
+        functools.partial(pool_kernel, ring, shares),
+        out_shape=[jax.ShapeDtypeStruct(shape, jnp.float32) for shape in shapes],
+        grid_spec=pltpu.PrefetchScalarGridSpec(
+            num_scalar_prefetch=1,
+            grid=(2,),
+            in_specs=[
+                pl.BlockSpec((slots, 1, rows, m), lambda b, at_ref: (0, b, 0, 0)),
+                pl.BlockSpec((1, det_rows, m), lambda b, at_ref: (b, 0, 0)),
+                pl.BlockSpec((1, m, m), lambda b, at_ref: (b, 0, 0)),
+                pl.BlockSpec((det_rows, share), lambda b, at_ref: (0, b)),
+            ],
+            out_specs=[pl.BlockSpec(shape, lambda b, at_ref: (0, 0)) for shape in shapes],
+            scratch_shapes=[pltpu.VMEM((slots * rows, share), jnp.float32)],
+        ),
+        cost_estimate=pl.CostEstimate(
+            flops=30 * slots * rows * m * share, bytes_accessed=8 * slots * rows * m, transcendentals=0
+        ),
+    )(at, banks, mode_bank, mode_mix, sums)
+
+
+def stack_kernel(at_ref, here_ref, there_ref, counts_ref, both_ref):
+    tm = at_ref[4]
+    rows, width = here_ref.shape
+    share = width // 2
+    for flip, ref in ((0, here_ref), (1, there_ref)):
+        for x in range(2):
+            first = pl.multiple_of(jnp.bitwise_xor(tm, 2 * x + flip) * share, share)
+            counts = jnp.maximum(counts_ref[:1, pl.ds(first, share)], 1.0)
+            high, low = halves(ref[:, x * share : (x + 1) * share] / counts)
+            both_ref[:rows, pl.ds(first, share)] = high
+            both_ref[rows:, pl.ds(first, share)] = low
+
+
+def stack_template(at, here, there, counts):
+    return pl.pallas_call(
+        stack_kernel,
+        out_shape=jax.ShapeDtypeStruct((2 * here.shape[0], NBIN), jnp.bfloat16),
+        in_specs=[pl.BlockSpec(memory_space=pltpu.SMEM)] + [pl.BlockSpec(memory_space=pltpu.VMEM)] * 3,
+        out_specs=pl.BlockSpec(memory_space=pltpu.VMEM),
+    )(at, here, there, counts)
+
+
+def finish_kernel(ring, count, template, at_ref, *refs):
+    data, back, refs, out_ref = refs[:ring], refs[ring : ring + count], refs[ring + count : -1], refs[-1]
+    step = pl.program_id(0)
     for s in range(ring):
 
         @pl.when(step == s)
         def _():
-            cleaned_ref[...] = data[s][...] - back[s][...]
-
-    rows = cleaned_ref.shape[0]
-    cleaned = jnp.concatenate(halves(cleaned_ref[...]), axis=0)
-    bins = lax.broadcasted_iota(jnp.int32, (fit_ref.shape[1], cleaned_ref.shape[1]), 0)
-    onehot = (bins == azimuth_ref[...]).astype(jnp.float32).astype(jnp.bfloat16)
-    sums = dot(cleaned, onehot, ((1,), (1,)))
-    fit_ref[...] += sums[:rows] + sums[rows:]
-
-
-def fit_piece(ring, at, start, data, back, azimuth, old):
+            if s < ring - count:
+                out_ref[...] = data[s][...]
+            else:
+                out_ref[...] = data[s][...] - back[s - ring + count][...]
+
+    if template:
+        both_ref, azimuth_ref = refs[:2]
+        rows = out_ref.shape[0]
+        levels = dot(both_ref[...], onehot_of(azimuth_ref[...], both_ref.shape[1]))
+        out_ref[...] -= levels[:rows] + levels[rows:]
+
+
+def finish_piece(ring, at, start, data, back, template, azimuth, old):
     rows, width = data[0].shape
     samples = azimuth.shape[1]
     per_block, offset = BLOCK // width, start // width
@@ -195,74 +313,53 @@
     def where(s, at_ref):
         return 0, lax.rem(at_ref[0] + s, ring) * per_block + offset
 
-    full = pl.BlockSpec((rows, width), lambda s, at_ref: (0, 0))
-    sums = pl.BlockSpec((rows, NBIN), lambda s, at_ref: (0, 0))
-    more = old is not None
-    return pl.pallas_call(
-        functools.partial(fit_kernel, ring, more),
-        out_shape=[
-            jax.ShapeDtypeStruct((rows, samples), jnp.float32),
-            jax.ShapeDtypeStruct((rows, NBIN), jnp.float32),
-        ],
+    specs = [pl.BlockSpec((rows, width), lambda s, at_ref: (0, 0))] * (len(data) + len(back))
+    operands = [*data, *back]
+    if template is not None:
+        specs += [pl.BlockSpec(template.shape, lambda s, at_ref: (0, 0)), pl.BlockSpec((1, width), where)]
+        operands += [template, azimuth]
+    if old is not None:
+        specs += [pl.BlockSpec(memory_space=pl.ANY)]
+        operands += [old]
+    return pl.pallas_call(
+        functools.partial(finish_kernel, ring, len(back), template is not None),
+        out_shape=jax.ShapeDtypeStruct((rows, samples), jnp.float32),
         grid_spec=pltpu.PrefetchScalarGridSpec(
             num_scalar_prefetch=1,
             grid=(ring,),
-            in_specs=[full] * (2 * ring)
-            + [pl.BlockSpec((1, width), where)]
-            + ([pl.BlockSpec(memory_space=pl.ANY), sums] if more else []),
-            out_specs=[pl.BlockSpec((rows, width), where), sums],
-        ),
-        input_output_aliases={2 * ring + 2: 0} if more else {},
-        cost_estimate=pl.CostEstimate(
-            flops=4 * ring * rows * width * NBIN, bytes_accessed=12 * ring * rows * width, transcendentals=0
-        ),
-    )(at, *data, *back, azimuth, *(old if more else ()))
-
-
-def template_kernel(at_ref, cleaned_ref, azimuth_ref, own_ref, mate_ref, counts_ref, out_ref, both_ref):
-    half = own_ref.shape[0]
-    core = at_ref[3]
-
-    @pl.when(pl.program_id(0) == 0)
-    def _():
-        counts = jnp.maximum(counts_ref[...], 1.0)
-        for ref, side in ((own_ref, core), (mate_ref, 1 - core)):
-            first = pl.multiple_of(side * half, half)
-            high, low = halves(ref[...] / counts)
-            both_ref[pl.ds(first, half), :] = high
-            both_ref[pl.ds(2 * half + first, half), :] = low
-
-    bins = lax.broadcasted_iota(jnp.int32, (both_ref.shape[1], cleaned_ref.shape[1]), 0)
-    onehot = (bins == azimuth_ref[...]).astype(jnp.float32).astype(jnp.bfloat16)
-    template = dot(both_ref[...], onehot)
-    out_ref[...] = cleaned_ref[...] - (template[: 2 * half] + template[2 * half :])
-
-
-def remove_template(at, cleaned, azimuth, own, mate, counts):
-    rows, samples = cleaned.shape
-    tile = 512
-    column = pl.BlockSpec((rows, tile), lambda i, at_ref: (0, i))
-    whole = pl.BlockSpec(own.shape, lambda i, at_ref: (0, 0))
-    return pl.pallas_call(
-        template_kernel,
-        out_shape=jax.ShapeDtypeStruct((rows, samples), jnp.float32),
-        grid_spec=pltpu.PrefetchScalarGridSpec(
-            num_scalar_prefetch=1,
-            grid=(samples // tile,),
-            in_specs=[
-                column,
-                pl.BlockSpec((1, tile), lambda i, at_ref: (0, i)),
-                whole,
-                whole,
-                pl.BlockSpec(counts.shape, lambda i, at_ref: (0, 0)),
-            ],
-            out_specs=column,
-            scratch_shapes=[pltpu.VMEM((2 * rows, own.shape[1]), jnp.bfloat16)],
-        ),
-        cost_estimate=pl.CostEstimate(
-            flops=4 * rows * samples * NBIN, bytes_accessed=8 * rows * samples, transcendentals=0
-        ),
-    )(at, cleaned, azimuth, own, mate, counts)
+            in_specs=specs,
+            out_specs=pl.BlockSpec((rows, width), where),
+        ),
+        input_output_aliases={len(operands): 0} if old is not None else {},
+        cost_estimate=pl.CostEstimate(
+            flops=4 * ring * rows * width * (NBIN if template is not None else 1),
+            bytes_accessed=12 * ring * rows * width,
+            transcendentals=0,
+        ),
+    )(at, *operands)
+
+
+def level_kernel(ring, start, at_ref, both_ref, azimuth_ref, back_ref, *refs):
+    data, outs = refs[:ring], refs[ring:]
+    rows, width = outs[0].shape
+    for s in range(ring):
+        azimuth = azimuth_ref[:, pl.ds(block_start(ring, at_ref[0], s, start), width)]
+        levels = dot(both_ref[...], onehot_of(azimuth, both_ref.shape[1]))
+        value = data[s][...] - (levels[:rows] + levels[rows:])
+        outs[s][...] = value - back_ref[...] if s == 0 else value
+
+
+def level_piece(ring, at, start, data, back, template, azimuth):
+    rows, width = data[0].shape
+    return pl.pallas_call(
+        functools.partial(level_kernel, ring, start),
+        out_shape=[jax.ShapeDtypeStruct((rows, width), jnp.float32)] * ring,
+        in_specs=[pl.BlockSpec(memory_space=pltpu.SMEM)] + [pl.BlockSpec(memory_space=pltpu.VMEM)] * (3 + ring),
+        out_specs=[pl.BlockSpec(memory_space=pltpu.VMEM)] * ring,
+        cost_estimate=pl.CostEstimate(
+            flops=4 * ring * rows * width * NBIN, bytes_accessed=8 * ring * rows * width, transcendentals=0
+        ),
+    )(at, template, azimuth, back, *data)
 
 
 def exchanged_blocks(ring, shares, tod, gain_knots, intervals, fraction, azimuth, mode_index, mode_bank, mode_mix):
@@ -270,10 +367,9 @@
     me = lax.axis_index("det")
     tm = lax.axis_index("tm")
     part_of = lax.axis_index("groups") * lax.axis_size("tm") + tm
-    core = lax.rem(tm, 2)
     which = lax.dynamic_index_in_dim(mode_index, me, 0, False)
     me_only = jnp.full((1,), me, jnp.int32)
-    at = jnp.stack([me, which, part_of, core])
+    at = jnp.stack([me, which, part_of, lax.rem(tm, 2), tm])
 
     def send(array, shift):
         return lax.ppermute(array, "det", [(i, (i + shift) % ring) for i in range(ring)])
@@ -295,27 +391,43 @@
 
     rows = det_rows // shares
     banks = lax.dynamic_slice_in_dim(mode_bank, part_of * rows, rows, 1)[None]
-    for axis, bit in (("det", 2), ("det", 1), ("tm", 2), ("groups", 1), ("tm", 1)):
-        banks = jnp.concatenate([banks, swap(banks, axis, bit)], axis=0)
-    modes = prepare_modes(ring, shares, at, banks, mode_mix)
+    for bit in (2, 1):
+        banks = jnp.concatenate([banks, swap(banks, "det", bit)], axis=0)
+    by_x = swap(banks, "tm", 2)
+    by_y = swap(banks, "groups", 1)
+    diagonal = [swap(by_x[:2], "groups", 1), swap(by_y[2:], "tm", 2)]
+    banks = jnp.concatenate([banks, by_x, by_y, *diagonal], axis=0)
+    banks = jnp.concatenate([banks, swap(banks, "tm", 1)], axis=0)
+
+    pieces = [piece for part in order for piece in part]
+    keep, other = bin_data(ring, at, mode_index, azimuth, pieces, [data[s, start] for s, start, _ in pieces])
+    sums = keep + swap(other, "tm", 1)
+    half = NBIN // 2
+    sums = sums[:, :half] + swap(sums[:, half:], "tm", 2)
+    mine, cross, near = pool(ring, shares, at, banks, mode_bank, mode_mix, sums)
+    near = swap(near, "det", 1)
+    cross = swap(cross + near[det_rows:], "det", 2)
+    template = mine - near[:det_rows] - cross
+    template = jnp.concatenate([template, swap(template, "tm", 2)], axis=1)
+    other = swap(template, "tm", 1)
 
     counts = jnp.sum((lax.broadcasted_iota(jnp.int32, (NBIN, samples), 0) == azimuth).astype(jnp.float32), axis=1)
     counts = jnp.broadcast_to(counts[None, :], (8, NBIN))
     for bit in (1, 2):
         counts = counts + swap(counts, "tm", bit)
-
-    state = None
-    for start, width in PIECES:
+    template = stack_template(at, template, other, counts)
+
+    modes = prepare_modes(ring, shares, at, banks, mode_mix)
+    out = None
+    for part, (start, width) in enumerate(PIECES):
         removed = common_mode(ring, modes, [arrived[s, start] for s in range(ring)])
         back = [send(removed[s], -s) if s else removed[s] for s in range(ring)]
-        state = fit_piece(ring, at, start, [data[s, start] for s in range(ring)], back, azimuth, state)
-    cleaned, fit = state
-    half = det_rows // 2
-    own = lax.dynamic_slice_in_dim(fit, core * half, half, 0)
-    own = own + swap(lax.dynamic_slice_in_dim(fit, (1 - core) * half, half, 0), "tm", 1)
-    own = own + swap(own, "tm", 2)
-    mate = swap(own, "tm", 1)
-    return remove_template(at, cleaned, azimuth, own, mate, counts[:1])
+        mine = [data[s, start] for s in range(ring)]
+        if part == len(PIECES) - 1:
+            mine = level_piece(ring, at, start, mine, back[0], template, azimuth)
+            back, template = back[1:], None
+        out = finish_piece(ring, at, start, mine, back, template, azimuth, out)
+    return out
 
 
 def solution(mesh):
@@ -334,7 +446,7 @@
 
     def on_device(tod, gain_knots, intervals, fraction, azimuth, mode_index, mode_bank, mode_mix):
         args = (tod, gain_knots, intervals, fraction, azimuth, mode_index, mode_bank, mode_mix)
-        if ring == 4 and mode_index.shape[0] == ring and shares == 8 and tod.shape[0] % (16 * shares) == 0:
+        if ring == 4 and mode_index.shape[0] == ring and shares == 8 and mesh.shape["tm"] == 4 and mode_bank.shape[0] == 2 and tod.shape[0] % (16 * shares) == 0:
             return exchanged_blocks(ring, shares, *args)
         return gathered_sums(*args)
 

time: 282 us -> 262 us (0.929)
  waiting for transfers between devices: 134 us -> 111 us
  Pallas kernels: 63.9 us -> 72.1 us
  starting transfers between devices: 66.7 us -> 59.6 us
    ppermute x18, waiting for transfers between devices: 82.1 us -> 47.5 us  [send(): lax.ppermute(array, 'det', [(i, (i + shift) % ring) for i in range(ring)])]
    ppermute x18, starting transfers between devices: 55.8 us -> 36.6 us  [send(): lax.ppermute(array, 'det', [(i, (i + shift) % ring) for i in range(ring)])]
    ppermute x10 -> x15, starting transfers between devices: 10.9 us -> 23 us  [swap(): lax.ppermute(array, axis, [(i, i ^ bit) for i in range(lax.axis_size(axis...]
    ppermute x10 -> x15, waiting for transfers between devices: 51.6 us -> 63.7 us  [swap(): lax.ppermute(array, axis, [(i, i ^ bit) for i in range(lax.axis_size(axis...]
    pallas_call x4 -> x7, Pallas kernels: 25.5 us -> 33.7 us  [the longest x3 15.1 us: finish_piece(): pl.pallas_call(functools.partial(finish_kernel, ring, len(back), template...]
    unnamed x53 -> x61, local copies, waits for them, and re-layouts: 8.19 us -> 10.3 us
  transfers between devices with their start and end apart: 28 -> 33, of which waited for: 10 -> 13; matrix products, arithmetic and copies ran while one was open for 3% -> 5% of each run, Pallas kernels for 18% -> 26%
where the time goes in v2:
time: 262 us; the launch traced here: 261 us
  waiting for transfers between devices  111 us (42%)
  Pallas kernels  72.1 us (28%)
  starting transfers between devices  59.6 us (23%)
  local copies, waits for them, and re-layouts  14.7 us (6%)
  other arithmetic  3.51 us (1%)
    ppermute x15, waiting for transfers between devices, swap(): lax.ppermute(array, axis, [(i, i ^ bit) for i in range(lax.axis_size(axis...  63.7 us
    ppermute x18, waiting for transfers between devices, send(): lax.ppermute(array, 'det', [(i, (i + shift) % ring) for i in range(ring)])  47.5 us
    ppermute x18, starting transfers between devices, send(): lax.ppermute(array, 'det', [(i, (i + shift) % ring) for i in range(ring)])  36.6 us
    pallas_call x3, Pallas kernels, common_mode(): pl.pallas_call(functools.partial(filter_kernel, ring), out_shape=[jax.Sha...  23.6 us
    ppermute x15, starting transfers between devices, swap(): lax.ppermute(array, axis, [(i, i ^ bit) for i in range(lax.axis_size(axis...  23 us
    pallas_call x3, Pallas kernels, finish_piece(): pl.pallas_call(functools.partial(finish_kernel, ring, len(back), template...  15.1 us
    unnamed x61, local copies, waits for them, and re-layouts  10.3 us
    pallas_call x3, Pallas kernels, calibrate(): pl.pallas_call(functools.partial(calibrate_kernel, len(pieces)), out_shap...  8.33 us
  transfers between devices with their start and end apart: 33, of which 13 were waited for; matrix products, arithmetic and copies ran while one was open for 5% of the time, Pallas kernels for 26%

profile of v2, /device:TPU:0, one launch (start us, length us, event | category | flops | bytes accessed | tf_op | source)
XLA Modules:
  0.0 261.3 jit_solution(285422996870607849)
XLA Ops:
  0.0 1.6 constant_dynamic-update-slice_fusion.6
  1.6 4.1 %collective-permute-start = (f32[1,2,32,512]{3,2,1,0:T(8,128)S(1)}, f32[1,2,32,512]{3,2,1,0:T(8,128)S(1)}, u32[]{:S(2)}, u32[]{:S(2)}) collective-permute-start(f32[1,2,32,512]{3,2,1,0:T(8,128)S(1)} %get-tuple-element.80), channel_id=1, source_target_pairs={{0,8},{4,12},{8,0},{12,4},{1,9},{5,13},{9,1},{13,5},{2,10},{6,14},... | collective-permute-start | bytes 393224 | tf_op jit(solution)/shard_map/ppermute | solution.py:378
  5.6 6.3 %collective-permute-done = f32[1,2,32,512]{3,2,1,0:T(8,128)S(1)} collective-permute-done((f32[1,2,32,512]{3,2,1,0:T(8,128)S(1)}, f32[1,2,32,512]{3,2,1,0:T(8,128)S(1)}, u32[]{:S(2)}, u32[]{:S(2)}) %collective-permute-start) | collective-permute-done | bytes 131104 | tf_op jit(solution)/shard_map/ppermute | solution.py:378
  12.0 0.8 collective-permute-start.1
  12.8 6.7 %collective-permute-done.1 = f32[2,2,32,512]{3,2,1,0:T(8,128)S(1)} collective-permute-done((f32[2,2,32,512]{3,2,1,0:T(8,128)S(1)}, f32[2,2,32,512]{3,2,1,0:T(8,128)S(1)}, u32[]{:S(2)}, u32[]{:S(2)}) %collective-permute-start.1) | collective-permute-done | bytes 262176 | tf_op jit(solution)/shard_map/ppermute | solution.py:378
  19.6 1.4 collective-permute-start.2
  20.9 1.5 collective-permute-start.3
  22.4 0.7 constant_dynamic-update-slice_fusion.14
  23.1 0.7 constant_dynamic-update-slice_fusion.5
  23.8 0.8 constant_dynamic-update-slice_fusion.4
  24.7 7.2 %collective-permute-done.2 = f32[4,2,32,512]{3,2,1,0:T(8,128)S(1)} collective-permute-done((f32[4,2,32,512]{3,2,1,0:T(8,128)S(1)}, f32[4,2,32,512]{3,2,1,0:T(8,128)S(1)}, u32[]{:S(2)}, u32[]{:S(2)}) %collective-permute-start.2) | collective-permute-done | bytes 524320 | tf_op jit(solution)/shard_map/ppermute | solution.py:378
  31.9 1.3 collective-permute-start.4
  33.6 1.2 collective-permute-start.5
  34.8 1.1 constant_dynamic-update-slice_fusion.3
  35.9 1.1 constant_dynamic-update-slice_fusion.2
  37.0 1.5 collective-permute-done.4
  38.4 0.9 constant_dynamic-update-slice_fusion.1
  39.3 0.7 collective-permute-done.5
  40.0 0.9 constant_dynamic-update-slice_fusion
  41.5 1.3 stack.20.at_ref
  42.8 2.3 shard_map.82
  45.1 2.9 %shard_map.83 = (f32[256,512]{1,0:T(8,128)}, f32[256,512]{1,0:T(8,128)}, f32[256,512]{1,0:T(8,128)}) custom-call(s32[1]{0:T(128)} %bitcast.me_ref, f32[64,256]{1,0:T(8,128)} %bitcast.36, f32[256,4096]{1,0:T(8,128)} %refs_15_.1, s32[1,4096]{1,0:T(1,128)} %bitcast.14, f32[1,4096]{1,0:T(1,128)} %bitcast.26, f32[256,4096]{1,0:T(8,128)} %refs_15_.1, ...), custom_call_target="tpu_custom_call" | custom-call | flops 201326592 | bytes 3145728 | tf_op jit(solution)/shard_map/pallas_call | solution.py:80
  48.0 3.1 %shard_map.84 = (f32[256,256]{1,0:T(8,128)}, f32[256,256]{1,0:T(8,128)}, f32[256,256]{1,0:T(8,128)}, f32[256,256]{1,0:T(8,128)}, f32[256,512]{1,0:T(8,128)}, /*index=5*/f32[256,256]{1,0:T(8,128)}) custom-call(s32[1]{0:T(128)} %bitcast.me_ref, f32[64,256]{1,0:T(8,128)} %bitcast.37, f32[256,4096]{1,0:T(8,128)} %refs_15_.1, s32[1,4096]{1,0:T(1,128)} %bitcast.17, ...), custom_call_target="tpu_custom_call" | custom-call | flops 234881024 | bytes 3670016 | tf_op jit(solution)/shard_map/pallas_call | solution.py:80
  51.1 5.7 %shard_map.85 = (f32[256,512]{1,0:T(8,128)}, f32[256,512]{1,0:T(8,128)}) custom-call(s32[5]{0:T(128)} %stack.20.at_ref, s32[4]{0:T(128)} %index_ref.1, s32[1,4096]{1,0:T(1,128)} %bitcast.38, f32[256,256]{1,0:T(8,128)} %get-tuple-element.42.refs_0_.refs_1_, f32[256,256]{1,0:T(8,128)} %get-tuple-element.43.refs_1_.refs_2_, ...), custom_call_target="tpu_custom_call" | custom-call | flops 2147483648 | bytes 4194304 | tf_op jit(solution)/shard_map/pallas_call | solution.py:197
  57.4 1.7 collective-permute-done.7
  59.1 1.1 add.28
  60.3 1.2 collective-permute-start.8
  61.5 2.5 collective-permute-start.21
  64.0 3.4 %collective-permute-start.22 = (f32[256,512]{1,0:T(8,128)S(1)}, f32[256,512]{1,0:T(8,128)}, u32[]{:S(2)}, u32[]{:S(2)}) collective-permute-start(f32[256,512]{1,0:T(8,128)S(1)} %copy-done.2), channel_id=1, source_target_pairs={{0,8},{4,12},{8,0},{12,4},{1,9},{5,13},{9,1},{13,5},{2,10},{6,14},... | collective-permute-start | bytes 1572872 | tf_op jit(solution)/shard_map/ppermute | solution.py:375
  67.4 1.6 collective-permute-start.23
  69.0 0.9 convert_reduce_fusion
  69.9 1.2 collective-permute-start.27
  71.1 0.7 slice_add_fusion.sums_ref
  71.8 1.6 constant_dynamic-update-slice_fusion.7.bank_ref
  73.4 8.0 %shard_map.86 = (f32[256,128]{1,0:T(8,128)}, f32[256,128]{1,0:T(8,128)}, f32[512,128]{1,0:T(8,128)}) custom-call(s32[5]{0:T(128)} %stack.20.at_ref, f32[32,2,32,512]{3,2,1,0:T(8,128)} %constant_dynamic-update-slice_fusion.7.bank_ref, f32[2,256,512]{2,1,0:T(8,128)} %own_ref.1, f32[2,512,512]{2,1,0:T(8,128)} %mix_ref.3, f32[256,256]{1,0:T(8,128)} %slice_add_fusion.sums_ref), custom_call_target="tpu_custom_call" | custom-call | flops 2013265920 | bytes 4194304 | tf_op jit(solution)/shard_map/pallas_call | solution.py:246
  81.4 2.7 %collective-permute-start.9 = (f32[512,128]{1,0:T(8,128)}, f32[512,128]{1,0:T(8,128)S(1)}, u32[]{:S(2)}, u32[]{:S(2)}) collective-permute-start(f32[512,128]{1,0:T(8,128)} %get-tuple-element.57), channel_id=1, source_target_pairs={{0,4},{4,0},{8,12},{12,8},{1,5},{5,1},{9,13},{13,9},{2,6},{6,2},{1... | collective-permute-start | bytes 786440 | tf_op jit(solution)/shard_map/ppermute | solution.py:378
  84.1 6.4 %shard_map.88 = (bf16[512,1024]{1,0:T(8,128)(2,1)}, bf16[512,1024]{1,0:T(8,128)(2,1)}, bf16[1024,512]{1,0:T(8,128)(2,1)}, bf16[1024,512]{1,0:T(8,128)(2,1)}) custom-call(s32[5]{0:T(128)} %stack.20.at_ref, f32[32,2,32,512]{3,2,1,0:T(8,128)} %constant_dynamic-update-slice_fusion.7.bank_ref, f32[2,512,512]{2,1,0:T(8,128)} %mix_ref.3), custom_call_target="tpu_custom_call" | custom-call | flops 1610612736 | bytes 6291456 | tf_op jit(solution)/shard_map/pallas_call | solution.py:118
  90.4 22.3 %collective-permute-done.9 = f32[512,128]{1,0:T(8,128)S(1)} collective-permute-done((f32[512,128]{1,0:T(8,128)}, f32[512,128]{1,0:T(8,128)S(1)}, u32[]{:S(2)}, u32[]{:S(2)}) %collective-permute-start.9) | collective-permute-done | bytes 262176 | tf_op jit(solution)/shard_map/ppermute | solution.py:378
  112.7 1.5 collective-permute-start.28
  114.2 1.8 collective-permute-start.29
  116.1 1.5 collective-permute-start.14
  117.5 6.2 %collective-permute-start.10 = (f32[256,128]{1,0:T(8,128)S(1)}, f32[256,128]{1,0:T(8,128)S(1)}, u32[]{:S(2)}, u32[]{:S(2)}) collective-permute-start(f32[256,128]{1,0:T(8,128)S(1)} %slice_add_fusion.1), channel_id=1, source_target_pairs={{0,8},{4,12},{8,0},{12,4},{1,9},{5,13},{9,1},{13,5},{2,10},{6,14},... | collective-permute-start | bytes 393224 | tf_op jit(solution)/shard_map/ppermute | solution.py:378
  123.7 10.3 %shard_map.91 = (f32[256,512]{1,0:T(8,128)}, f32[256,512]{1,0:T(8,128)}, f32[256,512]{1,0:T(8,128)}, f32[256,512]{1,0:T(8,128)}) custom-call(bf16[512,1024]{1,0:T(8,128)(2,1)} %get-tuple-element.59.first_high, bf16[512,1024]{1,0:T(8,128)(2,1)} %get-tuple-element.60.first_low, bf16[1024,512]{1,0:T(8,128)(2,1)} %get-tuple-element.61.second_high, ...), custom_call_target="tpu_custom_call" | custom-call | flops 3221225472 | bytes 4194304 | tf_op jit(solution)/shard_map/pallas_call | solution.py:154
  134.1 1.1 collective-permute-start.15
  135.2 16.9 %collective-permute-done.10 = f32[256,128]{1,0:T(8,128)S(1)} collective-permute-done((f32[256,128]{1,0:T(8,128)S(1)}, f32[256,128]{1,0:T(8,128)S(1)}, u32[]{:S(2)}, u32[]{:S(2)}) %collective-permute-start.10) | collective-permute-done | bytes 131104 | tf_op jit(solution)/shard_map/ppermute | solution.py:378
  152.4 4.4 %collective-permute-start.24 = (f32[256,512]{1,0:T(8,128)}, f32[256,512]{1,0:T(8,128)S(1)}, u32[]{:S(2)}, u32[]{:S(2)}) collective-permute-start(f32[256,512]{1,0:T(8,128)} %get-tuple-element.72), channel_id=1, source_target_pairs={{0,12},{4,0},{8,4},{12,8},{1,13},{5,1},{9,5},{13,9},{2,14},{6,2},{... | collective-permute-start | bytes 1572872 | tf_op jit(solution)/shard_map/ppermute | solution.py:375
  157.5 6.6 %shard_map.92 = (f32[256,256]{1,0:T(8,128)}, f32[256,256]{1,0:T(8,128)}, f32[256,256]{1,0:T(8,128)}, f32[256,256]{1,0:T(8,128)}) custom-call(bf16[512,1024]{1,0:T(8,128)(2,1)} %get-tuple-element.59.first_high, bf16[512,1024]{1,0:T(8,128)(2,1)} %get-tuple-element.60.first_low, bf16[1024,512]{1,0:T(8,128)(2,1)} %get-tuple-element.61.second_high, ...), custom_call_target="tpu_custom_call" | custom-call | flops 1610612736 | bytes 2097152 | tf_op jit(solution)/shard_map/pallas_call | solution.py:154
  164.3 0.7 copy-done.23
  164.9 2.0 collective-permute-start.32
  167.0 16.1 %collective-permute-done.30.refs_5_ = f32[256,256]{1,0:T(8,128)S(1)} collective-permute-done((f32[256,256]{1,0:T(8,128)}, f32[256,256]{1,0:T(8,128)S(1)}, u32[]{:S(2)}, u32[]{:S(2)}) %collective-permute-start.30) | collective-permute-done | bytes 262176 | tf_op jit(solution)/shard_map/ppermute | solution.py:375
  183.1 12.5 %collective-permute-start.25 = (f32[256,512]{1,0:T(8,128)}, f32[256,512]{1,0:T(8,128)S(1)}, u32[]{:S(2)}, u32[]{:S(2)}) collective-permute-start(f32[256,512]{1,0:T(8,128)} %get-tuple-element.73), channel_id=1, source_target_pairs={{0,8},{4,12},{8,0},{12,4},{1,9},{5,13},{9,1},{13,5},{2,10},{6,14},... | collective-permute-start | bytes 1572872 | tf_op jit(solution)/shard_map/ppermute | solution.py:375
  195.6 17.2 %collective-permute-done.31.refs_6_ = f32[256,256]{1,0:T(8,128)S(1)} collective-permute-done((f32[256,256]{1,0:T(8,128)}, f32[256,256]{1,0:T(8,128)S(1)}, u32[]{:S(2)}, u32[]{:S(2)}) %collective-permute-start.31) | collective-permute-done | bytes 262176 | tf_op jit(solution)/shard_map/ppermute | solution.py:375
  212.8 6.7 %shard_map.89 = (f32[256,256]{1,0:T(8,128)}, f32[256,256]{1,0:T(8,128)}, f32[256,256]{1,0:T(8,128)}, f32[256,256]{1,0:T(8,128)}) custom-call(bf16[512,1024]{1,0:T(8,128)(2,1)} %get-tuple-element.59.first_high, bf16[512,1024]{1,0:T(8,128)(2,1)} %get-tuple-element.60.first_low, bf16[1024,512]{1,0:T(8,128)(2,1)} %get-tuple-element.61.second_high, ...), custom_call_target="tpu_custom_call" | custom-call | flops 1610612736 | bytes 2097152 | tf_op jit(solution)/shard_map/pallas_call | solution.py:154
  219.5 3.8 %collective-permute-start.18 = (f32[256,256]{1,0:T(8,128)}, f32[256,256]{1,0:T(8,128)S(1)}, u32[]{:S(2)}, u32[]{:S(2)}) collective-permute-start(f32[256,256]{1,0:T(8,128)} %get-tuple-element.68), channel_id=1, source_target_pairs={{0,12},{4,0},{8,4},{12,8},{1,13},{5,1},{9,5},{13,9},{2,14},{6,2},{... | collective-permute-start | bytes 786440 | tf_op jit(solution)/shard_map/ppermute | solution.py:375
  223.3 0.7 copy-done.15
  225.3 2.0 shard_map.87.both_ref.refs_8_
  227.2 3.0 %shard_map.90 = (f32[256,256]{1,0:T(8,128)}, f32[256,256]{1,0:T(8,128)}, f32[256,256]{1,0:T(8,128)}, f32[256,256]{1,0:T(8,128)}) custom-call(s32[5]{0:T(128)} %stack.20.at_ref, bf16[512,512]{1,0:T(8,128)(2,1)} %shard_map.87.both_ref.refs_8_, s32[1,4096]{1,0:T(1,128)} %bitcast.39, f32[256,256]{1,0:T(8,128)} %get-tuple-element.63.back_ref, ...), custom_call_target="tpu_custom_call" | custom-call | flops 536870912 | bytes 2097152 | tf_op jit(solution)/shard_map/pallas_call | solution.py:354
  230.2 5.1 %shard_map.93.refs_10_ = f32[256,4096]{1,0:T(8,128)} custom-call(s32[5]{0:T(128)} %stack.20.at_ref, f32[256,256]{1,0:T(8,128)} %get-tuple-element.51.refs_9_.refs_0_, f32[256,256]{1,0:T(8,128)} %get-tuple-element.42.refs_0_.refs_1_, f32[256,256]{1,0:T(8,128)} %get-tuple-element.43.refs_1_.refs_2_, f32[256,256]{1,0:T(8,128)} %get-tuple-element.44.refs_2_.refs_3_, ...), custom_call_target="tpu_custom_call" | custom-call | flops 536870912 | bytes 3145728 | tf_op jit(solution)/shard_map/pallas_call | solution.py:324
  235.4 11.2 %collective-permute-done.25.refs_6_ = f32[256,512]{1,0:T(8,128)S(1)} collective-permute-done((f32[256,512]{1,0:T(8,128)}, f32[256,512]{1,0:T(8,128)S(1)}, u32[]{:S(2)}, u32[]{:S(2)}) %collective-permute-start.25) | collective-permute-done | bytes 524320 | tf_op jit(solution)/shard_map/ppermute | solution.py:375
  246.5 0.8 copy-done.4
  247.5 6.3 %shard_map.94.refs_7_ = f32[256,4096]{1,0:T(8,128)} custom-call(s32[5]{0:T(128)} %stack.20.at_ref, f32[256,512]{1,0:T(8,128)} %get-tuple-element.52.refs_10_.refs_0_, f32[256,512]{1,0:T(8,128)} %get-tuple-element.45.refs_3_.refs_1_, f32[256,512]{1,0:T(8,128)} %get-tuple-element.46.refs_4_.refs_2_, ...), custom_call_target="tpu_custom_call", output_to_operand_aliasing={{}: (11, {})} | custom-call | flops 1073741824 | bytes 6291456 | tf_op jit(solution)/shard_map/pallas_call | solution.py:324
  253.8 3.0 %collective-permute-done.19.refs_5_ = f32[256,256]{1,0:T(8,128)S(1)} collective-permute-done((f32[256,256]{1,0:T(8,128)}, f32[256,256]{1,0:T(8,128)S(1)}, u32[]{:S(2)}, u32[]{:S(2)}) %collective-permute-start.19) | collective-permute-done | bytes 262176 | tf_op jit(solution)/shard_map/ppermute | solution.py:375
  256.8 0.7 copy-done.13
  257.7 3.7 %shard_map.95 = f32[256,4096]{1,0:T(8,128)} custom-call(s32[5]{0:T(128)} %stack.20.at_ref, f32[256,256]{1,0:T(8,128)} %get-tuple-element.64.refs_0_, f32[256,256]{1,0:T(8,128)} %get-tuple-element.65.refs_1_, f32[256,256]{1,0:T(8,128)} %get-tuple-element.66.refs_2_, f32[256,256]{1,0:T(8,128)} %get-tuple-element.67.refs_3_, ...), custom_call_target="tpu_custom_call", output_to_operand_aliasing={{}: (8, {})} | custom-call | flops 1048576 | bytes 3145728 | tf_op jit(solution)/shard_map/pallas_call | solution.py:324
  (95 shorter events, 4.5 us)
Async XLA Ops:
  1.6 10.4 %collective-permute-start = (f32[1,2,32,512]{3,2,1,0:T(8,128)S(1)}, f32[1,2,32,512]{3,2,1,0:T(8,128)S(1)}, u32[]{:S(2)}, u32[]{:S(2)}) collective-permute-start(f32[1,2,32,512]{3,2,1,0:T(8,128)S(1)} %get-tuple-element.80), channel_id=1, source_target_pairs={{0,8},{4,12},{8,0},{12,4},{1,9},{5,13},{9,1},{13,5},{2,10},{6,14},... | collective-permute-start | bytes 393224 | tf_op jit(solution)/shard_map/ppermute | solution.py:378
  12.0 28.9 %copy-start.26 = (s32[4]{0:T(128)S(1)}, s32[4]{0:T(128)}, u32[]{:S(2)}) copy-start(s32[4]{0:T(128)} %index_ref.1) | copy-start | bytes 52
  12.0 7.5 %collective-permute-start.1 = (f32[2,2,32,512]{3,2,1,0:T(8,128)S(1)}, f32[2,2,32,512]{3,2,1,0:T(8,128)S(1)}, u32[]{:S(2)}, u32[]{:S(2)}) collective-permute-start(f32[2,2,32,512]{3,2,1,0:T(8,128)S(1)} %pad_maximum_fusion.1), channel_id=1, source_target_pairs={{0,4},{4,0},{8,12},{12,8},{1,5},{5,1},{9,13},{13,9},{2,6},{6,2},{1... | collective-permute-start | bytes 786440 | tf_op jit(solution)/shard_map/ppermute | solution.py:378
  19.6 12.3 %collective-permute-start.2 = (f32[4,2,32,512]{3,2,1,0:T(8,128)S(1)}, f32[4,2,32,512]{3,2,1,0:T(8,128)S(1)}, u32[]{:S(2)}, u32[]{:S(2)}) collective-permute-start(f32[4,2,32,512]{3,2,1,0:T(8,128)S(1)} %pad_maximum_fusion), channel_id=1, source_target_pairs={{0,2},{1,3},{2,0},{3,1},{4,6},{5,7},{6,4},{7,5},{8,10},{9,11},{10,... | collective-permute-start | bytes 1572872 | tf_op jit(solution)/shard_map/ppermute | solution.py:378
  20.9 12.7 %collective-permute-start.3 = (f32[4,2,32,512]{3,2,1,0:T(8,128)S(1)}, f32[4,2,32,512]{3,2,1,0:T(8,128)S(1)}, u32[]{:S(2)}, u32[]{:S(2)}) collective-permute-start(f32[4,2,32,512]{3,2,1,0:T(8,128)S(1)} %pad_maximum_fusion), channel_id=1, source_target_pairs={{0,16},{16,0},{1,17},{17,1},{2,18},{18,2},{3,19},{19,3},{4,20},{20... | collective-permute-start | bytes 1572872 | tf_op jit(solution)/shard_map/ppermute | solution.py:378
  31.9 6.6 %collective-permute-start.4 = (f32[2,2,32,512]{3,2,1,0:T(8,128)S(1)}, f32[2,2,32,512]{3,2,1,0:T(8,128)S(1)}, u32[]{:S(2)}, u32[]{:S(2)}) collective-permute-start(f32[2,2,32,512]{3,2,1,0:T(8,128)S(1)} %slice.24), channel_id=1, source_target_pairs={{0,16},{16,0},{1,17},{17,1},{2,18},{18,2},{3,19},{19,3},{4,20},{20... | collective-permute-start | bytes 786440 | tf_op jit(solution)/shard_map/ppermute | solution.py:378
  33.6 6.4 %collective-permute-start.5 = (f32[2,2,32,512]{3,2,1,0:T(8,128)S(1)}, f32[2,2,32,512]{3,2,1,0:T(8,128)S(1)}, u32[]{:S(2)}, u32[]{:S(2)}) collective-permute-start(f32[2,2,32,512]{3,2,1,0:T(8,128)S(1)} %slice.25), channel_id=1, source_target_pairs={{0,2},{1,3},{2,0},{3,1},{4,6},{5,7},{6,4},{7,5},{8,10},{9,11},{10,... | collective-permute-start | bytes 786440 | tf_op jit(solution)/shard_map/ppermute | solution.py:378
  40.9 31.0 %collective-permute-start.6 = (f32[16,2,32,512]{3,2,1,0:T(8,128)}, f32[16,2,32,512]{3,2,1,0:T(8,128)S(1)}, u32[]{:S(2)}, u32[]{:S(2)}) collective-permute-start(f32[16,2,32,512]{3,2,1,0:T(8,128)} %get-tuple-element.85), channel_id=1, source_target_pairs={{0,1},{1,0},{2,3},{3,2},{4,5},{5,4},{6,7},{7,6},{8,9},{9,8},{10,11... | collective-permute-start | bytes 6291464 | tf_op jit(solution)/shard_map/ppermute | solution.py:378
  51.1 10.4 %copy-start.1 = (f32[256,512]{1,0:T(8,128)S(1)}, f32[256,512]{1,0:T(8,128)}, u32[]{:S(2)}) copy-start(f32[256,512]{1,0:T(8,128)} %get-tuple-element.45.refs_3_.refs_1_) | copy-start | bytes 1572868
  51.1 12.9 %copy-start.2 = (f32[256,512]{1,0:T(8,128)S(1)}, f32[256,512]{1,0:T(8,128)}, u32[]{:S(2)}) copy-start(f32[256,512]{1,0:T(8,128)} %get-tuple-element.46.refs_4_.refs_2_) | copy-start | bytes 1572868
  51.1 17.9 %copy-start.18 = (s32[4096]{0:T(1024)S(1)}, s32[4096]{0:T(1024)}, u32[]{:S(2)}) copy-start(s32[4096]{0:T(1024)} %param.12) | copy-start | bytes 49156
  51.1 18.8 %copy-start.6 = (f32[256,256]{1,0:T(8,128)S(1)}, f32[256,256]{1,0:T(8,128)}, u32[]{:S(2)}) copy-start(f32[256,256]{1,0:T(8,128)} %get-tuple-element.42.refs_0_.refs_1_) | copy-start | bytes 786436
  56.9 2.2 collective-permute-start.7
  60.3 9.6 %collective-permute-start.8 = (f32[256,256]{1,0:T(8,128)S(1)}, f32[256,256]{1,0:T(8,128)S(1)}, u32[]{:S(2)}, u32[]{:S(2)}) collective-permute-start(f32[256,256]{1,0:T(8,128)S(1)} %slice.27), channel_id=1, source_target_pairs={{0,2},{1,3},{2,0},{3,1},{4,6},{5,7},{6,4},{7,5},{8,10},{9,11},{10,... | collective-permute-start | bytes 786440 | tf_op jit(solution)/shard_map/ppermute | solution.py:378
  61.5 52.7 %collective-permute-start.21 = (f32[256,512]{1,0:T(8,128)S(1)}, f32[256,512]{1,0:T(8,128)}, u32[]{:S(2)}, u32[]{:S(2)}) collective-permute-start(f32[256,512]{1,0:T(8,128)S(1)} %copy-done.1), channel_id=1, source_target_pairs={{0,4},{4,8},{8,12},{12,0},{1,5},{5,9},{9,13},{13,1},{2,6},{6,10},{... | collective-permute-start | bytes 1572872 | tf_op jit(solution)/shard_map/ppermute | solution.py:375
  64.0 52.1 %collective-permute-start.22 = (f32[256,512]{1,0:T(8,128)S(1)}, f32[256,512]{1,0:T(8,128)}, u32[]{:S(2)}, u32[]{:S(2)}) collective-permute-start(f32[256,512]{1,0:T(8,128)S(1)} %copy-done.2), channel_id=1, source_target_pairs={{0,8},{4,12},{8,0},{12,4},{1,9},{5,13},{9,1},{13,5},{2,10},{6,14},... | collective-permute-start | bytes 1572872 | tf_op jit(solution)/shard_map/ppermute | solution.py:375
  67.4 50.2 %collective-permute-start.23 = (f32[256,512]{1,0:T(8,128)}, f32[256,512]{1,0:T(8,128)}, u32[]{:S(2)}, u32[]{:S(2)}) collective-permute-start(f32[256,512]{1,0:T(8,128)} %get-tuple-element.47.refs_5_.refs_3_), channel_id=1, source_target_pairs={{0,12},{4,0},{8,4},{12,8},{1,13},{5,1},{9,5},{13,9},{2,14},{6,2},{... | collective-permute-start | bytes 1572872 | tf_op jit(solution)/shard_map/ppermute | solution.py:375
  69.9 82.2 %collective-permute-start.27 = (f32[256,256]{1,0:T(8,128)S(1)}, f32[256,256]{1,0:T(8,128)}, u32[]{:S(2)}, u32[]{:S(2)}) collective-permute-start(f32[256,256]{1,0:T(8,128)S(1)} %copy-done.6), channel_id=1, source_target_pairs={{0,4},{4,8},{8,12},{12,0},{1,5},{5,9},{9,13},{13,1},{2,6},{6,10},{... | collective-permute-start | bytes 786440 | tf_op jit(solution)/shard_map/ppermute | solution.py:375
  71.8 9.5 %collective-permute-start.13 = (f32[8,512]{1,0:T(8,128)S(1)}, f32[8,512]{1,0:T(8,128)S(1)}, u32[]{:S(2)}, u32[]{:S(2)}) collective-permute-start(f32[8,512]{1,0:T(8,128)S(1)} %broadcast_in_dim.23), channel_id=1, source_target_pairs={{0,1},{1,0},{2,3},{3,2},{4,5},{5,4},{6,7},{7,6},{8,9},{9,8},{10,11... | collective-permute-start | bytes 49160 | tf_op jit(solution)/shard_map/ppermute | solution.py:378
  81.4 31.3 %copy-start.7 = (f32[256,256]{1,0:T(8,128)S(1)}, f32[256,256]{1,0:T(8,128)}, u32[]{:S(2)}) copy-start(f32[256,256]{1,0:T(8,128)} %get-tuple-element.43.refs_1_.refs_2_) | copy-start | bytes 786436
  81.4 32.8 %copy-start.16 = (f32[256,128]{1,0:T(8,128)S(1)}, f32[256,128]{1,0:T(8,128)}, u32[]{:S(2)}) copy-start(f32[256,128]{1,0:T(8,128)} %get-tuple-element.58) | copy-start | bytes 393220
  81.4 32.8 %copy-start.8 = (f32[256,256]{1,0:T(8,128)S(1)}, f32[256,256]{1,0:T(8,128)}, u32[]{:S(2)}) copy-start(f32[256,256]{1,0:T(8,128)} %get-tuple-element.44.refs_2_.refs_3_) | copy-start | bytes 786436
  81.4 31.3 %collective-permute-start.9 = (f32[512,128]{1,0:T(8,128)}, f32[512,128]{1,0:T(8,128)S(1)}, u32[]{:S(2)}, u32[]{:S(2)}) collective-permute-start(f32[512,128]{1,0:T(8,128)} %get-tuple-element.57), channel_id=1, source_target_pairs={{0,4},{4,0},{8,12},{12,8},{1,5},{5,1},{9,13},{13,9},{2,6},{6,2},{1... | collective-permute-start | bytes 786440 | tf_op jit(solution)/shard_map/ppermute | solution.py:378
  112.7 39.7 %collective-permute-start.28 = (f32[256,256]{1,0:T(8,128)S(1)}, f32[256,256]{1,0:T(8,128)}, u32[]{:S(2)}, u32[]{:S(2)}) collective-permute-start(f32[256,256]{1,0:T(8,128)S(1)} %copy-done.7), channel_id=1, source_target_pairs={{0,8},{4,12},{8,0},{12,4},{1,9},{5,13},{9,1},{13,5},{2,10},{6,14},... | collective-permute-start | bytes 786440 | tf_op jit(solution)/shard_map/ppermute | solution.py:375
  114.2 42.6 %collective-permute-start.29 = (f32[256,256]{1,0:T(8,128)S(1)}, f32[256,256]{1,0:T(8,128)S(1)}, u32[]{:S(2)}, u32[]{:S(2)}) collective-permute-start(f32[256,256]{1,0:T(8,128)S(1)} %copy-done.8), channel_id=1, source_target_pairs={{0,12},{4,0},{8,4},{12,8},{1,13},{5,1},{9,5},{13,9},{2,14},{6,2},{... | collective-permute-start | bytes 786440 | tf_op jit(solution)/shard_map/ppermute | solution.py:375
  116.1 18.0 %collective-permute-start.14 = (f32[8,512]{1,0:T(8,128)S(1)}, f32[8,512]{1,0:T(8,128)S(1)}, u32[]{:S(2)}, u32[]{:S(2)}) collective-permute-start(f32[8,512]{1,0:T(8,128)S(1)} %broadcast_add_fusion), channel_id=1, source_target_pairs={{0,2},{1,3},{2,0},{3,1},{4,6},{5,7},{6,4},{7,5},{8,10},{9,11},{10,... | collective-permute-start | bytes 49160 | tf_op jit(solution)/shard_map/ppermute | solution.py:378
  117.5 34.6 %collective-permute-start.10 = (f32[256,128]{1,0:T(8,128)S(1)}, f32[256,128]{1,0:T(8,128)S(1)}, u32[]{:S(2)}, u32[]{:S(2)}) collective-permute-start(f32[256,128]{1,0:T(8,128)S(1)} %slice_add_fusion.1), channel_id=1, source_target_pairs={{0,8},{4,12},{8,0},{12,4},{1,9},{5,13},{9,1},{13,5},{2,10},{6,14},... | collective-permute-start | bytes 393224 | tf_op jit(solution)/shard_map/ppermute | solution.py:378
  123.7 10.4 %copy-start.19 = (f32[256,256]{1,0:T(8,128)S(1)}, f32[256,256]{1,0:T(8,128)}, u32[]{:S(2)}) copy-start(f32[256,256]{1,0:T(8,128)} %get-tuple-element.48.refs_6_.refs_1_) | copy-start | bytes 786436
  123.7 28.4 %copy-start.20 = (f32[256,256]{1,0:T(8,128)S(1)}, f32[256,256]{1,0:T(8,128)}, u32[]{:S(2)}) copy-start(f32[256,256]{1,0:T(8,128)} %get-tuple-element.49.refs_7_.refs_2_) | copy-start | bytes 786436
  123.7 28.4 %copy-start.17 = (f32[256,128]{1,0:T(8,128)S(1)}, f32[256,128]{1,0:T(8,128)}, u32[]{:S(2)}) copy-start(f32[256,128]{1,0:T(8,128)} %get-tuple-element.56) | copy-start | bytes 393220
  123.7 28.4 %copy-start.21 = (f32[256,256]{1,0:T(8,128)S(1)}, f32[256,256]{1,0:T(8,128)}, u32[]{:S(2)}) copy-start(f32[256,256]{1,0:T(8,128)} %get-tuple-element.50.refs_8_.refs_3_) | copy-start | bytes 786436
  134.1 30.0 %collective-permute-start.15 = (f32[256,256]{1,0:T(8,128)S(1)}, f32[256,256]{1,0:T(8,128)S(1)}, u32[]{:S(2)}, u32[]{:S(2)}) collective-permute-start(f32[256,256]{1,0:T(8,128)S(1)} %copy-done.19), channel_id=1, source_target_pairs={{0,4},{4,8},{8,12},{12,0},{1,5},{5,9},{9,13},{13,1},{2,6},{6,10},{... | collective-permute-start | bytes 786440 | tf_op jit(solution)/shard_map/ppermute | solution.py:375
  152.1 12.1 %collective-permute-start.16 = (f32[256,256]{1,0:T(8,128)S(1)}, f32[256,256]{1,0:T(8,128)S(1)}, u32[]{:S(2)}, u32[]{:S(2)}) collective-permute-start(f32[256,256]{1,0:T(8,128)S(1)} %copy-done.20), channel_id=1, source_target_pairs={{0,8},{4,12},{8,0},{12,4},{1,9},{5,13},{9,1},{13,5},{2,10},{6,14},... | collective-permute-start | bytes 786440 | tf_op jit(solution)/shard_map/ppermute | solution.py:375
  152.2 14.8 %collective-permute-start.17 = (f32[256,256]{1,0:T(8,128)S(1)}, f32[256,256]{1,0:T(8,128)S(1)}, u32[]{:S(2)}, u32[]{:S(2)}) collective-permute-start(f32[256,256]{1,0:T(8,128)S(1)} %copy-done.21), channel_id=1, source_target_pairs={{0,12},{4,0},{8,4},{12,8},{1,13},{5,1},{9,5},{13,9},{2,14},{6,2},{... | collective-permute-start | bytes 786440 | tf_op jit(solution)/shard_map/ppermute | solution.py:375
  152.4 70.9 %collective-permute-start.24 = (f32[256,512]{1,0:T(8,128)}, f32[256,512]{1,0:T(8,128)S(1)}, u32[]{:S(2)}, u32[]{:S(2)}) collective-permute-start(f32[256,512]{1,0:T(8,128)} %get-tuple-element.72), channel_id=1, source_target_pairs={{0,12},{4,0},{8,4},{12,8},{1,13},{5,1},{9,5},{13,9},{2,14},{6,2},{... | collective-permute-start | bytes 1572872 | tf_op jit(solution)/shard_map/ppermute | solution.py:375
  156.8 0.7 copy-start.25
  156.8 7.5 %collective-permute-start.11 = (f32[256,128]{1,0:T(8,128)S(1)}, f32[256,128]{1,0:T(8,128)S(1)}, u32[]{:S(2)}, u32[]{:S(2)}) collective-permute-start(f32[256,128]{1,0:T(8,128)S(1)} %fusion), channel_id=1, source_target_pairs={{0,2},{1,3},{2,0},{3,1},{4,6},{5,7},{6,4},{7,5},{8,10},{9,11},{10,... | collective-permute-start | bytes 393224 | tf_op jit(solution)/shard_map/ppermute | solution.py:378
  164.1 19.0 %copy-start.22 = (f32[256,256]{1,0:T(8,128)}, f32[256,256]{1,0:T(8,128)S(1)}, u32[]{:S(2)}) copy-start(f32[256,256]{1,0:T(8,128)S(1)} %collective-permute-done.15.refs_1_) | copy-start | bytes 786436
  164.1 19.0 %collective-permute-start.30 = (f32[256,256]{1,0:T(8,128)}, f32[256,256]{1,0:T(8,128)S(1)}, u32[]{:S(2)}, u32[]{:S(2)}) collective-permute-start(f32[256,256]{1,0:T(8,128)} %get-tuple-element.76), channel_id=1, source_target_pairs={{0,12},{4,0},{8,4},{12,8},{1,13},{5,1},{9,5},{13,9},{2,14},{6,2},{... | collective-permute-start | bytes 786440 | tf_op jit(solution)/shard_map/ppermute | solution.py:375
  164.2 0.7 copy-start.23
  164.2 48.5 %collective-permute-start.31 = (f32[256,256]{1,0:T(8,128)}, f32[256,256]{1,0:T(8,128)S(1)}, u32[]{:S(2)}, u32[]{:S(2)}) collective-permute-start(f32[256,256]{1,0:T(8,128)} %get-tuple-element.77), channel_id=1, source_target_pairs={{0,8},{4,12},{8,0},{12,4},{1,9},{5,13},{9,1},{13,5},{2,10},{6,14},... | collective-permute-start | bytes 786440 | tf_op jit(solution)/shard_map/ppermute | solution.py:375
  164.9 54.6 %collective-permute-start.32 = (f32[256,256]{1,0:T(8,128)}, f32[256,256]{1,0:T(8,128)S(1)}, u32[]{:S(2)}, u32[]{:S(2)}) collective-permute-start(f32[256,256]{1,0:T(8,128)} %get-tuple-element.78), channel_id=1, source_target_pairs={{0,4},{4,8},{8,12},{12,0},{1,5},{5,9},{9,13},{13,1},{2,6},{6,10},{... | collective-permute-start | bytes 786440 | tf_op jit(solution)/shard_map/ppermute | solution.py:375
  166.9 58.4 %copy-start = (f32[256,256]{1,0:T(8,128)}, f32[256,256]{1,0:T(8,128)S(1)}, u32[]{:S(2)}) copy-start(f32[256,256]{1,0:T(8,128)S(1)} %pad_maximum_fusion.2.here_ref) | copy-start | bytes 786436
  167.0 16.2 %copy-start.24 = (f32[256,256]{1,0:T(8,128)}, f32[256,256]{1,0:T(8,128)S(1)}, u32[]{:S(2)}) copy-start(f32[256,256]{1,0:T(8,128)S(1)} %collective-permute-done.17.refs_3_) | copy-start | bytes 786436
  167.0 56.3 %collective-permute-start.12 = (f32[256,256]{1,0:T(8,128)S(1)}, f32[256,256]{1,0:T(8,128)S(1)}, u32[]{:S(2)}, u32[]{:S(2)}) collective-permute-start(f32[256,256]{1,0:T(8,128)S(1)} %pad_maximum_fusion.2.here_ref), channel_id=1, source_target_pairs={{0,1},{1,0},{2,3},{3,2},{4,5},{5,4},{6,7},{7,6},{8,9},{9,8},{10,11... | collective-permute-start | bytes 786440 | tf_op jit(solution)/shard_map/ppermute | solution.py:378
  183.1 47.1 %copy-start.9 = (f32[256,256]{1,0:T(8,128)}, f32[256,256]{1,0:T(8,128)S(1)}, u32[]{:S(2)}) copy-start(f32[256,256]{1,0:T(8,128)S(1)} %collective-permute-done.30.refs_5_) | copy-start | bytes 786436
  183.1 63.4 %collective-permute-start.25 = (f32[256,512]{1,0:T(8,128)}, f32[256,512]{1,0:T(8,128)S(1)}, u32[]{:S(2)}, u32[]{:S(2)}) collective-permute-start(f32[256,512]{1,0:T(8,128)} %get-tuple-element.73), channel_id=1, source_target_pairs={{0,8},{4,12},{8,0},{12,4},{1,9},{5,13},{9,1},{13,5},{2,10},{6,14},... | collective-permute-start | bytes 1572872 | tf_op jit(solution)/shard_map/ppermute | solution.py:375
  212.8 17.4 %copy-start.10 = (f32[256,256]{1,0:T(8,128)}, f32[256,256]{1,0:T(8,128)S(1)}, u32[]{:S(2)}) copy-start(f32[256,256]{1,0:T(8,128)S(1)} %collective-permute-done.31.refs_6_) | copy-start | bytes 786436
  212.8 33.8 %collective-permute-start.26 = (f32[256,512]{1,0:T(8,128)}, f32[256,512]{1,0:T(8,128)S(1)}, u32[]{:S(2)}, u32[]{:S(2)}) collective-permute-start(f32[256,512]{1,0:T(8,128)} %get-tuple-element.74), channel_id=1, source_target_pairs={{0,4},{4,8},{8,12},{12,0},{1,5},{5,9},{9,13},{13,1},{2,6},{6,10},{... | collective-permute-start | bytes 1572872 | tf_op jit(solution)/shard_map/ppermute | solution.py:375
  219.5 10.7 %copy-start.11 = (f32[256,256]{1,0:T(8,128)}, f32[256,256]{1,0:T(8,128)S(1)}, u32[]{:S(2)}) copy-start(f32[256,256]{1,0:T(8,128)S(1)} %collective-permute-done.32.refs_7_) | copy-start | bytes 786436
  219.5 34.3 %collective-permute-start.18 = (f32[256,256]{1,0:T(8,128)}, f32[256,256]{1,0:T(8,128)S(1)}, u32[]{:S(2)}, u32[]{:S(2)}) collective-permute-start(f32[256,256]{1,0:T(8,128)} %get-tuple-element.68), channel_id=1, source_target_pairs={{0,12},{4,0},{8,4},{12,8},{1,13},{5,1},{9,5},{13,9},{2,14},{6,2},{... | collective-permute-start | bytes 786440 | tf_op jit(solution)/shard_map/ppermute | solution.py:375
  223.3 12.1 %copy-start.3 = (f32[256,512]{1,0:T(8,128)}, f32[256,512]{1,0:T(8,128)S(1)}, u32[]{:S(2)}) copy-start(f32[256,512]{1,0:T(8,128)S(1)} %collective-permute-done.24.refs_5_) | copy-start | bytes 1572868
  223.3 33.5 %collective-permute-start.19 = (f32[256,256]{1,0:T(8,128)}, f32[256,256]{1,0:T(8,128)S(1)}, u32[]{:S(2)}, u32[]{:S(2)}) collective-permute-start(f32[256,256]{1,0:T(8,128)} %get-tuple-element.69), channel_id=1, source_target_pairs={{0,8},{4,12},{8,0},{12,4},{1,9},{5,13},{9,1},{13,5},{2,10},{6,14},... | collective-permute-start | bytes 786440 | tf_op jit(solution)/shard_map/ppermute | solution.py:375
  223.3 0.8 copy-start.15
  224.1 32.8 %collective-permute-start.20 = (f32[256,256]{1,0:T(8,128)}, f32[256,256]{1,0:T(8,128)S(1)}, u32[]{:S(2)}, u32[]{:S(2)}) collective-permute-start(f32[256,256]{1,0:T(8,128)} %get-tuple-element.70), channel_id=1, source_target_pairs={{0,4},{4,8},{8,12},{12,0},{1,5},{5,9},{9,13},{13,1},{2,6},{6,10},{... | collective-permute-start | bytes 786440 | tf_op jit(solution)/shard_map/ppermute | solution.py:375
  246.5 0.8 copy-start.4
  246.5 1.0 copy-start.5
  253.8 3.0 %copy-start.12 = (f32[256,256]{1,0:T(8,128)}, f32[256,256]{1,0:T(8,128)S(1)}, u32[]{:S(2)}) copy-start(f32[256,256]{1,0:T(8,128)S(1)} %collective-permute-done.18.refs_4_) | copy-start | bytes 786436
  256.8 0.7 copy-start.13
  256.8 0.8 copy-start.14

commit v3 on v2

--- a/solution.py
+++ b/solution.py
@@ -8,7 +8,8 @@
 
 BLOCK = 1024
 NBIN = 512
-PIECES = ((0, 256), (512, 512), (256, 256))
+PIECES = ((0, 256), (512, 512), (256, 128), (384, 128))
+LATE = 2
 
 
 def gathered_sums(tod, gain_knots, intervals, fraction, azimuth, mode_index, mode_bank, mode_mix):
@@ -163,6 +164,55 @@
     )(*modes, *arrived)
 
 
+def share_kernel(part_ref, bank_ref, out_ref):
+    out_ref[0] = bank_ref[...]
+
+
+def own_share(part, mode_bank, shares):
+    count, rows, m = mode_bank.shape
+    return pl.pallas_call(
+        share_kernel,
+        out_shape=jax.ShapeDtypeStruct((1, count, rows // shares, m), jnp.float32),
+        grid_spec=pltpu.PrefetchScalarGridSpec(
+            num_scalar_prefetch=1,
+            grid=(1,),
+            in_specs=[pl.BlockSpec((count, rows // shares, m), lambda i, part_ref: (0, part_ref[0], 0))],
+            out_specs=pl.BlockSpec((1, count, rows // shares, m), lambda i, part_ref: (0, 0, 0, 0)),
+        ),
+    )(part, mode_bank)
+
+
+def last_kernel(ring, start, at_ref, *refs):
+    data, back = refs[:ring], refs[ring : 2 * ring - 1]
+    out_ref, held, done = refs[-3:]
+    copies = []
+    for s in range(ring):
+        held[s] = data[s][...] - back[s - 1][...] if s else data[s][...]
+        column = pl.ds(block_start(ring, at_ref[0], s, start), held.shape[2])
+        copies.append(pltpu.make_async_copy(held.at[s], out_ref.at[:, column], done.at[s]))
+        copies[s].start()
+    for copy in copies:
+        copy.wait()
+
+
+def last_piece(ring, at, start, data, back, old):
+    rows, width = data[0].shape
+    return pl.pallas_call(
+        functools.partial(last_kernel, ring, start),
+        out_shape=jax.ShapeDtypeStruct(old.shape, jnp.float32),
+        in_specs=[pl.BlockSpec(memory_space=pltpu.SMEM)]
+        + [pl.BlockSpec(memory_space=pltpu.VMEM)] * (2 * ring - 1)
+        + [pl.BlockSpec(memory_space=pl.ANY)],
+        out_specs=pl.BlockSpec(memory_space=pl.ANY),
+        scratch_shapes=[pltpu.VMEM((ring, rows, width), jnp.float32), pltpu.SemaphoreType.DMA((ring,))],
+        input_output_aliases={2 * ring: 0},
+        compiler_params=pltpu.CompilerParams(vmem_limit_bytes=65_000_000),
+        cost_estimate=pl.CostEstimate(
+            flops=ring * rows * width, bytes_accessed=12 * ring * rows * width, transcendentals=0
+        ),
+    )(at, *data, *back, old)
+
+
 def onehot_of(azimuth, bins):
     row = lax.broadcasted_iota(jnp.int32, (bins, azimuth.shape[1]), 0)
     return (row == azimuth).astype(jnp.float32).astype(jnp.bfloat16)
@@ -286,23 +336,18 @@
     )(at, here, there, counts)
 
 
-def finish_kernel(ring, count, template, at_ref, *refs):
-    data, back, refs, out_ref = refs[:ring], refs[ring : ring + count], refs[ring + count : -1], refs[-1]
-    step = pl.program_id(0)
+def finish_kernel(ring, at_ref, *refs):
+    data, back = refs[:ring], refs[ring : 2 * ring]
+    both_ref, azimuth_ref = refs[2 * ring : 2 * ring + 2]
+    out_ref = refs[-1]
+    rows = out_ref.shape[0]
+    levels = dot(both_ref[...], onehot_of(azimuth_ref[...], both_ref.shape[1]))
+    levels = levels[:rows] + levels[rows:]
     for s in range(ring):
 
-        @pl.when(step == s)
+        @pl.when(pl.program_id(0) == s)
         def _():
-            if s < ring - count:
-                out_ref[...] = data[s][...]
-            else:
-                out_ref[...] = data[s][...] - back[s - ring + count][...]
-
-    if template:
-        both_ref, azimuth_ref = refs[:2]
-        rows = out_ref.shape[0]
-        levels = dot(both_ref[...], onehot_of(azimuth_ref[...], both_ref.shape[1]))
-        out_ref[...] -= levels[:rows] + levels[rows:]
+            out_ref[...] = data[s][...] - back[s][...] - levels
 
 
 def finish_piece(ring, at, start, data, back, template, azimuth, old):
@@ -313,16 +358,14 @@
     def where(s, at_ref):
         return 0, lax.rem(at_ref[0] + s, ring) * per_block + offset
 
-    specs = [pl.BlockSpec((rows, width), lambda s, at_ref: (0, 0))] * (len(data) + len(back))
-    operands = [*data, *back]
-    if template is not None:
-        specs += [pl.BlockSpec(template.shape, lambda s, at_ref: (0, 0)), pl.BlockSpec((1, width), where)]
-        operands += [template, azimuth]
+    operands = [*data, *back, template, azimuth]
+    specs = [pl.BlockSpec((rows, width), lambda s, at_ref: (0, 0))] * (2 * ring)
+    specs += [pl.BlockSpec(template.shape, lambda s, at_ref: (0, 0)), pl.BlockSpec((1, width), where)]
     if old is not None:
         specs += [pl.BlockSpec(memory_space=pl.ANY)]
         operands += [old]
     return pl.pallas_call(
-        functools.partial(finish_kernel, ring, len(back), template is not None),
+        functools.partial(finish_kernel, ring),
         out_shape=jax.ShapeDtypeStruct((rows, samples), jnp.float32),
         grid_spec=pltpu.PrefetchScalarGridSpec(
             num_scalar_prefetch=1,
@@ -332,9 +375,7 @@
         ),
         input_output_aliases={len(operands): 0} if old is not None else {},
         cost_estimate=pl.CostEstimate(
-            flops=4 * ring * rows * width * (NBIN if template is not None else 1),
-            bytes_accessed=12 * ring * rows * width,
-            transcendentals=0,
+            flops=4 * ring * rows * width * NBIN, bytes_accessed=12 * ring * rows * width, transcendentals=0
         ),
     )(at, *operands)
 
@@ -389,8 +430,7 @@
             data[s, start] = block
             arrived[s, start] = send(block, s) if s else block
 
-    rows = det_rows // shares
-    banks = lax.dynamic_slice_in_dim(mode_bank, part_of * rows, rows, 1)[None]
+    banks = own_share(jnp.full((1,), part_of, jnp.int32), mode_bank, shares)
     for bit in (2, 1):
         banks = jnp.concatenate([banks, swap(banks, "det", bit)], axis=0)
     by_x = swap(banks, "tm", 2)
@@ -423,10 +463,11 @@
         removed = common_mode(ring, modes, [arrived[s, start] for s in range(ring)])
         back = [send(removed[s], -s) if s else removed[s] for s in range(ring)]
         mine = [data[s, start] for s in range(ring)]
-        if part == len(PIECES) - 1:
+        if part < len(PIECES) - LATE:
+            out = finish_piece(ring, at, start, mine, back, template, azimuth, out)
+        else:
             mine = level_piece(ring, at, start, mine, back[0], template, azimuth)
-            back, template = back[1:], None
-        out = finish_piece(ring, at, start, mine, back, template, azimuth, out)
+            out = last_piece(ring, at, start, mine, back[1:], out)
     return out
 
 

time: 262 us -> 301 us (1.15)
  waiting for transfers between devices: 111 us -> 133 us
  Pallas kernels: 72.1 us -> 85.2 us
  other arithmetic: 3.51 us -> 7.71 us
    ppermute x18 -> x24, waiting for transfers between devices: 47.5 us -> 67.8 us  [send(): lax.ppermute(array, 'det', [(i, (i + shift) % ring) for i in range(ring)])]
    pallas_call x3 -> x4, Pallas kernels: 23.6 us -> 29.7 us  [common_mode(): pl.pallas_call(functools.partial(filter_kernel, ring), out_shape=[jax.Sha...]
    ppermute x18 -> x24, starting transfers between devices: 36.6 us -> 42.5 us  [send(): lax.ppermute(array, 'det', [(i, (i + shift) % ring) for i in range(ring)])]
    ppermute x15, starting transfers between devices: 23 us -> 18.9 us  [swap(): lax.ppermute(array, axis, [(i, i ^ bit) for i in range(lax.axis_size(axis...]
    unnamed x61 -> x96, local copies, waits for them, and re-layouts: 10.3 us -> 7.82 us
    pallas_call x3 -> x5, Pallas kernels: 15.1 us -> 17.2 us  [the longest x2 11.5 us: finish_piece(): pl.pallas_call(functools.partial(finish_kernel, ring), out_shape=jax.Shap...]
    pallas_call x3 -> x4, Pallas kernels: 8.33 us -> 10.2 us  [calibrate(): pl.pallas_call(functools.partial(calibrate_kernel, len(pieces)), out_shap...]
  transfers between devices with their start and end apart: 33 -> 39, of which waited for: 13 -> 14; matrix products, arithmetic and copies ran while one was open for 5% -> 5% of each run, Pallas kernels for 26% -> 24%
where the time goes in v3:
time: 301 us
  waiting for transfers between devices  133 us (44%)
  Pallas kernels  85.2 us (28%)
  starting transfers between devices  61.4 us (20%)
  local copies, waits for them, and re-layouts  12.2 us (4%)
  other arithmetic  7.71 us (3%)
    ppermute x24, waiting for transfers between devices, send(): lax.ppermute(array, 'det', [(i, (i + shift) % ring) for i in range(ring)])  67.8 us
    ppermute x15, waiting for transfers between devices, swap(): lax.ppermute(array, axis, [(i, i ^ bit) for i in range(lax.axis_size(axis...  65.7 us
    ppermute x24, starting transfers between devices, send(): lax.ppermute(array, 'det', [(i, (i + shift) % ring) for i in range(ring)])  42.5 us
    pallas_call x4, Pallas kernels, common_mode(): pl.pallas_call(functools.partial(filter_kernel, ring), out_shape=[jax.Sha...  29.7 us
    ppermute x15, starting transfers between devices, swap(): lax.ppermute(array, axis, [(i, i ^ bit) for i in range(lax.axis_size(axis...  18.9 us
    pallas_call x2, Pallas kernels, finish_piece(): pl.pallas_call(functools.partial(finish_kernel, ring), out_shape=jax.Shap...  11.5 us
    pallas_call x4, Pallas kernels, calibrate(): pl.pallas_call(functools.partial(calibrate_kernel, len(pieces)), out_shap...  10.2 us
    pallas_call x1, Pallas kernels, pool(): pl.pallas_call(functools.partial(pool_kernel, ring, shares), out_shape=[j...  8.11 us
  transfers between devices with their start and end apart: 39, of which 14 were waited for; matrix products, arithmetic and copies ran while one was open for 5% of the time, Pallas kernels for 24%

profile of v3, /device:TPU:0, one launch (start us, length us, event | category | flops | bytes accessed | tf_op | source)
XLA Modules:
  0.0 300.6 jit_solution(12534056000619031705)
XLA Ops:
  0.0 1.6 shard_map.82
  1.6 4.1 %collective-permute-start = (f32[1,2,32,512]{3,2,1,0:T(8,128)}, f32[1,2,32,512]{3,2,1,0:T(8,128)S(1)}, u32[]{:S(2)}, u32[]{:S(2)}) collective-permute-start(f32[1,2,32,512]{3,2,1,0:T(8,128)} %shard_map.82), channel_id=1, source_target_pairs={{0,8},{4,12},{8,0},{12,4},{1,9},{5,13},{9,1},{13,5},{2,10},{6,14},... | collective-permute-start | bytes 393224 | tf_op jit(solution)/shard_map/ppermute | solution.py:419
  5.6 6.5 %collective-permute-done = f32[1,2,32,512]{3,2,1,0:T(8,128)S(1)} collective-permute-done((f32[1,2,32,512]{3,2,1,0:T(8,128)}, f32[1,2,32,512]{3,2,1,0:T(8,128)S(1)}, u32[]{:S(2)}, u32[]{:S(2)}) %collective-permute-start) | collective-permute-done | bytes 131104 | tf_op jit(solution)/shard_map/ppermute | solution.py:419
  12.1 0.9 pad_maximum_fusion.1
  14.0 6.6 %collective-permute-done.1 = f32[2,2,32,512]{3,2,1,0:T(8,128)S(1)} collective-permute-done((f32[2,2,32,512]{3,2,1,0:T(8,128)S(1)}, f32[2,2,32,512]{3,2,1,0:T(8,128)S(1)}, u32[]{:S(2)}, u32[]{:S(2)}) %collective-permute-start.1) | collective-permute-done | bytes 262176 | tf_op jit(solution)/shard_map/ppermute | solution.py:419
  20.6 0.9 pad_maximum_fusion
  21.6 1.4 collective-permute-start.2
  23.0 1.5 collective-permute-start.3
  24.5 1.6 constant_dynamic-update-slice_fusion.6
  27.7 6.2 %collective-permute-done.2 = f32[4,2,32,512]{3,2,1,0:T(8,128)S(1)} collective-permute-done((f32[4,2,32,512]{3,2,1,0:T(8,128)S(1)}, f32[4,2,32,512]{3,2,1,0:T(8,128)S(1)}, u32[]{:S(2)}, u32[]{:S(2)}) %collective-permute-start.2) | collective-permute-done | bytes 524320 | tf_op jit(solution)/shard_map/ppermute | solution.py:419
  33.9 1.4 collective-permute-start.4
  35.8 1.1 collective-permute-start.5
  36.9 1.1 constant_dynamic-update-slice_fusion.3
  38.0 1.1 constant_dynamic-update-slice_fusion.2
  39.1 1.5 collective-permute-done.4
  43.8 1.3 stack.20.at_ref
  45.0 2.1 shard_map.85
  47.2 2.3 shard_map.83
  49.5 2.9 shard_map.86
  52.3 2.9 shard_map.84
  55.2 6.2 %shard_map.87 = (f32[256,512]{1,0:T(8,128)}, f32[256,512]{1,0:T(8,128)}) custom-call(s32[5]{0:T(128)} %stack.20.at_ref, s32[4]{0:T(128)} %index_ref.1, s32[1,4096]{1,0:T(1,128)} %bitcast.44, f32[256,256]{1,0:T(8,128)} %get-tuple-element.54.refs_0_.refs_1_, f32[256,256]{1,0:T(8,128)} %get-tuple-element.55.refs_1_.refs_2_, ...), custom_call_target="tpu_custom_call" | custom-call | flops 2147483648 | bytes 4194304 | tf_op jit(solution)/shard_map/pallas_call | solution.py:247
  61.9 1.7 collective-permute-done.7
  63.7 1.1 add.24
  64.8 1.1 collective-permute-start.8
  65.9 7.5 %collective-permute-done.8 = f32[256,256]{1,0:T(8,128)S(1)} collective-permute-done((f32[256,256]{1,0:T(8,128)S(1)}, f32[256,256]{1,0:T(8,128)S(1)}, u32[]{:S(2)}, u32[]{:S(2)}) %collective-permute-start.8) | collective-permute-done | bytes 262176 | tf_op jit(solution)/shard_map/ppermute | solution.py:419
  74.2 1.5 constant_dynamic-update-slice_fusion.7.bank_ref
  75.8 8.1 %shard_map.88 = (f32[256,128]{1,0:T(8,128)}, f32[256,128]{1,0:T(8,128)}, f32[512,128]{1,0:T(8,128)}) custom-call(s32[5]{0:T(128)} %stack.20.at_ref, f32[32,2,32,512]{3,2,1,0:T(8,128)} %constant_dynamic-update-slice_fusion.7.bank_ref, f32[2,256,512]{2,1,0:T(8,128)} %own_ref.1, f32[2,512,512]{2,1,0:T(8,128)} %mix_ref.3, f32[256,256]{1,0:T(8,128)} %slice_add_fusion.sums_ref), custom_call_target="tpu_custom_call" | custom-call | flops 2013265920 | bytes 4194304 | tf_op jit(solution)/shard_map/pallas_call | solution.py:296
  83.9 2.1 collective-permute-start.9
  87.1 4.0 %collective-permute-start.22 = (f32[256,128]{1,0:T(8,128)S(1)}, f32[256,128]{1,0:T(8,128)S(1)}, u32[]{:S(2)}, u32[]{:S(2)}) collective-permute-start(f32[256,128]{1,0:T(8,128)S(1)} %copy-done.25), channel_id=1, source_target_pairs={{0,8},{4,12},{8,0},{12,4},{1,9},{5,13},{9,1},{13,5},{2,10},{6,14},... | collective-permute-start | bytes 393224 | tf_op jit(solution)/shard_map/ppermute | solution.py:416
  91.5 2.4 collective-permute-start.34
  94.5 2.5 collective-permute-done.9
  97.0 2.1 collective-permute-start.35
  100.1 1.6 collective-permute-start.10
  101.7 6.4 %shard_map.90 = (bf16[512,1024]{1,0:T(8,128)(2,1)}, bf16[512,1024]{1,0:T(8,128)(2,1)}, bf16[1024,512]{1,0:T(8,128)(2,1)}, bf16[1024,512]{1,0:T(8,128)(2,1)}) custom-call(s32[5]{0:T(128)} %stack.20.at_ref, f32[32,2,32,512]{3,2,1,0:T(8,128)} %constant_dynamic-update-slice_fusion.7.bank_ref, f32[2,512,512]{2,1,0:T(8,128)} %mix_ref.3), custom_call_target="tpu_custom_call" | custom-call | flops 1610612736 | bytes 6291456 | tf_op jit(solution)/shard_map/pallas_call | solution.py:119
  108.0 2.9 collective-permute-done.22.refs_2_
  111.0 11.2 %collective-permute-start.28 = (f32[256,512]{1,0:T(8,128)S(1)}, f32[256,512]{1,0:T(8,128)}, u32[]{:S(2)}, u32[]{:S(2)}) collective-permute-start(f32[256,512]{1,0:T(8,128)S(1)} %copy-done.2), channel_id=1, source_target_pairs={{0,8},{4,12},{8,0},{12,4},{1,9},{5,13},{9,1},{13,5},{2,10},{6,14},... | collective-permute-start | bytes 1572872 | tf_op jit(solution)/shard_map/ppermute | solution.py:416
  122.1 29.6 %collective-permute-done.10 = f32[256,128]{1,0:T(8,128)} collective-permute-done((f32[256,128]{1,0:T(8,128)S(1)}, f32[256,128]{1,0:T(8,128)}, u32[]{:S(2)}, u32[]{:S(2)}) %collective-permute-start.10) | collective-permute-done | bytes 131104 | tf_op jit(solution)/shard_map/ppermute | solution.py:419
  151.8 0.9 fusion
  152.7 1.1 collective-permute-start.23
  153.8 1.5 collective-permute-start.11
  155.4 6.7 %shard_map.96 = (f32[256,256]{1,0:T(8,128)}, f32[256,256]{1,0:T(8,128)}, f32[256,256]{1,0:T(8,128)}, f32[256,256]{1,0:T(8,128)}) custom-call(bf16[512,1024]{1,0:T(8,128)(2,1)} %get-tuple-element.75.first_high, bf16[512,1024]{1,0:T(8,128)(2,1)} %get-tuple-element.76.first_low, bf16[1024,512]{1,0:T(8,128)(2,1)} %get-tuple-element.77.second_high, ...), custom_call_target="tpu_custom_call" | custom-call | flops 1610612736 | bytes 2097152 | tf_op jit(solution)/shard_map/pallas_call | solution.py:155
  162.0 14.4 %collective-permute-done.23.refs_3_ = f32[256,128]{1,0:T(8,128)S(1)} collective-permute-done((f32[256,128]{1,0:T(8,128)S(1)}, f32[256,128]{1,0:T(8,128)S(1)}, u32[]{:S(2)}, u32[]{:S(2)}) %collective-permute-start.23) | collective-permute-done | bytes 131104 | tf_op jit(solution)/shard_map/ppermute | solution.py:416
  177.0 6.4 %shard_map.93 = (f32[256,128]{1,0:T(8,128)}, f32[256,128]{1,0:T(8,128)}, f32[256,128]{1,0:T(8,128)}, f32[256,128]{1,0:T(8,128)}) custom-call(bf16[512,1024]{1,0:T(8,128)(2,1)} %get-tuple-element.75.first_high, bf16[512,1024]{1,0:T(8,128)(2,1)} %get-tuple-element.76.first_low, bf16[1024,512]{1,0:T(8,128)(2,1)} %get-tuple-element.77.second_high, ...), custom_call_target="tpu_custom_call" | custom-call | flops 805306368 | bytes 1048576 | tf_op jit(solution)/shard_map/pallas_call | solution.py:155
  183.4 1.6 collective-permute-start.14
  185.0 2.2 collective-permute-done.14
  187.3 3.2 %collective-permute-start.17 = (f32[256,128]{1,0:T(8,128)S(1)}, f32[256,128]{1,0:T(8,128)S(1)}, u32[]{:S(2)}, u32[]{:S(2)}) collective-permute-start(f32[256,128]{1,0:T(8,128)S(1)} %copy-done.23), channel_id=1, source_target_pairs={{0,12},{4,0},{8,4},{12,8},{1,13},{5,1},{9,5},{13,9},{2,14},{6,2},{... | collective-permute-start | bytes 393224 | tf_op jit(solution)/shard_map/ppermute | solution.py:416
  190.5 1.2 collective-permute-start.24
  191.7 2.3 collective-permute-start.36
  194.0 10.3 %shard_map.95 = (f32[256,512]{1,0:T(8,128)}, f32[256,512]{1,0:T(8,128)}, f32[256,512]{1,0:T(8,128)}, f32[256,512]{1,0:T(8,128)}) custom-call(bf16[512,1024]{1,0:T(8,128)(2,1)} %get-tuple-element.75.first_high, bf16[512,1024]{1,0:T(8,128)(2,1)} %get-tuple-element.76.first_low, bf16[1024,512]{1,0:T(8,128)(2,1)} %get-tuple-element.77.second_high, ...), custom_call_target="tpu_custom_call" | custom-call | flops 3221225472 | bytes 4194304 | tf_op jit(solution)/shard_map/pallas_call | solution.py:155
  204.3 3.6 %collective-permute-start.30 = (f32[256,512]{1,0:T(8,128)}, f32[256,512]{1,0:T(8,128)S(1)}, u32[]{:S(2)}, u32[]{:S(2)}) collective-permute-start(f32[256,512]{1,0:T(8,128)} %get-tuple-element.96), channel_id=1, source_target_pairs={{0,12},{4,0},{8,4},{12,8},{1,13},{5,1},{9,5},{13,9},{2,14},{6,2},{... | collective-permute-start | bytes 1572872 | tf_op jit(solution)/shard_map/ppermute | solution.py:416
  208.6 2.4 collective-permute-start.37
  211.0 1.5 collective-permute-start.38
  213.1 6.4 %shard_map.91 = (f32[256,128]{1,0:T(8,128)}, f32[256,128]{1,0:T(8,128)}, f32[256,128]{1,0:T(8,128)}, f32[256,128]{1,0:T(8,128)}) custom-call(bf16[512,1024]{1,0:T(8,128)(2,1)} %get-tuple-element.75.first_high, bf16[512,1024]{1,0:T(8,128)(2,1)} %get-tuple-element.76.first_low, bf16[1024,512]{1,0:T(8,128)(2,1)} %get-tuple-element.77.second_high, ...), custom_call_target="tpu_custom_call" | custom-call | flops 805306368 | bytes 1048576 | tf_op jit(solution)/shard_map/pallas_call | solution.py:155
  219.5 2.0 shard_map.89.both_ref.refs_8_
  221.5 50.4 %collective-permute-done.37.refs_6_ = f32[256,256]{1,0:T(8,128)S(1)} collective-permute-done((f32[256,256]{1,0:T(8,128)}, f32[256,256]{1,0:T(8,128)S(1)}, u32[]{:S(2)}, u32[]{:S(2)}) %collective-permute-start.37) | collective-permute-done | bytes 262176 | tf_op jit(solution)/shard_map/ppermute | solution.py:416
  272.0 1.2 collective-permute-start.26
  273.2 5.2 %shard_map.97.refs_10_ = f32[256,4096]{1,0:T(8,128)} custom-call(s32[5]{0:T(128)} %stack.20.at_ref, f32[256,256]{1,0:T(8,128)} %get-tuple-element.66.refs_12_.refs_0_, f32[256,256]{1,0:T(8,128)} %get-tuple-element.54.refs_0_.refs_1_, f32[256,256]{1,0:T(8,128)} %get-tuple-element.55.refs_1_.refs_2_, f32[256,256]{1,0:T(8,128)} %get-tuple-element.56.refs_2_.refs_3_, ...), custom_call_target="tpu_custom_call" | custom-call | flops 536870912 | bytes 3145728 | tf_op jit(solution)/shard_map/pallas_call | solution.py:367
  278.4 2.7 collective-permute-start.18
  281.1 1.2 collective-permute-start.19
  283.1 2.7 shard_map.94
  285.8 6.3 %shard_map.98.refs_7_ = f32[256,4096]{1,0:T(8,128)} custom-call(s32[5]{0:T(128)} %stack.20.at_ref, f32[256,512]{1,0:T(8,128)} %get-tuple-element.67.refs_13_.refs_0_, f32[256,512]{1,0:T(8,128)} %get-tuple-element.57.refs_3_.refs_1_, f32[256,512]{1,0:T(8,128)} %get-tuple-element.58.refs_4_.refs_2_, ...), custom_call_target="tpu_custom_call", output_to_operand_aliasing={{}: (11, {})} | custom-call | flops 1073741824 | bytes 6291456 | tf_op jit(solution)/shard_map/pallas_call | solution.py:367
  292.9 2.1 shard_map.99.refs_7_
  294.9 2.7 shard_map.92
  298.4 2.1 shard_map.100
  (147 shorter events, 14.7 us)
Async XLA Ops:
  1.6 10.6 %collective-permute-start = (f32[1,2,32,512]{3,2,1,0:T(8,128)}, f32[1,2,32,512]{3,2,1,0:T(8,128)S(1)}, u32[]{:S(2)}, u32[]{:S(2)}) collective-permute-start(f32[1,2,32,512]{3,2,1,0:T(8,128)} %shard_map.82), channel_id=1, source_target_pairs={{0,8},{4,12},{8,0},{12,4},{1,9},{5,13},{9,1},{13,5},{2,10},{6,14},... | collective-permute-start | bytes 393224 | tf_op jit(solution)/shard_map/ppermute | solution.py:419
  13.1 30.0 %copy-start.44 = (s32[4]{0:T(128)S(1)}, s32[4]{0:T(128)}, u32[]{:S(2)}) copy-start(s32[4]{0:T(128)} %index_ref.1) | copy-start | bytes 52
  13.1 7.5 %collective-permute-start.1 = (f32[2,2,32,512]{3,2,1,0:T(8,128)S(1)}, f32[2,2,32,512]{3,2,1,0:T(8,128)S(1)}, u32[]{:S(2)}, u32[]{:S(2)}) collective-permute-start(f32[2,2,32,512]{3,2,1,0:T(8,128)S(1)} %pad_maximum_fusion.1), channel_id=1, source_target_pairs={{0,4},{4,0},{8,12},{12,8},{1,5},{5,1},{9,13},{13,9},{2,6},{6,2},{1... | collective-permute-start | bytes 786440 | tf_op jit(solution)/shard_map/ppermute | solution.py:419
  21.6 12.3 %collective-permute-start.2 = (f32[4,2,32,512]{3,2,1,0:T(8,128)S(1)}, f32[4,2,32,512]{3,2,1,0:T(8,128)S(1)}, u32[]{:S(2)}, u32[]{:S(2)}) collective-permute-start(f32[4,2,32,512]{3,2,1,0:T(8,128)S(1)} %pad_maximum_fusion), channel_id=1, source_target_pairs={{0,2},{1,3},{2,0},{3,1},{4,6},{5,7},{6,4},{7,5},{8,10},{9,11},{10,... | collective-permute-start | bytes 1572872 | tf_op jit(solution)/shard_map/ppermute | solution.py:419
  23.0 12.8 %collective-permute-start.3 = (f32[4,2,32,512]{3,2,1,0:T(8,128)S(1)}, f32[4,2,32,512]{3,2,1,0:T(8,128)S(1)}, u32[]{:S(2)}, u32[]{:S(2)}) collective-permute-start(f32[4,2,32,512]{3,2,1,0:T(8,128)S(1)} %pad_maximum_fusion), channel_id=1, source_target_pairs={{0,16},{16,0},{1,17},{17,1},{2,18},{18,2},{3,19},{19,3},{4,20},{20... | collective-permute-start | bytes 1572872 | tf_op jit(solution)/shard_map/ppermute | solution.py:419
  33.9 6.7 %collective-permute-start.4 = (f32[2,2,32,512]{3,2,1,0:T(8,128)S(1)}, f32[2,2,32,512]{3,2,1,0:T(8,128)S(1)}, u32[]{:S(2)}, u32[]{:S(2)}) collective-permute-start(f32[2,2,32,512]{3,2,1,0:T(8,128)S(1)} %slice.24), channel_id=1, source_target_pairs={{0,16},{16,0},{1,17},{17,1},{2,18},{18,2},{3,19},{19,3},{4,20},{20... | collective-permute-start | bytes 786440 | tf_op jit(solution)/shard_map/ppermute | solution.py:419
  35.8 6.4 %collective-permute-start.5 = (f32[2,2,32,512]{3,2,1,0:T(8,128)S(1)}, f32[2,2,32,512]{3,2,1,0:T(8,128)S(1)}, u32[]{:S(2)}, u32[]{:S(2)}) collective-permute-start(f32[2,2,32,512]{3,2,1,0:T(8,128)S(1)} %slice.25), channel_id=1, source_target_pairs={{0,2},{1,3},{2,0},{3,1},{4,6},{5,7},{6,4},{7,5},{8,10},{9,11},{10,... | collective-permute-start | bytes 786440 | tf_op jit(solution)/shard_map/ppermute | solution.py:419
  43.1 31.1 %collective-permute-start.6 = (f32[16,2,32,512]{3,2,1,0:T(8,128)}, f32[16,2,32,512]{3,2,1,0:T(8,128)S(1)}, u32[]{:S(2)}, u32[]{:S(2)}) collective-permute-start(f32[16,2,32,512]{3,2,1,0:T(8,128)} %get-tuple-element.107), channel_id=1, source_target_pairs={{0,1},{1,0},{2,3},{3,2},{4,5},{5,4},{6,7},{7,6},{8,9},{9,8},{10,11... | collective-permute-start | bytes 6291464 | tf_op jit(solution)/shard_map/ppermute | solution.py:419
  61.4 2.3 collective-permute-start.7
  64.8 8.7 %collective-permute-start.8 = (f32[256,256]{1,0:T(8,128)S(1)}, f32[256,256]{1,0:T(8,128)S(1)}, u32[]{:S(2)}, u32[]{:S(2)}) collective-permute-start(f32[256,256]{1,0:T(8,128)S(1)} %slice.27), channel_id=1, source_target_pairs={{0,2},{1,3},{2,0},{3,1},{4,6},{5,7},{6,4},{7,5},{8,10},{9,11},{10,... | collective-permute-start | bytes 786440 | tf_op jit(solution)/shard_map/ppermute | solution.py:419
  75.8 21.3 %copy-start.10 = (f32[256,256]{1,0:T(8,128)S(1)}, f32[256,256]{1,0:T(8,128)}, u32[]{:S(2)}) copy-start(f32[256,256]{1,0:T(8,128)} %get-tuple-element.56.refs_2_.refs_3_) | copy-start | bytes 786436
  83.9 27.0 %copy-start.1 = (f32[256,512]{1,0:T(8,128)S(1)}, f32[256,512]{1,0:T(8,128)}, u32[]{:S(2)}) copy-start(f32[256,512]{1,0:T(8,128)} %get-tuple-element.57.refs_3_.refs_1_) | copy-start | bytes 1572868
  83.9 27.1 %copy-start.2 = (f32[256,512]{1,0:T(8,128)S(1)}, f32[256,512]{1,0:T(8,128)}, u32[]{:S(2)}) copy-start(f32[256,512]{1,0:T(8,128)} %get-tuple-element.58.refs_4_.refs_2_) | copy-start | bytes 1572868
  83.9 67.8 %copy-start.3 = (f32[256,512]{1,0:T(8,128)S(1)}, f32[256,512]{1,0:T(8,128)}, u32[]{:S(2)}) copy-start(f32[256,512]{1,0:T(8,128)} %get-tuple-element.59.refs_5_.refs_3_) | copy-start | bytes 1572868
  83.9 68.8 %copy-start.26 = (f32[256,128]{1,0:T(8,128)S(1)}, f32[256,128]{1,0:T(8,128)}, u32[]{:S(2)}) copy-start(f32[256,128]{1,0:T(8,128)} %get-tuple-element.62.refs_8_.refs_3_) | copy-start | bytes 393220
  83.9 13.1 %collective-permute-start.9 = (f32[512,128]{1,0:T(8,128)}, f32[512,128]{1,0:T(8,128)S(1)}, u32[]{:S(2)}, u32[]{:S(2)}) collective-permute-start(f32[512,128]{1,0:T(8,128)} %get-tuple-element.73), channel_id=1, source_target_pairs={{0,4},{4,0},{8,12},{12,8},{1,5},{5,1},{9,13},{13,9},{2,6},{6,2},{1... | collective-permute-start | bytes 786440 | tf_op jit(solution)/shard_map/ppermute | solution.py:419
  86.9 4.5 %collective-permute-start.13 = (f32[8,512]{1,0:T(8,128)S(1)}, f32[8,512]{1,0:T(8,128)S(1)}, u32[]{:S(2)}, u32[]{:S(2)}) collective-permute-start(f32[8,512]{1,0:T(8,128)S(1)} %broadcast_in_dim.20), channel_id=1, source_target_pairs={{0,1},{1,0},{2,3},{3,2},{4,5},{5,4},{6,7},{7,6},{8,9},{9,8},{10,11... | collective-permute-start | bytes 49160 | tf_op jit(solution)/shard_map/ppermute | solution.py:419
  87.0 13.0 %collective-permute-start.21 = (f32[256,128]{1,0:T(8,128)S(1)}, f32[256,128]{1,0:T(8,128)S(1)}, u32[]{:S(2)}, u32[]{:S(2)}) collective-permute-start(f32[256,128]{1,0:T(8,128)S(1)} %copy-done.24), channel_id=1, source_target_pairs={{0,4},{4,8},{8,12},{12,0},{1,5},{5,9},{9,13},{13,1},{2,6},{6,10},{... | collective-permute-start | bytes 393224 | tf_op jit(solution)/shard_map/ppermute | solution.py:416
  87.1 23.8 %collective-permute-start.22 = (f32[256,128]{1,0:T(8,128)S(1)}, f32[256,128]{1,0:T(8,128)S(1)}, u32[]{:S(2)}, u32[]{:S(2)}) collective-permute-start(f32[256,128]{1,0:T(8,128)S(1)} %copy-done.25), channel_id=1, source_target_pairs={{0,8},{4,12},{8,0},{12,4},{1,9},{5,13},{9,1},{13,5},{2,10},{6,14},... | collective-permute-start | bytes 393224 | tf_op jit(solution)/shard_map/ppermute | solution.py:416
  91.1 19.9 %collective-permute-start.33 = (f32[256,256]{1,0:T(8,128)S(1)}, f32[256,256]{1,0:T(8,128)}, u32[]{:S(2)}, u32[]{:S(2)}) collective-permute-start(f32[256,256]{1,0:T(8,128)S(1)} %copy-done.8), channel_id=1, source_target_pairs={{0,4},{4,8},{8,12},{12,0},{1,5},{5,9},{9,13},{13,1},{2,6},{6,10},{... | collective-permute-start | bytes 786440 | tf_op jit(solution)/shard_map/ppermute | solution.py:416
  91.5 62.4 %copy-start.34 = (f32[8,512]{1,0:T(8,128)}, f32[8,512]{1,0:T(8,128)S(1)}, u32[]{:S(2)}) copy-start(f32[8,512]{1,0:T(8,128)S(1)} %collective-permute-done.13) | copy-start | bytes 49156
  91.5 61.2 %collective-permute-start.34 = (f32[256,256]{1,0:T(8,128)S(1)}, f32[256,256]{1,0:T(8,128)}, u32[]{:S(2)}, u32[]{:S(2)}) collective-permute-start(f32[256,256]{1,0:T(8,128)S(1)} %copy-done.9), channel_id=1, source_target_pairs={{0,8},{4,12},{8,0},{12,4},{1,9},{5,13},{9,1},{13,5},{2,10},{6,14},... | collective-permute-start | bytes 786440 | tf_op jit(solution)/shard_map/ppermute | solution.py:416
  97.0 56.8 %collective-permute-start.35 = (f32[256,256]{1,0:T(8,128)S(1)}, f32[256,256]{1,0:T(8,128)}, u32[]{:S(2)}, u32[]{:S(2)}) collective-permute-start(f32[256,256]{1,0:T(8,128)S(1)} %copy-done.10), channel_id=1, source_target_pairs={{0,12},{4,0},{8,4},{12,8},{1,13},{5,1},{9,5},{13,9},{2,14},{6,2},{... | collective-permute-start | bytes 786440 | tf_op jit(solution)/shard_map/ppermute | solution.py:416
  100.0 51.7 %copy-start.28 = (f32[256,128]{1,0:T(8,128)}, f32[256,128]{1,0:T(8,128)S(1)}, u32[]{:S(2)}) copy-start(f32[256,128]{1,0:T(8,128)S(1)} %collective-permute-done.21.refs_1_) | copy-start | bytes 393220
  100.1 51.7 %copy-start.33 = (f32[256,128]{1,0:T(8,128)S(1)}, f32[256,128]{1,0:T(8,128)}, u32[]{:S(2)}) copy-start(f32[256,128]{1,0:T(8,128)} %get-tuple-element.72) | copy-start | bytes 393220
  100.1 51.7 %collective-permute-start.10 = (f32[256,128]{1,0:T(8,128)S(1)}, f32[256,128]{1,0:T(8,128)}, u32[]{:S(2)}, u32[]{:S(2)}) collective-permute-start(f32[256,128]{1,0:T(8,128)S(1)} %slice_add_fusion.1), channel_id=1, source_target_pairs={{0,8},{4,12},{8,0},{12,4},{1,9},{5,13},{9,1},{13,5},{2,10},{6,14},... | collective-permute-start | bytes 393224 | tf_op jit(solution)/shard_map/ppermute | solution.py:419
  108.0 68.4 %copy-start.21 = (f32[256,128]{1,0:T(8,128)S(1)}, f32[256,128]{1,0:T(8,128)}, u32[]{:S(2)}) copy-start(f32[256,128]{1,0:T(8,128)} %get-tuple-element.63.refs_9_.refs_1_) | copy-start | bytes 393220
  110.9 44.4 %copy-start.29 = (f32[256,128]{1,0:T(8,128)}, f32[256,128]{1,0:T(8,128)S(1)}, u32[]{:S(2)}) copy-start(f32[256,128]{1,0:T(8,128)S(1)} %collective-permute-done.22.refs_2_) | copy-start | bytes 393220
  110.9 79.6 %collective-permute-start.27 = (f32[256,512]{1,0:T(8,128)S(1)}, f32[256,512]{1,0:T(8,128)}, u32[]{:S(2)}, u32[]{:S(2)}) collective-permute-start(f32[256,512]{1,0:T(8,128)S(1)} %copy-done.1), channel_id=1, source_target_pairs={{0,4},{4,8},{8,12},{12,0},{1,5},{5,9},{9,13},{13,1},{2,6},{6,10},{... | collective-permute-start | bytes 1572872 | tf_op jit(solution)/shard_map/ppermute | solution.py:416
  111.0 80.7 %collective-permute-start.28 = (f32[256,512]{1,0:T(8,128)S(1)}, f32[256,512]{1,0:T(8,128)}, u32[]{:S(2)}, u32[]{:S(2)}) collective-permute-start(f32[256,512]{1,0:T(8,128)S(1)} %copy-done.2), channel_id=1, source_target_pairs={{0,8},{4,12},{8,0},{12,4},{1,9},{5,13},{9,1},{13,5},{2,10},{6,14},... | collective-permute-start | bytes 1572872 | tf_op jit(solution)/shard_map/ppermute | solution.py:416
  151.7 42.2 %collective-permute-start.29 = (f32[256,512]{1,0:T(8,128)S(1)}, f32[256,512]{1,0:T(8,128)}, u32[]{:S(2)}, u32[]{:S(2)}) collective-permute-start(f32[256,512]{1,0:T(8,128)S(1)} %copy-done.3), channel_id=1, source_target_pairs={{0,12},{4,0},{8,4},{12,8},{1,13},{5,1},{9,5},{13,9},{2,14},{6,2},{... | collective-permute-start | bytes 1572872 | tf_op jit(solution)/shard_map/ppermute | solution.py:416
  152.7 23.7 %collective-permute-start.23 = (f32[256,128]{1,0:T(8,128)S(1)}, f32[256,128]{1,0:T(8,128)S(1)}, u32[]{:S(2)}, u32[]{:S(2)}) collective-permute-start(f32[256,128]{1,0:T(8,128)S(1)} %copy-done.26), channel_id=1, source_target_pairs={{0,12},{4,0},{8,4},{12,8},{1,13},{5,1},{9,5},{13,9},{2,14},{6,2},{... | collective-permute-start | bytes 393224 | tf_op jit(solution)/shard_map/ppermute | solution.py:416
  153.8 29.6 %collective-permute-start.11 = (f32[256,128]{1,0:T(8,128)S(1)}, f32[256,128]{1,0:T(8,128)S(1)}, u32[]{:S(2)}, u32[]{:S(2)}) collective-permute-start(f32[256,128]{1,0:T(8,128)S(1)} %fusion), channel_id=1, source_target_pairs={{0,2},{1,3},{2,0},{3,1},{4,6},{5,7},{6,4},{7,5},{8,10},{9,11},{10,... | collective-permute-start | bytes 393224 | tf_op jit(solution)/shard_map/ppermute | solution.py:419
  155.3 28.1 %copy-start.38 = (f32[8,512]{1,0:T(8,128)S(1)}, f32[8,512]{1,0:T(8,128)}, u32[]{:S(2)}) copy-start(f32[8,512]{1,0:T(8,128)} %broadcast_add_fusion) | copy-start | bytes 49156
  155.3 31.9 %copy-start.22 = (f32[256,128]{1,0:T(8,128)S(1)}, f32[256,128]{1,0:T(8,128)}, u32[]{:S(2)}) copy-start(f32[256,128]{1,0:T(8,128)} %get-tuple-element.64.refs_10_.refs_2_) | copy-start | bytes 393220
  155.3 31.9 %copy-start.23 = (f32[256,128]{1,0:T(8,128)S(1)}, f32[256,128]{1,0:T(8,128)}, u32[]{:S(2)}) copy-start(f32[256,128]{1,0:T(8,128)} %get-tuple-element.65.refs_11_.refs_3_) | copy-start | bytes 393220
  176.4 10.9 %collective-permute-start.15 = (f32[256,128]{1,0:T(8,128)S(1)}, f32[256,128]{1,0:T(8,128)S(1)}, u32[]{:S(2)}, u32[]{:S(2)}) collective-permute-start(f32[256,128]{1,0:T(8,128)S(1)} %copy-done.21), channel_id=1, source_target_pairs={{0,4},{4,8},{8,12},{12,0},{1,5},{5,9},{9,13},{13,1},{2,6},{6,10},{... | collective-permute-start | bytes 393224 | tf_op jit(solution)/shard_map/ppermute | solution.py:416
  183.4 3.8 %collective-permute-start.14 = (f32[8,512]{1,0:T(8,128)S(1)}, f32[8,512]{1,0:T(8,128)S(1)}, u32[]{:S(2)}, u32[]{:S(2)}) collective-permute-start(f32[8,512]{1,0:T(8,128)S(1)} %copy-done.38), channel_id=1, source_target_pairs={{0,2},{1,3},{2,0},{3,1},{4,6},{5,7},{6,4},{7,5},{8,10},{9,11},{10,... | collective-permute-start | bytes 49160 | tf_op jit(solution)/shard_map/ppermute | solution.py:419
  185.0 19.3 %copy-start = (f32[256,256]{1,0:T(8,128)}, f32[256,256]{1,0:T(8,128)S(1)}, u32[]{:S(2)}) copy-start(f32[256,256]{1,0:T(8,128)S(1)} %pad_maximum_fusion.2.here_ref) | copy-start | bytes 786436
  187.2 17.1 %collective-permute-start.16 = (f32[256,128]{1,0:T(8,128)S(1)}, f32[256,128]{1,0:T(8,128)S(1)}, u32[]{:S(2)}, u32[]{:S(2)}) collective-permute-start(f32[256,128]{1,0:T(8,128)S(1)} %copy-done.22), channel_id=1, source_target_pairs={{0,8},{4,12},{8,0},{12,4},{1,9},{5,13},{9,1},{13,5},{2,10},{6,14},... | collective-permute-start | bytes 393224 | tf_op jit(solution)/shard_map/ppermute | solution.py:416
  187.3 17.0 %copy-start.27 = (f32[256,128]{1,0:T(8,128)}, f32[256,128]{1,0:T(8,128)S(1)}, u32[]{:S(2)}) copy-start(f32[256,128]{1,0:T(8,128)S(1)} %collective-permute-done.15.refs_1_) | copy-start | bytes 393220
  187.3 20.7 %collective-permute-start.17 = (f32[256,128]{1,0:T(8,128)S(1)}, f32[256,128]{1,0:T(8,128)S(1)}, u32[]{:S(2)}, u32[]{:S(2)}) collective-permute-start(f32[256,128]{1,0:T(8,128)S(1)} %copy-done.23), channel_id=1, source_target_pairs={{0,12},{4,0},{8,4},{12,8},{1,13},{5,1},{9,5},{13,9},{2,14},{6,2},{... | collective-permute-start | bytes 393224 | tf_op jit(solution)/shard_map/ppermute | solution.py:416
  190.5 17.5 %collective-permute-start.24 = (f32[256,128]{1,0:T(8,128)}, f32[256,128]{1,0:T(8,128)S(1)}, u32[]{:S(2)}, u32[]{:S(2)}) collective-permute-start(f32[256,128]{1,0:T(8,128)} %get-tuple-element.92), channel_id=1, source_target_pairs={{0,12},{4,0},{8,4},{12,8},{1,13},{5,1},{9,5},{13,9},{2,14},{6,2},{... | collective-permute-start | bytes 393224 | tf_op jit(solution)/shard_map/ppermute | solution.py:416
  191.7 20.8 %copy-start.35 = (f32[8,512]{1,0:T(8,128)S(1)}, f32[8,512]{1,0:T(8,128)}, u32[]{:S(2)}) copy-start(f32[8,512]{1,0:T(8,128)} %copy-done.34) | copy-start | bytes 49156
  191.7 20.8 %copy-start.37 = (f32[512]{0:T(512)S(1)}, f32[512]{0:T(512)}, u32[]{:S(2)}) copy-start(f32[512]{0:T(512)} %copy-done.36) | copy-start | bytes 6148
  191.7 16.9 %collective-permute-start.36 = (f32[256,256]{1,0:T(8,128)}, f32[256,256]{1,0:T(8,128)S(1)}, u32[]{:S(2)}, u32[]{:S(2)}) collective-permute-start(f32[256,256]{1,0:T(8,128)} %get-tuple-element.100), channel_id=1, source_target_pairs={{0,12},{4,0},{8,4},{12,8},{1,13},{5,1},{9,5},{13,9},{2,14},{6,2},{... | collective-permute-start | bytes 786440 | tf_op jit(solution)/shard_map/ppermute | solution.py:416
  194.0 17.0 %collective-permute-start.12 = (f32[256,256]{1,0:T(8,128)S(1)}, f32[256,256]{1,0:T(8,128)S(1)}, u32[]{:S(2)}, u32[]{:S(2)}) collective-permute-start(f32[256,256]{1,0:T(8,128)S(1)} %pad_maximum_fusion.2.here_ref), channel_id=1, source_target_pairs={{0,1},{1,0},{2,3},{3,2},{4,5},{5,4},{6,7},{7,6},{8,9},{9,8},{10,11... | collective-permute-start | bytes 786440 | tf_op jit(solution)/shard_map/ppermute | solution.py:419
  204.3 67.6 %copy-start.40 = (f32[256,128]{1,0:T(8,128)S(1)}, f32[256,128]{1,0:T(8,128)}, u32[]{:S(2)}) copy-start(f32[256,128]{1,0:T(8,128)} %get-tuple-element.93) | copy-start | bytes 393220
  204.3 67.6 %copy-start.39 = (f32[256,128]{1,0:T(8,128)S(1)}, f32[256,128]{1,0:T(8,128)}, u32[]{:S(2)}) copy-start(f32[256,128]{1,0:T(8,128)} %get-tuple-element.94) | copy-start | bytes 393220
  204.3 74.0 %collective-permute-start.30 = (f32[256,512]{1,0:T(8,128)}, f32[256,512]{1,0:T(8,128)S(1)}, u32[]{:S(2)}, u32[]{:S(2)}) collective-permute-start(f32[256,512]{1,0:T(8,128)} %get-tuple-element.96), channel_id=1, source_target_pairs={{0,12},{4,0},{8,4},{12,8},{1,13},{5,1},{9,5},{13,9},{2,14},{6,2},{... | collective-permute-start | bytes 1572872 | tf_op jit(solution)/shard_map/ppermute | solution.py:416
  208.0 73.1 %collective-permute-start.31 = (f32[256,512]{1,0:T(8,128)}, f32[256,512]{1,0:T(8,128)S(1)}, u32[]{:S(2)}, u32[]{:S(2)}) collective-permute-start(f32[256,512]{1,0:T(8,128)} %get-tuple-element.97), channel_id=1, source_target_pairs={{0,8},{4,12},{8,0},{12,4},{1,9},{5,13},{9,1},{13,5},{2,10},{6,14},... | collective-permute-start | bytes 1572872 | tf_op jit(solution)/shard_map/ppermute | solution.py:416
  208.0 70.3 %copy-start.15 = (f32[256,128]{1,0:T(8,128)}, f32[256,128]{1,0:T(8,128)S(1)}, u32[]{:S(2)}) copy-start(f32[256,128]{1,0:T(8,128)S(1)} %collective-permute-done.24.refs_4_) | copy-start | bytes 393220
  208.0 74.3 %collective-permute-start.32 = (f32[256,512]{1,0:T(8,128)}, f32[256,512]{1,0:T(8,128)S(1)}, u32[]{:S(2)}, u32[]{:S(2)}) collective-permute-start(f32[256,512]{1,0:T(8,128)} %get-tuple-element.98), channel_id=1, source_target_pairs={{0,4},{4,8},{8,12},{12,0},{1,5},{5,9},{9,13},{13,1},{2,6},{6,10},{... | collective-permute-start | bytes 1572872 | tf_op jit(solution)/shard_map/ppermute | solution.py:416
  208.6 64.5 %copy-start.11 = (f32[256,256]{1,0:T(8,128)}, f32[256,256]{1,0:T(8,128)S(1)}, u32[]{:S(2)}) copy-start(f32[256,256]{1,0:T(8,128)S(1)} %collective-permute-done.36.refs_5_) | copy-start | bytes 786436
  208.6 63.3 %collective-permute-start.37 = (f32[256,256]{1,0:T(8,128)}, f32[256,256]{1,0:T(8,128)S(1)}, u32[]{:S(2)}, u32[]{:S(2)}) collective-permute-start(f32[256,256]{1,0:T(8,128)} %get-tuple-element.101), channel_id=1, source_target_pairs={{0,8},{4,12},{8,0},{12,4},{1,9},{5,13},{9,1},{13,5},{2,10},{6,14},... | collective-permute-start | bytes 786440 | tf_op jit(solution)/shard_map/ppermute | solution.py:416
  211.0 60.9 %collective-permute-start.38 = (f32[256,256]{1,0:T(8,128)}, f32[256,256]{1,0:T(8,128)S(1)}, u32[]{:S(2)}, u32[]{:S(2)}) collective-permute-start(f32[256,256]{1,0:T(8,128)} %get-tuple-element.102), channel_id=1, source_target_pairs={{0,4},{4,8},{8,12},{12,0},{1,5},{5,9},{9,13},{13,1},{2,6},{6,10},{... | collective-permute-start | bytes 786440 | tf_op jit(solution)/shard_map/ppermute | solution.py:416
  219.5 58.9 %copy-start.43 = (f32[256,128]{1,0:T(8,128)S(1)}, f32[256,128]{1,0:T(8,128)}, u32[]{:S(2)}) copy-start(f32[256,128]{1,0:T(8,128)} %get-tuple-element.84) | copy-start | bytes 393220
  219.5 61.6 %copy-start.42 = (f32[256,128]{1,0:T(8,128)S(1)}, f32[256,128]{1,0:T(8,128)}, u32[]{:S(2)}) copy-start(f32[256,128]{1,0:T(8,128)} %get-tuple-element.85) | copy-start | bytes 393220
  219.5 62.9 %copy-start.41 = (f32[256,128]{1,0:T(8,128)S(1)}, f32[256,128]{1,0:T(8,128)}, u32[]{:S(2)}) copy-start(f32[256,128]{1,0:T(8,128)} %get-tuple-element.86) | copy-start | bytes 393220
  271.9 20.2 %collective-permute-start.25 = (f32[256,128]{1,0:T(8,128)S(1)}, f32[256,128]{1,0:T(8,128)S(1)}, u32[]{:S(2)}, u32[]{:S(2)}) collective-permute-start(f32[256,128]{1,0:T(8,128)S(1)} %copy-done.40), channel_id=1, source_target_pairs={{0,8},{4,12},{8,0},{12,4},{1,9},{5,13},{9,1},{13,5},{2,10},{6,14},... | collective-permute-start | bytes 393224 | tf_op jit(solution)/shard_map/ppermute | solution.py:416
  272.0 20.2 %collective-permute-start.26 = (f32[256,128]{1,0:T(8,128)S(1)}, f32[256,128]{1,0:T(8,128)S(1)}, u32[]{:S(2)}, u32[]{:S(2)}) collective-permute-start(f32[256,128]{1,0:T(8,128)S(1)} %copy-done.39), channel_id=1, source_target_pairs={{0,4},{4,8},{8,12},{12,0},{1,5},{5,9},{9,13},{13,1},{2,6},{6,10},{... | collective-permute-start | bytes 393224 | tf_op jit(solution)/shard_map/ppermute | solution.py:416
  278.4 19.3 %collective-permute-start.18 = (f32[256,128]{1,0:T(8,128)S(1)}, f32[256,128]{1,0:T(8,128)S(1)}, u32[]{:S(2)}, u32[]{:S(2)}) collective-permute-start(f32[256,128]{1,0:T(8,128)S(1)} %copy-done.43), channel_id=1, source_target_pairs={{0,12},{4,0},{8,4},{12,8},{1,13},{5,1},{9,5},{13,9},{2,14},{6,2},{... | collective-permute-start | bytes 393224 | tf_op jit(solution)/shard_map/ppermute | solution.py:416
  281.1 16.6 %collective-permute-start.19 = (f32[256,128]{1,0:T(8,128)S(1)}, f32[256,128]{1,0:T(8,128)S(1)}, u32[]{:S(2)}, u32[]{:S(2)}) collective-permute-start(f32[256,128]{1,0:T(8,128)S(1)} %copy-done.42), channel_id=1, source_target_pairs={{0,8},{4,12},{8,0},{12,4},{1,9},{5,13},{9,1},{13,5},{2,10},{6,14},... | collective-permute-start | bytes 393224 | tf_op jit(solution)/shard_map/ppermute | solution.py:416
  282.3 15.4 %collective-permute-start.20 = (f32[256,128]{1,0:T(8,128)S(1)}, f32[256,128]{1,0:T(8,128)S(1)}, u32[]{:S(2)}, u32[]{:S(2)}) collective-permute-start(f32[256,128]{1,0:T(8,128)S(1)} %copy-done.41), channel_id=1, source_target_pairs={{0,4},{4,8},{8,12},{12,0},{1,5},{5,9},{9,13},{13,1},{2,6},{6,10},{... | collective-permute-start | bytes 393224 | tf_op jit(solution)/shard_map/ppermute | solution.py:416
  (20 other events, 123.1 us)

commit v4 on v3

--- a/solution.py
+++ b/solution.py
@@ -10,6 +10,7 @@
 NBIN = 512
 PIECES = ((0, 256), (512, 512), (256, 128), (384, 128))
 LATE = 2
+GRANT = pltpu.CompilerParams(vmem_limit_bytes=32 * 1024 * 1024)
 
 
 def gathered_sums(tod, gain_knots, intervals, fraction, azimuth, mode_index, mode_bank, mode_mix):
@@ -67,20 +68,21 @@
         refs[3 * count + n][...] = tod_ref[...] * dot(gains, spreads, ((0,), (0,)))
 
 
-def calibrate(ring, me, tod, gains, where, share, pieces):
+def calibrate(me, tod, gains, where, share, pieces, grant, place):
     rows = tod.shape[0]
     specs, operands = [], []
     for shift, start, width in pieces:
         per_block, offset = BLOCK // width, start // width
 
         def at(i, me_ref, shift=shift, per_block=per_block, offset=offset):
-            return 0, lax.rem(me_ref[0] + shift, ring) * per_block + offset
+            return 0, jnp.bitwise_xor(me_ref[0], shift) * per_block + offset
 
         specs += [pl.BlockSpec((rows, width), at)] + [pl.BlockSpec((1, width), at)] * 2
         operands += [tod, where, share]
     return pl.pallas_call(
         functools.partial(calibrate_kernel, len(pieces)),
-        out_shape=[jax.ShapeDtypeStruct((rows, width), jnp.float32) for _, _, width in pieces],
+        compiler_params=grant,
+        out_shape=[place((rows, width), jnp.float32) for _, _, width in pieces],
         grid_spec=pltpu.PrefetchScalarGridSpec(
             num_scalar_prefetch=1,
             grid=(1,),
@@ -97,8 +99,8 @@
 
 def modes_kernel(ring, shares, at_ref, bank_ref, mix_ref, first_high, first_low, second_high, second_low, modes):
     rows = bank_ref.shape[2]
-    me, part = at_ref[0], at_ref[2]
-    other = jnp.bitwise_xor(me, lax.rem(me - pl.program_id(0) + ring, ring))
+    part = at_ref[2]
+    other = pl.program_id(0)
     z_slot = (other // 2) + 2 * lax.rem(other, 2)
     for share in range(shares):
         flip = jnp.bitwise_xor(part, share)
@@ -118,6 +120,7 @@
     total = ring * det_rows
     return pl.pallas_call(
         functools.partial(modes_kernel, ring, shares),
+        compiler_params=GRANT,
         out_shape=[jax.ShapeDtypeStruct((m, total), jnp.bfloat16)] * 2
         + [jax.ShapeDtypeStruct((total, m), jnp.bfloat16)] * 2,
         grid_spec=pltpu.PrefetchScalarGridSpec(
@@ -154,6 +157,7 @@
     column = pl.BlockSpec((rows, tile), lambda i: (0, i))
     return pl.pallas_call(
         functools.partial(filter_kernel, ring),
+        compiler_params=GRANT,
         out_shape=[jax.ShapeDtypeStruct((rows, width), jnp.float32)] * ring,
         grid=(width // tile,),
         in_specs=whole + [column] * ring,
@@ -172,7 +176,7 @@
     count, rows, m = mode_bank.shape
     return pl.pallas_call(
         share_kernel,
-        out_shape=jax.ShapeDtypeStruct((1, count, rows // shares, m), jnp.float32),
+        out_shape=pltpu.VMEM((1, count, rows // shares, m), jnp.float32),
         grid_spec=pltpu.PrefetchScalarGridSpec(
             num_scalar_prefetch=1,
             grid=(1,),
@@ -188,7 +192,7 @@
     copies = []
     for s in range(ring):
         held[s] = data[s][...] - back[s - 1][...] if s else data[s][...]
-        column = pl.ds(block_start(ring, at_ref[0], s, start), held.shape[2])
+        column = pl.ds(block_start(at_ref[0], s, start), held.shape[2])
         copies.append(pltpu.make_async_copy(held.at[s], out_ref.at[:, column], done.at[s]))
         copies[s].start()
     for copy in copies:
@@ -206,7 +210,7 @@
         out_specs=pl.BlockSpec(memory_space=pl.ANY),
         scratch_shapes=[pltpu.VMEM((ring, rows, width), jnp.float32), pltpu.SemaphoreType.DMA((ring,))],
         input_output_aliases={2 * ring: 0},
-        compiler_params=pltpu.CompilerParams(vmem_limit_bytes=65_000_000),
+        compiler_params=GRANT,
         cost_estimate=pl.CostEstimate(
             flops=ring * rows * width, bytes_accessed=12 * ring * rows * width, transcendentals=0
         ),
@@ -218,20 +222,20 @@
     return (row == azimuth).astype(jnp.float32).astype(jnp.bfloat16)
 
 
-def block_start(ring, me, shift, start):
-    return pl.multiple_of(lax.rem(me + shift, ring) * BLOCK + start, 128)
-
-
-def bin_kernel(ring, pieces, at_ref, index_ref, azimuth_ref, *refs):
+def block_start(me, shift, start):
+    return pl.multiple_of(jnp.bitwise_xor(me, shift) * BLOCK + start, 128)
+
+
+def bin_kernel(pieces, at_ref, index_ref, azimuth_ref, *refs):
     data, (keep_ref, send_ref, sums) = refs[: len(pieces)], refs[len(pieces) :]
     me, tm = at_ref[0], at_ref[4]
     rows = keep_ref.shape[0]
     sums[...] = jnp.zeros_like(sums)
     for (shift, start, width), ref in zip(pieces, data):
         both = jnp.concatenate(halves(ref[...]), axis=0)
-        onehot = onehot_of(azimuth_ref[:, pl.ds(block_start(ring, me, shift, start), width)], sums.shape[2])
+        onehot = onehot_of(azimuth_ref[:, pl.ds(block_start(me, shift, start), width)], sums.shape[2])
         part = dot(both, onehot, ((1,), (1,)))
-        sums[index_ref[lax.rem(me + shift, ring)]] += part[:rows] + part[rows:]
+        sums[index_ref[jnp.bitwise_xor(me, shift)]] += part[:rows] + part[rows:]
     share = sums.shape[2] // 4
     for x in range(2):
         for bank in range(2):
@@ -241,11 +245,12 @@
                 ref[:, column] = sums[bank, :, pl.ds(first, share)]
 
 
-def bin_data(ring, at, mode_index, azimuth, pieces, data):
+def bin_data(at, mode_index, azimuth, pieces, data):
     rows = data[0].shape[0]
     work = sum(width for _, _, width in pieces)
     return pl.pallas_call(
-        functools.partial(bin_kernel, ring, pieces),
+        functools.partial(bin_kernel, pieces),
+        compiler_params=GRANT,
         out_shape=[jax.ShapeDtypeStruct((rows, NBIN), jnp.float32)] * 2,
         in_specs=[pl.BlockSpec(memory_space=pltpu.SMEM)] * 2 + [pl.BlockSpec(memory_space=pltpu.VMEM)] * (1 + len(data)),
         out_specs=[pl.BlockSpec(memory_space=pltpu.VMEM)] * 2,
@@ -295,6 +300,7 @@
     shapes = [(det_rows, share), (det_rows, share), (2 * det_rows, share)]
     return pl.pallas_call(
         functools.partial(pool_kernel, ring, shares),
+        compiler_params=GRANT,
         out_shape=[jax.ShapeDtypeStruct(shape, jnp.float32) for shape in shapes],
         grid_spec=pltpu.PrefetchScalarGridSpec(
             num_scalar_prefetch=1,
@@ -330,6 +336,7 @@
 def stack_template(at, here, there, counts):
     return pl.pallas_call(
         stack_kernel,
+        compiler_params=GRANT,
         out_shape=jax.ShapeDtypeStruct((2 * here.shape[0], NBIN), jnp.bfloat16),
         in_specs=[pl.BlockSpec(memory_space=pltpu.SMEM)] + [pl.BlockSpec(memory_space=pltpu.VMEM)] * 3,
         out_specs=pl.BlockSpec(memory_space=pltpu.VMEM),
@@ -356,7 +363,7 @@
     per_block, offset = BLOCK // width, start // width
 
     def where(s, at_ref):
-        return 0, lax.rem(at_ref[0] + s, ring) * per_block + offset
+        return 0, jnp.bitwise_xor(at_ref[0], s) * per_block + offset
 
     operands = [*data, *back, template, azimuth]
     specs = [pl.BlockSpec((rows, width), lambda s, at_ref: (0, 0))] * (2 * ring)
@@ -366,6 +373,7 @@
         operands += [old]
     return pl.pallas_call(
         functools.partial(finish_kernel, ring),
+        compiler_params=GRANT,
         out_shape=jax.ShapeDtypeStruct((rows, samples), jnp.float32),
         grid_spec=pltpu.PrefetchScalarGridSpec(
             num_scalar_prefetch=1,
@@ -384,7 +392,7 @@
     data, outs = refs[:ring], refs[ring:]
     rows, width = outs[0].shape
     for s in range(ring):
-        azimuth = azimuth_ref[:, pl.ds(block_start(ring, at_ref[0], s, start), width)]
+        azimuth = azimuth_ref[:, pl.ds(block_start(at_ref[0], s, start), width)]
         levels = dot(both_ref[...], onehot_of(azimuth, both_ref.shape[1]))
         value = data[s][...] - (levels[:rows] + levels[rows:])
         outs[s][...] = value - back_ref[...] if s == 0 else value
@@ -394,6 +402,7 @@
     rows, width = data[0].shape
     return pl.pallas_call(
         functools.partial(level_kernel, ring, start),
+        compiler_params=GRANT,
         out_shape=[jax.ShapeDtypeStruct((rows, width), jnp.float32)] * ring,
         in_specs=[pl.BlockSpec(memory_space=pltpu.SMEM)] + [pl.BlockSpec(memory_space=pltpu.VMEM)] * (3 + ring),
         out_specs=[pl.BlockSpec(memory_space=pltpu.VMEM)] * ring,
@@ -412,9 +421,6 @@
     me_only = jnp.full((1,), me, jnp.int32)
     at = jnp.stack([me, which, part_of, lax.rem(tm, 2), tm])
 
-    def send(array, shift):
-        return lax.ppermute(array, "det", [(i, (i + shift) % ring) for i in range(ring)])
-
     def swap(array, axis, bit):
         return lax.ppermute(array, axis, [(i, i ^ bit) for i in range(lax.axis_size(axis))])
 
@@ -424,11 +430,13 @@
     data, arrived = {}, {}
     order = [[(s, start, width) for s in (1, 2, 3)] for start, width in PIECES]
     order[-1] += [(0, start, width) for start, width in PIECES]
-    for pieces in order:
-        blocks = calibrate(ring, me_only, tod, gains, where, share, pieces)
+    for part, pieces in enumerate(order):
+        grant = GRANT if part else pltpu.CompilerParams()
+        place = jax.ShapeDtypeStruct if part else pltpu.VMEM
+        blocks = calibrate(me_only, tod, gains, where, share, pieces, grant, place)
         for (s, start, width), block in zip(pieces, blocks):
             data[s, start] = block
-            arrived[s, start] = send(block, s) if s else block
+            arrived[s, start] = swap(block, "det", s) if s else block
 
     banks = own_share(jnp.full((1,), part_of, jnp.int32), mode_bank, shares)
     for bit in (2, 1):
@@ -440,7 +448,7 @@
     banks = jnp.concatenate([banks, swap(banks, "tm", 1)], axis=0)
 
     pieces = [piece for part in order for piece in part]
-    keep, other = bin_data(ring, at, mode_index, azimuth, pieces, [data[s, start] for s, start, _ in pieces])
+    keep, other = bin_data(at, mode_index, azimuth, pieces, [data[s, start] for s, start, _ in pieces])
     sums = keep + swap(other, "tm", 1)
     half = NBIN // 2
     sums = sums[:, :half] + swap(sums[:, half:], "tm", 2)
@@ -461,7 +469,7 @@
     out = None
     for part, (start, width) in enumerate(PIECES):
         removed = common_mode(ring, modes, [arrived[s, start] for s in range(ring)])
-        back = [send(removed[s], -s) if s else removed[s] for s in range(ring)]
+        back = [swap(removed[s], "det", s) if s else removed[s] for s in range(ring)]
         mine = [data[s, start] for s in range(ring)]
         if part < len(PIECES) - LATE:
             out = finish_piece(ring, at, start, mine, back, template, azimuth, out)

time: 301 us -> 282 us (0.937)
  Pallas kernels: 85.2 us -> 49.7 us
  starting transfers between devices: 61.4 us -> 88.6 us
  other arithmetic: 7.71 us -> 1.16 us
  waiting for transfers between devices: 133 us -> 128 us
    ppermute x15 -> x39, starting transfers between devices: 18.9 us -> 88.6 us  [swap(): lax.ppermute(array, axis, [(i, i ^ bit) for i in range(lax.axis_size(axis...]
    ppermute x24 -> x0, waiting for transfers between devices: 67.8 us -> none  [send(): lax.ppermute(array, 'det', [(i, (i + shift) % ring) for i in range(ring)])]
    ppermute x15 -> x39, waiting for transfers between devices: 65.7 us -> 128 us  [swap(): lax.ppermute(array, axis, [(i, i ^ bit) for i in range(lax.axis_size(axis...]
    ppermute x24 -> x0, starting transfers between devices: 42.5 us -> none  [send(): lax.ppermute(array, 'det', [(i, (i + shift) % ring) for i in range(ring)])]
    pallas_call x17, Pallas kernels: 81.1 us -> 47 us  [the longest x4 17.8 us: common_mode(): pl.pallas_call(functools.partial(filter_kernel, ring), compiler_params=GR...]
    unnamed x96 -> x30, local copies, waits for them, and re-layouts: 7.82 us -> 10.1 us
  transfers between devices with their start and end apart: 39 -> 39, of which waited for: 14 -> 16; matrix products, arithmetic and copies ran while one was open for 5% -> 3% of each run, Pallas kernels for 24% -> 14%
where the time goes in v4:
time: 282 us
  waiting for transfers between devices  128 us (45%)
  starting transfers between devices  88.6 us (31%)
  Pallas kernels  49.7 us (18%)
  local copies, waits for them, and re-layouts  13.7 us (5%)
    ppermute x39, waiting for transfers between devices, swap(): lax.ppermute(array, axis, [(i, i ^ bit) for i in range(lax.axis_size(axis...  128 us
    ppermute x39, starting transfers between devices, swap(): lax.ppermute(array, axis, [(i, i ^ bit) for i in range(lax.axis_size(axis...  88.6 us
    pallas_call x4, Pallas kernels, common_mode(): pl.pallas_call(functools.partial(filter_kernel, ring), compiler_params=GR...  17.8 us
    unnamed x30, local copies, waits for them, and re-layouts  10.1 us
    pallas_call x2, Pallas kernels, finish_piece(): pl.pallas_call(functools.partial(finish_kernel, ring), compiler_params=GR...  6.84 us
    pallas_call x1, Pallas kernels, pool(): pl.pallas_call(functools.partial(pool_kernel, ring, shares), compiler_par...  6.83 us
  transfers between devices with their start and end apart: 39, of which 16 were waited for; matrix products, arithmetic and copies ran while one was open for 3% of the time, Pallas kernels for 14%

profile of v4, /device:TPU:0, one launch (start us, length us, event | category | flops | bytes accessed | tf_op | source)
XLA Modules:
  0.0 281.8 jit_solution(9843801713782454851)
XLA Ops:
  0.0 0.9 shard_map.82
  0.9 4.1 %collective-permute-start = (f32[1,2,32,512]{3,2,1,0:T(8,128)S(1)}, f32[1,2,32,512]{3,2,1,0:T(8,128)S(1)}, u32[]{:S(2)}, u32[]{:S(2)}) collective-permute-start(f32[1,2,32,512]{3,2,1,0:T(8,128)S(1)} %shard_map.82), channel_id=1, source_target_pairs={{0,8},{4,12},{8,0},{12,4},{1,9},{5,13},{9,1},{13,5},{2,10},{6,14},... | collective-permute-start | bytes 393224 | tf_op jit(solution)/shard_map/ppermute | solution.py:425
  5.0 6.3 %collective-permute-done = f32[1,2,32,512]{3,2,1,0:T(8,128)S(1)} collective-permute-done((f32[1,2,32,512]{3,2,1,0:T(8,128)S(1)}, f32[1,2,32,512]{3,2,1,0:T(8,128)S(1)}, u32[]{:S(2)}, u32[]{:S(2)}) %collective-permute-start) | collective-permute-done | bytes 131104 | tf_op jit(solution)/shard_map/ppermute | solution.py:425
  12.2 6.7 %collective-permute-done.1 = f32[2,2,32,512]{3,2,1,0:T(8,128)S(1)} collective-permute-done((f32[2,2,32,512]{3,2,1,0:T(8,128)S(1)}, f32[2,2,32,512]{3,2,1,0:T(8,128)S(1)}, u32[]{:S(2)}, u32[]{:S(2)}) %collective-permute-start.1) | collective-permute-done | bytes 262176 | tf_op jit(solution)/shard_map/ppermute | solution.py:425
  19.0 1.3 collective-permute-start.2
  20.3 1.5 collective-permute-start.3
  23.3 0.9 constant_dynamic-update-slice_fusion.4
  24.2 7.1 %collective-permute-done.2 = f32[4,2,32,512]{3,2,1,0:T(8,128)S(1)} collective-permute-done((f32[4,2,32,512]{3,2,1,0:T(8,128)S(1)}, f32[4,2,32,512]{3,2,1,0:T(8,128)S(1)}, u32[]{:S(2)}, u32[]{:S(2)}) %collective-permute-start.2) | collective-permute-done | bytes 524320 | tf_op jit(solution)/shard_map/ppermute | solution.py:425
  31.3 1.3 collective-permute-start.4
  33.0 1.2 collective-permute-start.5
  34.2 1.1 constant_dynamic-update-slice_fusion.3
  35.3 1.1 constant_dynamic-update-slice_fusion.2
  36.4 1.4 collective-permute-done.4
  37.9 0.9 constant_dynamic-update-slice_fusion.1
  39.5 0.9 constant_dynamic-update-slice_fusion
  41.6 2.2 copy-done
  44.1 1.5 shard_map.83
  45.7 2.2 copy-done.1
  49.0 3.7 %shard_map.87 = (f32[256,512]{1,0:T(8,128)S(1)}, f32[256,512]{1,0:T(8,128)S(1)}) custom-call(s32[5]{0:T(128)S(1)} %stack.20.at_ref, s32[4]{0:T(128)S(1)} %copy-done.11, s32[1,4096]{1,0:T(1,128)S(1)} %bitcast.44, f32[256,256]{1,0:T(8,128)S(1)} %get-tuple-element.54.refs_0_.refs_1_, f32[256,256]{1,0:T(8,128)S(1)} %get-tuple-element.55.refs_1_.refs_2_, ...), custom_call_target="tpu_custom_call" | custom-call | flops 2147483648 | bytes 4194304 | tf_op jit(solution)/shard_map/pallas_call | solution.py:251
  53.3 1.5 collective-permute-done.7
  55.0 1.2 collective-permute-start.8
  56.2 7.4 %collective-permute-done.8 = f32[256,256]{1,0:T(8,128)S(1)} collective-permute-done((f32[256,256]{1,0:T(8,128)S(1)}, f32[256,256]{1,0:T(8,128)S(1)}, u32[]{:S(2)}, u32[]{:S(2)}) %collective-permute-start.8) | collective-permute-done | bytes 262176 | tf_op jit(solution)/shard_map/ppermute | solution.py:425
  63.7 1.5 constant_dynamic-update-slice_fusion.7.bank_ref
  65.2 6.8 %shard_map.88 = (f32[256,128]{1,0:T(8,128)S(1)}, f32[256,128]{1,0:T(8,128)S(1)}, f32[512,128]{1,0:T(8,128)S(1)}) custom-call(s32[5]{0:T(128)S(1)} %stack.20.at_ref, f32[32,2,32,512]{3,2,1,0:T(8,128)} %constant_dynamic-update-slice_fusion.7.bank_ref, f32[2,256,512]{2,1,0:T(8,128)S(1)} %copy-done.7, f32[2,512,512]{2,1,0:T(8,128)S(1)} %copy-done.2, ...), custom_call_target="tpu_custom_call" | custom-call | flops 2013265920 | bytes 4194304 | tf_op jit(solution)/shard_map/pallas_call | solution.py:301
  72.0 2.2 collective-permute-start.9
  74.2 0.9 convert_reduce_fusion
  75.3 4.1 %collective-permute-start.22 = (f32[256,128]{1,0:T(8,128)S(1)}, f32[256,128]{1,0:T(8,128)S(1)}, u32[]{:S(2)}, u32[]{:S(2)}) collective-permute-start(f32[256,128]{1,0:T(8,128)S(1)} %get-tuple-element.61.refs_7_.refs_2_), channel_id=1, source_target_pairs={{0,8},{4,12},{8,0},{12,4},{1,9},{5,13},{9,1},{13,5},{2,10},{6,14},... | collective-permute-start | bytes 393224 | tf_op jit(solution)/shard_map/ppermute | solution.py:425
  79.4 1.3 collective-permute-start.33
  80.7 4.8 %collective-permute-done.9 = f32[512,128]{1,0:T(8,128)S(1)} collective-permute-done((f32[512,128]{1,0:T(8,128)S(1)}, f32[512,128]{1,0:T(8,128)S(1)}, u32[]{:S(2)}, u32[]{:S(2)}) %collective-permute-start.9) | collective-permute-done | bytes 262176 | tf_op jit(solution)/shard_map/ppermute | solution.py:425
  85.5 4.5 %collective-permute-start.35 = (f32[256,256]{1,0:T(8,128)S(1)}, f32[256,256]{1,0:T(8,128)S(1)}, u32[]{:S(2)}, u32[]{:S(2)}) collective-permute-start(f32[256,256]{1,0:T(8,128)S(1)} %get-tuple-element.56.refs_2_.refs_3_), channel_id=1, source_target_pairs={{0,12},{4,8},{8,4},{12,0},{1,13},{5,9},{9,5},{13,1},{2,14},{6,10},... | collective-permute-start | bytes 786440 | tf_op jit(solution)/shard_map/ppermute | solution.py:425
  90.0 1.8 collective-permute-done.21.refs_1_
  91.8 3.2 %collective-permute-start.10 = (f32[256,128]{1,0:T(8,128)S(1)}, f32[256,128]{1,0:T(8,128)S(1)}, u32[]{:S(2)}, u32[]{:S(2)}) collective-permute-start(f32[256,128]{1,0:T(8,128)S(1)} %slice_add_fusion.1), channel_id=1, source_target_pairs={{0,8},{4,12},{8,0},{12,4},{1,9},{5,13},{9,1},{13,5},{2,10},{6,14},... | collective-permute-start | bytes 393224 | tf_op jit(solution)/shard_map/ppermute | solution.py:425
  95.0 5.1 %shard_map.90 = (bf16[512,1024]{1,0:T(8,128)(2,1)S(1)}, bf16[512,1024]{1,0:T(8,128)(2,1)S(1)}, bf16[1024,512]{1,0:T(8,128)(2,1)S(1)}, bf16[1024,512]{1,0:T(8,128)(2,1)S(1)}) custom-call(s32[5]{0:T(128)S(1)} %stack.20.at_ref, f32[32,2,32,512]{3,2,1,0:T(8,128)} %constant_dynamic-update-slice_fusion.7.bank_ref, f32[2,512,512]{2,1,0:T(8,128)S(1)} %copy-done.2), custom_call_target="tpu_custom_call" | custom-call | flops 1610612736 | bytes 6291456 | tf_op jit(solution)/shard_map/pallas_call | solution.py:121
  100.1 2.7 collective-permute-start.27
  102.8 3.5 %collective-permute-start.28 = (f32[256,512]{1,0:T(8,128)S(1)}, f32[256,512]{1,0:T(8,128)S(1)}, u32[]{:S(2)}, u32[]{:S(2)}) collective-permute-start(f32[256,512]{1,0:T(8,128)S(1)} %get-tuple-element.58.refs_4_.refs_2_), channel_id=1, source_target_pairs={{0,8},{4,12},{8,0},{12,4},{1,9},{5,13},{9,1},{13,5},{2,10},{6,14},... | collective-permute-start | bytes 1572872 | tf_op jit(solution)/shard_map/ppermute | solution.py:425
  106.3 9.7 %collective-permute-done.10 = f32[256,128]{1,0:T(8,128)S(1)} collective-permute-done((f32[256,128]{1,0:T(8,128)S(1)}, f32[256,128]{1,0:T(8,128)S(1)}, u32[]{:S(2)}, u32[]{:S(2)}) %collective-permute-start.10) | collective-permute-done | bytes 131104 | tf_op jit(solution)/shard_map/ppermute | solution.py:425
  116.0 2.5 collective-permute-start.29
  118.5 1.4 collective-permute-start.23
  119.9 1.5 collective-permute-start.11
  121.4 3.4 %shard_map.96 = (f32[256,256]{1,0:T(8,128)S(1)}, f32[256,256]{1,0:T(8,128)S(1)}, f32[256,256]{1,0:T(8,128)S(1)}, f32[256,256]{1,0:T(8,128)S(1)}) custom-call(bf16[512,1024]{1,0:T(8,128)(2,1)S(1)} %get-tuple-element.75.first_high, bf16[512,1024]{1,0:T(8,128)(2,1)S(1)} %get-tuple-element.76.first_low, bf16[1024,512]{1,0:T(8,128)(2,1)S(1)} %get-tuple-element.77.second_high, ...), custom_call_target="tpu_custom_call" | custom-call | flops 1610612736 | bytes 2097152 | tf_op jit(solution)/shard_map/pallas_call | solution.py:158
  124.8 20.6 %collective-permute-done.23.refs_3_ = f32[256,128]{1,0:T(8,128)S(1)} collective-permute-done((f32[256,128]{1,0:T(8,128)S(1)}, f32[256,128]{1,0:T(8,128)S(1)}, u32[]{:S(2)}, u32[]{:S(2)}) %collective-permute-start.23) | collective-permute-done | bytes 131104 | tf_op jit(solution)/shard_map/ppermute | solution.py:425
  145.4 20.5 %collective-permute-start.15 = (f32[256,128]{1,0:T(8,128)S(1)}, f32[256,128]{1,0:T(8,128)S(1)}, u32[]{:S(2)}, u32[]{:S(2)}) collective-permute-start(f32[256,128]{1,0:T(8,128)S(1)} %get-tuple-element.63.refs_9_.refs_1_), channel_id=1, source_target_pairs={{0,4},{4,0},{8,12},{12,8},{1,5},{5,1},{9,13},{13,9},{2,6},{6,2},{1... | collective-permute-start | bytes 393224 | tf_op jit(solution)/shard_map/ppermute | solution.py:425
  165.9 3.5 %shard_map.93 = (f32[256,128]{1,0:T(8,128)S(1)}, f32[256,128]{1,0:T(8,128)S(1)}, f32[256,128]{1,0:T(8,128)S(1)}, f32[256,128]{1,0:T(8,128)S(1)}) custom-call(bf16[512,1024]{1,0:T(8,128)(2,1)S(1)} %get-tuple-element.75.first_high, bf16[512,1024]{1,0:T(8,128)(2,1)S(1)} %get-tuple-element.76.first_low, bf16[1024,512]{1,0:T(8,128)(2,1)S(1)} %get-tuple-element.77.second_high, ...), custom_call_target="tpu_custom_call" | custom-call | flops 805306368 | bytes 1048576 | tf_op jit(solution)/shard_map/pallas_call | solution.py:158
  169.4 1.5 collective-permute-start.14
  170.9 2.2 collective-permute-done.14
  173.2 1.4 collective-permute-start.16
  174.5 1.5 collective-permute-start.17
  176.7 1.4 collective-permute-start.36
  178.1 7.4 %shard_map.95 = (f32[256,512]{1,0:T(8,128)S(1)}, f32[256,512]{1,0:T(8,128)S(1)}, f32[256,512]{1,0:T(8,128)S(1)}, f32[256,512]{1,0:T(8,128)S(1)}) custom-call(bf16[512,1024]{1,0:T(8,128)(2,1)S(1)} %get-tuple-element.75.first_high, bf16[512,1024]{1,0:T(8,128)(2,1)S(1)} %get-tuple-element.76.first_low, bf16[1024,512]{1,0:T(8,128)(2,1)S(1)} %get-tuple-element.77.second_high, ...), custom_call_target="tpu_custom_call" | custom-call | flops 3221225472 | bytes 4194304 | tf_op jit(solution)/shard_map/pallas_call | solution.py:158
  186.2 2.3 collective-permute-start.31
  188.5 1.5 collective-permute-start.32
  190.0 11.3 %collective-permute-done.36.refs_5_ = f32[256,256]{1,0:T(8,128)S(1)} collective-permute-done((f32[256,256]{1,0:T(8,128)S(1)}, f32[256,256]{1,0:T(8,128)S(1)}, u32[]{:S(2)}, u32[]{:S(2)}) %collective-permute-start.36) | collective-permute-done | bytes 262176 | tf_op jit(solution)/shard_map/ppermute | solution.py:425
  201.3 1.9 collective-permute-start.38
  203.3 3.5 %shard_map.91 = (f32[256,128]{1,0:T(8,128)S(1)}, f32[256,128]{1,0:T(8,128)S(1)}, f32[256,128]{1,0:T(8,128)S(1)}, f32[256,128]{1,0:T(8,128)S(1)}) custom-call(bf16[512,1024]{1,0:T(8,128)(2,1)S(1)} %get-tuple-element.75.first_high, bf16[512,1024]{1,0:T(8,128)(2,1)S(1)} %get-tuple-element.76.first_low, bf16[1024,512]{1,0:T(8,128)(2,1)S(1)} %get-tuple-element.77.second_high, ...), custom_call_target="tpu_custom_call" | custom-call | flops 805306368 | bytes 1048576 | tf_op jit(solution)/shard_map/pallas_call | solution.py:158
  207.4 45.1 %collective-permute-done.37.refs_6_ = f32[256,256]{1,0:T(8,128)S(1)} collective-permute-done((f32[256,256]{1,0:T(8,128)S(1)}, f32[256,256]{1,0:T(8,128)S(1)}, u32[]{:S(2)}, u32[]{:S(2)}) %collective-permute-start.37) | collective-permute-done | bytes 262176 | tf_op jit(solution)/shard_map/ppermute | solution.py:425
  252.5 2.8 %collective-permute-start.26 = (f32[256,128]{1,0:T(8,128)S(1)}, f32[256,128]{1,0:T(8,128)S(1)}, u32[]{:S(2)}, u32[]{:S(2)}) collective-permute-start(f32[256,128]{1,0:T(8,128)S(1)} %get-tuple-element.94), channel_id=1, source_target_pairs={{0,12},{4,8},{8,4},{12,0},{1,13},{5,9},{9,5},{13,1},{2,14},{6,10},... | collective-permute-start | bytes 393224 | tf_op jit(solution)/shard_map/ppermute | solution.py:425
  255.4 3.0 %shard_map.97.refs_10_ = f32[256,4096]{1,0:T(8,128)} custom-call(s32[5]{0:T(128)S(1)} %stack.20.at_ref, f32[256,256]{1,0:T(8,128)S(1)} %get-tuple-element.66.refs_12_.refs_0_, f32[256,256]{1,0:T(8,128)S(1)} %get-tuple-element.54.refs_0_.refs_1_, f32[256,256]{1,0:T(8,128)S(1)} %get-tuple-element.55.refs_1_.refs_2_, ...), custom_call_target="tpu_custom_call" | custom-call | flops 536870912 | bytes 3145728 | tf_op jit(solution)/shard_map/pallas_call | solution.py:374
  258.4 10.9 %collective-permute-start.18 = (f32[256,128]{1,0:T(8,128)S(1)}, f32[256,128]{1,0:T(8,128)S(1)}, u32[]{:S(2)}, u32[]{:S(2)}) collective-permute-start(f32[256,128]{1,0:T(8,128)S(1)} %get-tuple-element.84), channel_id=1, source_target_pairs={{0,4},{4,0},{8,12},{12,8},{1,5},{5,1},{9,13},{13,9},{2,6},{6,2},{1... | collective-permute-start | bytes 393224 | tf_op jit(solution)/shard_map/ppermute | solution.py:425
  269.3 2.4 collective-permute-start.20
  271.8 1.3 shard_map.94
  273.0 3.8 %shard_map.98.refs_7_ = f32[256,4096]{1,0:T(8,128)} custom-call(s32[5]{0:T(128)S(1)} %stack.20.at_ref, f32[256,512]{1,0:T(8,128)S(1)} %get-tuple-element.67.refs_13_.refs_0_, f32[256,512]{1,0:T(8,128)S(1)} %get-tuple-element.57.refs_3_.refs_1_, f32[256,512]{1,0:T(8,128)S(1)} %get-tuple-element.58.refs_4_.refs_2_, ...), custom_call_target="tpu_custom_call", output_to_operand_aliasing={{}: (11, {})} | custom-call | flops 1073741824 | bytes 6291456 | tf_op jit(solution)/shard_map/pallas_call | solution.py:374
  276.8 1.4 shard_map.99.refs_7_
  278.2 1.3 shard_map.92
  280.2 1.4 shard_map.100
  (81 shorter events, 9.9 us)
Async XLA Ops:
  0.9 10.4 %collective-permute-start = (f32[1,2,32,512]{3,2,1,0:T(8,128)S(1)}, f32[1,2,32,512]{3,2,1,0:T(8,128)S(1)}, u32[]{:S(2)}, u32[]{:S(2)}) collective-permute-start(f32[1,2,32,512]{3,2,1,0:T(8,128)S(1)} %shard_map.82), channel_id=1, source_target_pairs={{0,8},{4,12},{8,0},{12,4},{1,9},{5,13},{9,1},{13,5},{2,10},{6,14},... | collective-permute-start | bytes 393224 | tf_op jit(solution)/shard_map/ppermute | solution.py:425
  11.4 28.9 %copy-start.11 = (s32[4]{0:T(128)S(1)}, s32[4]{0:T(128)}, u32[]{:S(2)}) copy-start(s32[4]{0:T(128)} %index_ref.1) | copy-start | bytes 52
  11.4 30.2 %copy-start.3 = (s32[4096]{0:T(1024)S(1)}, s32[4096]{0:T(1024)}, u32[]{:S(2)}) copy-start(s32[4096]{0:T(1024)} %param.10) | copy-start | bytes 49156
  11.4 30.2 %copy-start.5 = (f32[4096]{0:T(1024)S(1)}, f32[4096]{0:T(1024)}, u32[]{:S(2)}) copy-start(f32[4096]{0:T(1024)} %param.11) | copy-start | bytes 49156
  11.4 30.1 %copy-start.8 = (f32[256,64]{0,1:T(8,128)S(1)}, f32[256,64]{0,1:T(8,128)}, u32[]{:S(2)}) copy-start(f32[256,64]{0,1:T(8,128)} %param.9) | copy-start | bytes 196612
  11.4 7.5 %collective-permute-start.1 = (f32[2,2,32,512]{3,2,1,0:T(8,128)S(1)}, f32[2,2,32,512]{3,2,1,0:T(8,128)S(1)}, u32[]{:S(2)}, u32[]{:S(2)}) collective-permute-start(f32[2,2,32,512]{3,2,1,0:T(8,128)S(1)} %pad_maximum_fusion.1), channel_id=1, source_target_pairs={{0,4},{4,0},{8,12},{12,8},{1,5},{5,1},{9,13},{13,9},{2,6},{6,2},{1... | collective-permute-start | bytes 786440 | tf_op jit(solution)/shard_map/ppermute | solution.py:425
  19.0 12.3 %collective-permute-start.2 = (f32[4,2,32,512]{3,2,1,0:T(8,128)S(1)}, f32[4,2,32,512]{3,2,1,0:T(8,128)S(1)}, u32[]{:S(2)}, u32[]{:S(2)}) collective-permute-start(f32[4,2,32,512]{3,2,1,0:T(8,128)S(1)} %pad_maximum_fusion), channel_id=1, source_target_pairs={{0,2},{1,3},{2,0},{3,1},{4,6},{5,7},{6,4},{7,5},{8,10},{9,11},{10,... | collective-permute-start | bytes 1572872 | tf_op jit(solution)/shard_map/ppermute | solution.py:425
  20.3 12.7 %collective-permute-start.3 = (f32[4,2,32,512]{3,2,1,0:T(8,128)S(1)}, f32[4,2,32,512]{3,2,1,0:T(8,128)S(1)}, u32[]{:S(2)}, u32[]{:S(2)}) collective-permute-start(f32[4,2,32,512]{3,2,1,0:T(8,128)S(1)} %pad_maximum_fusion), channel_id=1, source_target_pairs={{0,16},{16,0},{1,17},{17,1},{2,18},{18,2},{3,19},{19,3},{4,20},{20... | collective-permute-start | bytes 1572872 | tf_op jit(solution)/shard_map/ppermute | solution.py:425
  31.3 6.6 %collective-permute-start.4 = (f32[2,2,32,512]{3,2,1,0:T(8,128)S(1)}, f32[2,2,32,512]{3,2,1,0:T(8,128)S(1)}, u32[]{:S(2)}, u32[]{:S(2)}) collective-permute-start(f32[2,2,32,512]{3,2,1,0:T(8,128)S(1)} %slice.24), channel_id=1, source_target_pairs={{0,16},{16,0},{1,17},{17,1},{2,18},{18,2},{3,19},{19,3},{4,20},{20... | collective-permute-start | bytes 786440 | tf_op jit(solution)/shard_map/ppermute | solution.py:425
  33.0 6.4 %collective-permute-start.5 = (f32[2,2,32,512]{3,2,1,0:T(8,128)S(1)}, f32[2,2,32,512]{3,2,1,0:T(8,128)S(1)}, u32[]{:S(2)}, u32[]{:S(2)}) collective-permute-start(f32[2,2,32,512]{3,2,1,0:T(8,128)S(1)} %slice.25), channel_id=1, source_target_pairs={{0,2},{1,3},{2,0},{3,1},{4,6},{5,7},{6,4},{7,5},{8,10},{9,11},{10,... | collective-permute-start | bytes 786440 | tf_op jit(solution)/shard_map/ppermute | solution.py:425
  40.3 23.3 %collective-permute-start.6 = (f32[16,2,32,512]{3,2,1,0:T(8,128)}, f32[16,2,32,512]{3,2,1,0:T(8,128)S(1)}, u32[]{:S(2)}, u32[]{:S(2)}) collective-permute-start(f32[16,2,32,512]{3,2,1,0:T(8,128)} %get-tuple-element.107), channel_id=1, source_target_pairs={{0,1},{1,0},{2,3},{3,2},{4,5},{5,4},{6,7},{7,6},{8,9},{9,8},{10,11... | collective-permute-start | bytes 6291464 | tf_op jit(solution)/shard_map/ppermute | solution.py:425
  41.6 2.2 copy-start
  44.1 1.6 copy-start.4
  44.1 1.6 copy-start.6
  44.1 1.6 copy-start.9
  45.7 2.2 copy-start.1
  48.3 0.7 copy-start.10
  52.7 12.4 %copy-start.2 = (f32[2,512,512]{2,1,0:T(8,128)S(1)}, f32[2,512,512]{2,1,0:T(8,128)}, u32[]{:S(2)}) copy-start(f32[2,512,512]{2,1,0:T(8,128)} %mix_ref.3) | copy-start | bytes 6291460
  52.7 12.4 %copy-start.7 = (f32[2,256,512]{2,1,0:T(8,128)S(1)}, f32[2,256,512]{2,1,0:T(8,128)}, u32[]{:S(2)}) copy-start(f32[2,256,512]{2,1,0:T(8,128)} %own_ref.1) | copy-start | bytes 3145732
  52.7 2.1 collective-permute-start.7
  55.0 8.7 %collective-permute-start.8 = (f32[256,256]{1,0:T(8,128)S(1)}, f32[256,256]{1,0:T(8,128)S(1)}, u32[]{:S(2)}, u32[]{:S(2)}) collective-permute-start(f32[256,256]{1,0:T(8,128)S(1)} %slice.27), channel_id=1, source_target_pairs={{0,2},{1,3},{2,0},{3,1},{4,6},{5,7},{6,4},{7,5},{8,10},{9,11},{10,... | collective-permute-start | bytes 786440 | tf_op jit(solution)/shard_map/ppermute | solution.py:425
  72.0 13.5 %collective-permute-start.9 = (f32[512,128]{1,0:T(8,128)S(1)}, f32[512,128]{1,0:T(8,128)S(1)}, u32[]{:S(2)}, u32[]{:S(2)}) collective-permute-start(f32[512,128]{1,0:T(8,128)S(1)} %get-tuple-element.73), channel_id=1, source_target_pairs={{0,4},{4,0},{8,12},{12,8},{1,5},{5,1},{9,13},{13,9},{2,6},{6,2},{1... | collective-permute-start | bytes 786440 | tf_op jit(solution)/shard_map/ppermute | solution.py:425
  75.1 5.6 %collective-permute-start.13 = (f32[8,512]{1,0:T(8,128)S(1)}, f32[8,512]{1,0:T(8,128)S(1)}, u32[]{:S(2)}, u32[]{:S(2)}) collective-permute-start(f32[8,512]{1,0:T(8,128)S(1)} %broadcast_in_dim.20), channel_id=1, source_target_pairs={{0,1},{1,0},{2,3},{3,2},{4,5},{5,4},{6,7},{7,6},{8,9},{9,8},{10,11... | collective-permute-start | bytes 49160 | tf_op jit(solution)/shard_map/ppermute | solution.py:425
  75.2 16.6 %collective-permute-start.21 = (f32[256,128]{1,0:T(8,128)S(1)}, f32[256,128]{1,0:T(8,128)S(1)}, u32[]{:S(2)}, u32[]{:S(2)}) collective-permute-start(f32[256,128]{1,0:T(8,128)S(1)} %get-tuple-element.60.refs_6_.refs_1_), channel_id=1, source_target_pairs={{0,4},{4,0},{8,12},{12,8},{1,5},{5,1},{9,13},{13,9},{2,6},{6,2},{1... | collective-permute-start | bytes 393224 | tf_op jit(solution)/shard_map/ppermute | solution.py:425
  75.3 24.8 %collective-permute-start.22 = (f32[256,128]{1,0:T(8,128)S(1)}, f32[256,128]{1,0:T(8,128)S(1)}, u32[]{:S(2)}, u32[]{:S(2)}) collective-permute-start(f32[256,128]{1,0:T(8,128)S(1)} %get-tuple-element.61.refs_7_.refs_2_), channel_id=1, source_target_pairs={{0,8},{4,12},{8,0},{12,4},{1,9},{5,13},{9,1},{13,5},{2,10},{6,14},... | collective-permute-start | bytes 393224 | tf_op jit(solution)/shard_map/ppermute | solution.py:425
  79.4 23.4 %collective-permute-start.33 = (f32[256,256]{1,0:T(8,128)S(1)}, f32[256,256]{1,0:T(8,128)S(1)}, u32[]{:S(2)}, u32[]{:S(2)}) collective-permute-start(f32[256,256]{1,0:T(8,128)S(1)} %get-tuple-element.54.refs_0_.refs_1_), channel_id=1, source_target_pairs={{0,4},{4,0},{8,12},{12,8},{1,5},{5,1},{9,13},{13,9},{2,6},{6,2},{1... | collective-permute-start | bytes 786440 | tf_op jit(solution)/shard_map/ppermute | solution.py:425
  80.7 37.8 %collective-permute-start.34 = (f32[256,256]{1,0:T(8,128)S(1)}, f32[256,256]{1,0:T(8,128)S(1)}, u32[]{:S(2)}, u32[]{:S(2)}) collective-permute-start(f32[256,256]{1,0:T(8,128)S(1)} %get-tuple-element.55.refs_1_.refs_2_), channel_id=1, source_target_pairs={{0,8},{4,12},{8,0},{12,4},{1,9},{5,13},{9,1},{13,5},{2,10},{6,14},... | collective-permute-start | bytes 786440 | tf_op jit(solution)/shard_map/ppermute | solution.py:425
  85.5 34.4 %collective-permute-start.35 = (f32[256,256]{1,0:T(8,128)S(1)}, f32[256,256]{1,0:T(8,128)S(1)}, u32[]{:S(2)}, u32[]{:S(2)}) collective-permute-start(f32[256,256]{1,0:T(8,128)S(1)} %get-tuple-element.56.refs_2_.refs_3_), channel_id=1, source_target_pairs={{0,12},{4,8},{8,4},{12,0},{1,13},{5,9},{9,5},{13,1},{2,14},{6,10},... | collective-permute-start | bytes 786440 | tf_op jit(solution)/shard_map/ppermute | solution.py:425
  91.8 24.2 %collective-permute-start.10 = (f32[256,128]{1,0:T(8,128)S(1)}, f32[256,128]{1,0:T(8,128)S(1)}, u32[]{:S(2)}, u32[]{:S(2)}) collective-permute-start(f32[256,128]{1,0:T(8,128)S(1)} %slice_add_fusion.1), channel_id=1, source_target_pairs={{0,8},{4,12},{8,0},{12,4},{1,9},{5,13},{9,1},{13,5},{2,10},{6,14},... | collective-permute-start | bytes 393224 | tf_op jit(solution)/shard_map/ppermute | solution.py:425
  100.1 75.9 %collective-permute-start.27 = (f32[256,512]{1,0:T(8,128)S(1)}, f32[256,512]{1,0:T(8,128)S(1)}, u32[]{:S(2)}, u32[]{:S(2)}) collective-permute-start(f32[256,512]{1,0:T(8,128)S(1)} %get-tuple-element.57.refs_3_.refs_1_), channel_id=1, source_target_pairs={{0,4},{4,0},{8,12},{12,8},{1,5},{5,1},{9,13},{13,9},{2,6},{6,2},{1... | collective-permute-start | bytes 1572872 | tf_op jit(solution)/shard_map/ppermute | solution.py:425
  102.8 73.9 %collective-permute-start.28 = (f32[256,512]{1,0:T(8,128)S(1)}, f32[256,512]{1,0:T(8,128)S(1)}, u32[]{:S(2)}, u32[]{:S(2)}) collective-permute-start(f32[256,512]{1,0:T(8,128)S(1)} %get-tuple-element.58.refs_4_.refs_2_), channel_id=1, source_target_pairs={{0,8},{4,12},{8,0},{12,4},{1,9},{5,13},{9,1},{13,5},{2,10},{6,14},... | collective-permute-start | bytes 1572872 | tf_op jit(solution)/shard_map/ppermute | solution.py:425
  116.0 62.1 %collective-permute-start.29 = (f32[256,512]{1,0:T(8,128)S(1)}, f32[256,512]{1,0:T(8,128)S(1)}, u32[]{:S(2)}, u32[]{:S(2)}) collective-permute-start(f32[256,512]{1,0:T(8,128)S(1)} %get-tuple-element.59.refs_5_.refs_3_), channel_id=1, source_target_pairs={{0,12},{4,8},{8,4},{12,0},{1,13},{5,9},{9,5},{13,1},{2,14},{6,10},... | collective-permute-start | bytes 1572872 | tf_op jit(solution)/shard_map/ppermute | solution.py:425
  118.5 26.9 %collective-permute-start.23 = (f32[256,128]{1,0:T(8,128)S(1)}, f32[256,128]{1,0:T(8,128)S(1)}, u32[]{:S(2)}, u32[]{:S(2)}) collective-permute-start(f32[256,128]{1,0:T(8,128)S(1)} %get-tuple-element.62.refs_8_.refs_3_), channel_id=1, source_target_pairs={{0,12},{4,8},{8,4},{12,0},{1,13},{5,9},{9,5},{13,1},{2,14},{6,10},... | collective-permute-start | bytes 393224 | tf_op jit(solution)/shard_map/ppermute | solution.py:425
  119.9 49.5 %collective-permute-start.11 = (f32[256,128]{1,0:T(8,128)S(1)}, f32[256,128]{1,0:T(8,128)S(1)}, u32[]{:S(2)}, u32[]{:S(2)}) collective-permute-start(f32[256,128]{1,0:T(8,128)S(1)} %fusion), channel_id=1, source_target_pairs={{0,2},{1,3},{2,0},{3,1},{4,6},{5,7},{6,4},{7,5},{8,10},{9,11},{10,... | collective-permute-start | bytes 393224 | tf_op jit(solution)/shard_map/ppermute | solution.py:425
  145.4 29.1 %collective-permute-start.15 = (f32[256,128]{1,0:T(8,128)S(1)}, f32[256,128]{1,0:T(8,128)S(1)}, u32[]{:S(2)}, u32[]{:S(2)}) collective-permute-start(f32[256,128]{1,0:T(8,128)S(1)} %get-tuple-element.63.refs_9_.refs_1_), channel_id=1, source_target_pairs={{0,4},{4,0},{8,12},{12,8},{1,5},{5,1},{9,13},{13,9},{2,6},{6,2},{1... | collective-permute-start | bytes 393224 | tf_op jit(solution)/shard_map/ppermute | solution.py:425
  169.4 3.8 %collective-permute-start.14 = (f32[8,512]{1,0:T(8,128)S(1)}, f32[8,512]{1,0:T(8,128)S(1)}, u32[]{:S(2)}, u32[]{:S(2)}) collective-permute-start(f32[8,512]{1,0:T(8,128)S(1)} %broadcast_add_fusion), channel_id=1, source_target_pairs={{0,2},{1,3},{2,0},{3,1},{4,6},{5,7},{6,4},{7,5},{8,10},{9,11},{10,... | collective-permute-start | bytes 49160 | tf_op jit(solution)/shard_map/ppermute | solution.py:425
  173.2 12.4 %collective-permute-start.16 = (f32[256,128]{1,0:T(8,128)S(1)}, f32[256,128]{1,0:T(8,128)S(1)}, u32[]{:S(2)}, u32[]{:S(2)}) collective-permute-start(f32[256,128]{1,0:T(8,128)S(1)} %get-tuple-element.64.refs_10_.refs_2_), channel_id=1, source_target_pairs={{0,8},{4,12},{8,0},{12,4},{1,9},{5,13},{9,1},{13,5},{2,10},{6,14},... | collective-permute-start | bytes 393224 | tf_op jit(solution)/shard_map/ppermute | solution.py:425
  174.5 11.7 %collective-permute-start.17 = (f32[256,128]{1,0:T(8,128)S(1)}, f32[256,128]{1,0:T(8,128)S(1)}, u32[]{:S(2)}, u32[]{:S(2)}) collective-permute-start(f32[256,128]{1,0:T(8,128)S(1)} %get-tuple-element.65.refs_11_.refs_3_), channel_id=1, source_target_pairs={{0,12},{4,8},{8,4},{12,0},{1,13},{5,9},{9,5},{13,1},{2,14},{6,10},... | collective-permute-start | bytes 393224 | tf_op jit(solution)/shard_map/ppermute | solution.py:425
  176.0 12.5 %collective-permute-start.24 = (f32[256,128]{1,0:T(8,128)S(1)}, f32[256,128]{1,0:T(8,128)S(1)}, u32[]{:S(2)}, u32[]{:S(2)}) collective-permute-start(f32[256,128]{1,0:T(8,128)S(1)} %get-tuple-element.92), channel_id=1, source_target_pairs={{0,4},{4,0},{8,12},{12,8},{1,5},{5,1},{9,13},{13,9},{2,6},{6,2},{1... | collective-permute-start | bytes 393224 | tf_op jit(solution)/shard_map/ppermute | solution.py:425
  176.7 24.7 %collective-permute-start.36 = (f32[256,256]{1,0:T(8,128)S(1)}, f32[256,256]{1,0:T(8,128)S(1)}, u32[]{:S(2)}, u32[]{:S(2)}) collective-permute-start(f32[256,256]{1,0:T(8,128)S(1)} %get-tuple-element.100), channel_id=1, source_target_pairs={{0,4},{4,0},{8,12},{12,8},{1,5},{5,1},{9,13},{13,9},{2,6},{6,2},{1... | collective-permute-start | bytes 786440 | tf_op jit(solution)/shard_map/ppermute | solution.py:425
  178.0 23.3 %collective-permute-start.12 = (f32[256,256]{1,0:T(8,128)S(1)}, f32[256,256]{1,0:T(8,128)S(1)}, u32[]{:S(2)}, u32[]{:S(2)}) collective-permute-start(f32[256,256]{1,0:T(8,128)S(1)} %pad_maximum_fusion.2.here_ref), channel_id=1, source_target_pairs={{0,1},{1,0},{2,3},{3,2},{4,5},{5,4},{6,7},{7,6},{8,9},{9,8},{10,11... | collective-permute-start | bytes 786440 | tf_op jit(solution)/shard_map/ppermute | solution.py:425
  185.5 72.9 %collective-permute-start.30 = (f32[256,512]{1,0:T(8,128)S(1)}, f32[256,512]{1,0:T(8,128)S(1)}, u32[]{:S(2)}, u32[]{:S(2)}) collective-permute-start(f32[256,512]{1,0:T(8,128)S(1)} %get-tuple-element.96), channel_id=1, source_target_pairs={{0,4},{4,0},{8,12},{12,8},{1,5},{5,1},{9,13},{13,9},{2,6},{6,2},{1... | collective-permute-start | bytes 1572872 | tf_op jit(solution)/shard_map/ppermute | solution.py:425
  186.2 83.1 %collective-permute-start.31 = (f32[256,512]{1,0:T(8,128)S(1)}, f32[256,512]{1,0:T(8,128)S(1)}, u32[]{:S(2)}, u32[]{:S(2)}) collective-permute-start(f32[256,512]{1,0:T(8,128)S(1)} %get-tuple-element.97), channel_id=1, source_target_pairs={{0,8},{4,12},{8,0},{12,4},{1,9},{5,13},{9,1},{13,5},{2,10},{6,14},... | collective-permute-start | bytes 1572872 | tf_op jit(solution)/shard_map/ppermute | solution.py:425
  188.5 80.8 %collective-permute-start.32 = (f32[256,512]{1,0:T(8,128)S(1)}, f32[256,512]{1,0:T(8,128)S(1)}, u32[]{:S(2)}, u32[]{:S(2)}) collective-permute-start(f32[256,512]{1,0:T(8,128)S(1)} %get-tuple-element.98), channel_id=1, source_target_pairs={{0,12},{4,8},{8,4},{12,0},{1,13},{5,9},{9,5},{13,1},{2,14},{6,10},... | collective-permute-start | bytes 1572872 | tf_op jit(solution)/shard_map/ppermute | solution.py:425
  201.3 51.2 %collective-permute-start.37 = (f32[256,256]{1,0:T(8,128)S(1)}, f32[256,256]{1,0:T(8,128)S(1)}, u32[]{:S(2)}, u32[]{:S(2)}) collective-permute-start(f32[256,256]{1,0:T(8,128)S(1)} %get-tuple-element.101), channel_id=1, source_target_pairs={{0,8},{4,12},{8,0},{12,4},{1,9},{5,13},{9,1},{13,5},{2,10},{6,14},... | collective-permute-start | bytes 786440 | tf_op jit(solution)/shard_map/ppermute | solution.py:425
  201.3 51.2 %collective-permute-start.38 = (f32[256,256]{1,0:T(8,128)S(1)}, f32[256,256]{1,0:T(8,128)S(1)}, u32[]{:S(2)}, u32[]{:S(2)}) collective-permute-start(f32[256,256]{1,0:T(8,128)S(1)} %get-tuple-element.102), channel_id=1, source_target_pairs={{0,12},{4,8},{8,4},{12,0},{1,13},{5,9},{9,5},{13,1},{2,14},{6,10},... | collective-permute-start | bytes 786440 | tf_op jit(solution)/shard_map/ppermute | solution.py:425
  252.5 24.3 %collective-permute-start.25 = (f32[256,128]{1,0:T(8,128)S(1)}, f32[256,128]{1,0:T(8,128)S(1)}, u32[]{:S(2)}, u32[]{:S(2)}) collective-permute-start(f32[256,128]{1,0:T(8,128)S(1)} %get-tuple-element.93), channel_id=1, source_target_pairs={{0,8},{4,12},{8,0},{12,4},{1,9},{5,13},{9,1},{13,5},{2,10},{6,14},... | collective-permute-start | bytes 393224 | tf_op jit(solution)/shard_map/ppermute | solution.py:425
  252.5 24.3 %collective-permute-start.26 = (f32[256,128]{1,0:T(8,128)S(1)}, f32[256,128]{1,0:T(8,128)S(1)}, u32[]{:S(2)}, u32[]{:S(2)}) collective-permute-start(f32[256,128]{1,0:T(8,128)S(1)} %get-tuple-element.94), channel_id=1, source_target_pairs={{0,12},{4,8},{8,4},{12,0},{1,13},{5,9},{9,5},{13,1},{2,14},{6,10},... | collective-permute-start | bytes 393224 | tf_op jit(solution)/shard_map/ppermute | solution.py:425
  258.4 21.1 %collective-permute-start.18 = (f32[256,128]{1,0:T(8,128)S(1)}, f32[256,128]{1,0:T(8,128)S(1)}, u32[]{:S(2)}, u32[]{:S(2)}) collective-permute-start(f32[256,128]{1,0:T(8,128)S(1)} %get-tuple-element.84), channel_id=1, source_target_pairs={{0,4},{4,0},{8,12},{12,8},{1,5},{5,1},{9,13},{13,9},{2,6},{6,2},{1... | collective-permute-start | bytes 393224 | tf_op jit(solution)/shard_map/ppermute | solution.py:425
  269.3 10.9 %collective-permute-start.19 = (f32[256,128]{1,0:T(8,128)S(1)}, f32[256,128]{1,0:T(8,128)S(1)}, u32[]{:S(2)}, u32[]{:S(2)}) collective-permute-start(f32[256,128]{1,0:T(8,128)S(1)} %get-tuple-element.85), channel_id=1, source_target_pairs={{0,8},{4,12},{8,0},{12,4},{1,9},{5,13},{9,1},{13,5},{2,10},{6,14},... | collective-permute-start | bytes 393224 | tf_op jit(solution)/shard_map/ppermute | solution.py:425
  269.3 10.9 %collective-permute-start.20 = (f32[256,128]{1,0:T(8,128)S(1)}, f32[256,128]{1,0:T(8,128)S(1)}, u32[]{:S(2)}, u32[]{:S(2)}) collective-permute-start(f32[256,128]{1,0:T(8,128)S(1)} %get-tuple-element.86), channel_id=1, source_target_pairs={{0,12},{4,8},{8,4},{12,0},{1,13},{5,9},{9,5},{13,1},{2,14},{6,10},... | collective-permute-start | bytes 393224 | tf_op jit(solution)/shard_map/ppermute | solution.py:425

commit v5 on v4

--- a/solution.py
+++ b/solution.py
@@ -9,6 +9,7 @@
 BLOCK = 1024
 NBIN = 512
 PIECES = ((0, 256), (512, 512), (256, 128), (384, 128))
+USED = 448
 LATE = 2
 GRANT = pltpu.CompilerParams(vmem_limit_bytes=32 * 1024 * 1024)
 
@@ -426,7 +427,9 @@
 
     gains = gain_knots.T
     where, share = intervals[None, :], fraction[None, :]
+    share_bins, used = NBIN // lax.axis_size("tm"), USED // lax.axis_size("tm")
     azimuth = azimuth[None, :]
+    azimuth = azimuth + (share_bins - used) * sum((azimuth >= n * used).astype(jnp.int32) for n in range(1, NBIN // share_bins))
     data, arrived = {}, {}
     order = [[(s, start, width) for s in (1, 2, 3)] for start, width in PIECES]
     order[-1] += [(0, start, width) for start, width in PIECES]
@@ -454,8 +457,8 @@
     sums = sums[:, :half] + swap(sums[:, half:], "tm", 2)
     mine, cross, near = pool(ring, shares, at, banks, mode_bank, mode_mix, sums)
     near = swap(near, "det", 1)
-    cross = swap(cross + near[det_rows:], "det", 2)
-    template = mine - near[:det_rows] - cross
+    cross = swap((cross + near[det_rows:]).T[:used], "det", 2)
+    template = mine - near[:det_rows] - jnp.pad(cross, ((0, share_bins - used), (0, 0))).T
     template = jnp.concatenate([template, swap(template, "tm", 2)], axis=1)
     other = swap(template, "tm", 1)
 

time: 282 us -> 282 us (level)
  no operation moved by 1% of the time
where the time goes in v5:
time: 282 us
  waiting for transfers between devices  128 us (45%)
  starting transfers between devices  88.5 us (31%)
  Pallas kernels  49.7 us (18%)
  local copies, waits for them, and re-layouts  13.7 us (5%)
    ppermute x39, waiting for transfers between devices, swap(): lax.ppermute(array, axis, [(i, i ^ bit) for i in range(lax.axis_size(axis...  128 us
    ppermute x39, starting transfers between devices, swap(): lax.ppermute(array, axis, [(i, i ^ bit) for i in range(lax.axis_size(axis...  88.5 us
    pallas_call x4, Pallas kernels, common_mode(): pl.pallas_call(functools.partial(filter_kernel, ring), compiler_params=GR...  17.8 us
    unnamed x30, local copies, waits for them, and re-layouts  10.1 us
    pallas_call x2, Pallas kernels, finish_piece(): pl.pallas_call(functools.partial(finish_kernel, ring), compiler_params=GR...  6.85 us
    pallas_call x1, Pallas kernels, pool(): pl.pallas_call(functools.partial(pool_kernel, ring, shares), compiler_par...  6.81 us
  transfers between devices with their start and end apart: 39, of which 16 were waited for; matrix products, arithmetic and copies ran while one was open for 3% of the time, Pallas kernels for 14%

profile of v5, /device:TPU:0, one launch (start us, length us, event | category | flops | bytes accessed | tf_op | source)
XLA Modules:
  0.0 281.8 jit_solution(4893178771721070582)
XLA Ops:
  0.0 0.9 shard_map.82
  0.9 4.1 %collective-permute-start = (f32[1,2,32,512]{3,2,1,0:T(8,128)S(1)}, f32[1,2,32,512]{3,2,1,0:T(8,128)S(1)}, u32[]{:S(2)}, u32[]{:S(2)}) collective-permute-start(f32[1,2,32,512]{3,2,1,0:T(8,128)S(1)} %shard_map.82), channel_id=1, source_target_pairs={{0,8},{4,12},{8,0},{12,4},{1,9},{5,13},{9,1},{13,5},{2,10},{6,14},... | collective-permute-start | bytes 393224 | tf_op jit(solution)/shard_map/ppermute | solution.py:426
  5.0 6.3 %collective-permute-done = f32[1,2,32,512]{3,2,1,0:T(8,128)S(1)} collective-permute-done((f32[1,2,32,512]{3,2,1,0:T(8,128)S(1)}, f32[1,2,32,512]{3,2,1,0:T(8,128)S(1)}, u32[]{:S(2)}, u32[]{:S(2)}) %collective-permute-start) | collective-permute-done | bytes 131104 | tf_op jit(solution)/shard_map/ppermute | solution.py:426
  12.2 6.7 %collective-permute-done.1 = f32[2,2,32,512]{3,2,1,0:T(8,128)S(1)} collective-permute-done((f32[2,2,32,512]{3,2,1,0:T(8,128)S(1)}, f32[2,2,32,512]{3,2,1,0:T(8,128)S(1)}, u32[]{:S(2)}, u32[]{:S(2)}) %collective-permute-start.1) | collective-permute-done | bytes 262176 | tf_op jit(solution)/shard_map/ppermute | solution.py:426
  19.0 1.3 collective-permute-start.2
  20.3 1.5 collective-permute-start.3
  23.3 0.9 constant_dynamic-update-slice_fusion.4
  24.2 7.1 %collective-permute-done.2 = f32[4,2,32,512]{3,2,1,0:T(8,128)S(1)} collective-permute-done((f32[4,2,32,512]{3,2,1,0:T(8,128)S(1)}, f32[4,2,32,512]{3,2,1,0:T(8,128)S(1)}, u32[]{:S(2)}, u32[]{:S(2)}) %collective-permute-start.2) | collective-permute-done | bytes 524320 | tf_op jit(solution)/shard_map/ppermute | solution.py:426
  31.3 1.3 collective-permute-start.4
  33.0 1.2 collective-permute-start.5
  34.2 1.1 constant_dynamic-update-slice_fusion.3
  35.3 1.1 constant_dynamic-update-slice_fusion.2
  36.4 1.4 collective-permute-done.4
  37.9 0.9 constant_dynamic-update-slice_fusion.1
  39.5 0.9 constant_dynamic-update-slice_fusion
  41.6 2.2 copy-done
  44.1 1.5 shard_map.83
  45.7 2.2 copy-done.1
  49.1 3.7 %shard_map.87 = (f32[256,512]{1,0:T(8,128)S(1)}, f32[256,512]{1,0:T(8,128)S(1)}) custom-call(s32[5]{0:T(128)S(1)} %stack.20.at_ref, s32[4]{0:T(128)S(1)} %copy-done.10, s32[1,4096]{1,0:T(1,128)S(1)} %bitcast.49, f32[256,256]{1,0:T(8,128)S(1)} %get-tuple-element.54.refs_0_.refs_1_, f32[256,256]{1,0:T(8,128)S(1)} %get-tuple-element.55.refs_1_.refs_2_, ...), custom_call_target="tpu_custom_call" | custom-call | flops 2147483648 | bytes 4194304 | tf_op jit(solution)/shard_map/pallas_call | solution.py:252
  53.4 1.5 collective-permute-done.7
  55.0 1.2 collective-permute-start.8
  56.2 7.4 %collective-permute-done.8 = f32[256,256]{1,0:T(8,128)S(1)} collective-permute-done((f32[256,256]{1,0:T(8,128)S(1)}, f32[256,256]{1,0:T(8,128)S(1)}, u32[]{:S(2)}, u32[]{:S(2)}) %collective-permute-start.8) | collective-permute-done | bytes 262176 | tf_op jit(solution)/shard_map/ppermute | solution.py:426
  63.7 1.5 constant_dynamic-update-slice_fusion.7.bank_ref
  65.2 6.8 %shard_map.88 = (f32[256,128]{1,0:T(8,128)S(1)}, f32[256,128]{1,0:T(8,128)S(1)}, f32[512,128]{1,0:T(8,128)S(1)}) custom-call(s32[5]{0:T(128)S(1)} %stack.20.at_ref, f32[32,2,32,512]{3,2,1,0:T(8,128)} %constant_dynamic-update-slice_fusion.7.bank_ref, f32[2,256,512]{2,1,0:T(8,128)S(1)} %copy-done.7, f32[2,512,512]{2,1,0:T(8,128)S(1)} %copy-done.2, ...), custom_call_target="tpu_custom_call" | custom-call | flops 2013265920 | bytes 4194304 | tf_op jit(solution)/shard_map/pallas_call | solution.py:302
  72.0 2.2 collective-permute-start.9
  74.2 0.9 convert_reduce_fusion
  75.3 4.1 %collective-permute-start.22 = (f32[256,128]{1,0:T(8,128)S(1)}, f32[256,128]{1,0:T(8,128)S(1)}, u32[]{:S(2)}, u32[]{:S(2)}) collective-permute-start(f32[256,128]{1,0:T(8,128)S(1)} %get-tuple-element.61.refs_7_.refs_2_), channel_id=1, source_target_pairs={{0,8},{4,12},{8,0},{12,4},{1,9},{5,13},{9,1},{13,5},{2,10},{6,14},... | collective-permute-start | bytes 393224 | tf_op jit(solution)/shard_map/ppermute | solution.py:426
  79.4 1.3 collective-permute-start.33
  80.7 4.8 %collective-permute-done.9 = f32[512,128]{1,0:T(8,128)S(1)} collective-permute-done((f32[512,128]{1,0:T(8,128)S(1)}, f32[512,128]{1,0:T(8,128)S(1)}, u32[]{:S(2)}, u32[]{:S(2)}) %collective-permute-start.9) | collective-permute-done | bytes 262176 | tf_op jit(solution)/shard_map/ppermute | solution.py:426
  85.5 4.5 %collective-permute-start.35 = (f32[256,256]{1,0:T(8,128)S(1)}, f32[256,256]{1,0:T(8,128)S(1)}, u32[]{:S(2)}, u32[]{:S(2)}) collective-permute-start(f32[256,256]{1,0:T(8,128)S(1)} %get-tuple-element.56.refs_2_.refs_3_), channel_id=1, source_target_pairs={{0,12},{4,8},{8,4},{12,0},{1,13},{5,9},{9,5},{13,1},{2,14},{6,10},... | collective-permute-start | bytes 786440 | tf_op jit(solution)/shard_map/ppermute | solution.py:426
  90.0 1.8 collective-permute-done.21.refs_1_
  91.8 3.2 %collective-permute-start.10 = (f32[112,256]{0,1:T(8,128)S(1)}, f32[112,256]{0,1:T(8,128)S(1)}, u32[]{:S(2)}, u32[]{:S(2)}) collective-permute-start(f32[112,256]{0,1:T(8,128)S(1)} %bitcast.54), channel_id=1, source_target_pairs={{0,8},{4,12},{8,0},{12,4},{1,9},{5,13},{9,1},{13,5},{2,10},{6,14},... | collective-permute-start | bytes 344072 | tf_op jit(solution)/shard_map/ppermute | solution.py:426
  95.0 5.1 %shard_map.90 = (bf16[512,1024]{1,0:T(8,128)(2,1)S(1)}, bf16[512,1024]{1,0:T(8,128)(2,1)S(1)}, bf16[1024,512]{1,0:T(8,128)(2,1)S(1)}, bf16[1024,512]{1,0:T(8,128)(2,1)S(1)}) custom-call(s32[5]{0:T(128)S(1)} %stack.20.at_ref, f32[32,2,32,512]{3,2,1,0:T(8,128)} %constant_dynamic-update-slice_fusion.7.bank_ref, f32[2,512,512]{2,1,0:T(8,128)S(1)} %copy-done.2), custom_call_target="tpu_custom_call" | custom-call | flops 1610612736 | bytes 6291456 | tf_op jit(solution)/shard_map/pallas_call | solution.py:122
  100.1 2.7 collective-permute-start.27
  102.8 3.5 %collective-permute-start.28 = (f32[256,512]{1,0:T(8,128)S(1)}, f32[256,512]{1,0:T(8,128)S(1)}, u32[]{:S(2)}, u32[]{:S(2)}) collective-permute-start(f32[256,512]{1,0:T(8,128)S(1)} %get-tuple-element.58.refs_4_.refs_2_), channel_id=1, source_target_pairs={{0,8},{4,12},{8,0},{12,4},{1,9},{5,13},{9,1},{13,5},{2,10},{6,14},... | collective-permute-start | bytes 1572872 | tf_op jit(solution)/shard_map/ppermute | solution.py:426
  106.3 9.7 %collective-permute-done.10 = f32[112,256]{0,1:T(8,128)S(1)} collective-permute-done((f32[112,256]{0,1:T(8,128)S(1)}, f32[112,256]{0,1:T(8,128)S(1)}, u32[]{:S(2)}, u32[]{:S(2)}) %collective-permute-start.10) | collective-permute-done | bytes 114720 | tf_op jit(solution)/shard_map/ppermute | solution.py:426
  116.0 2.5 collective-permute-start.29
  118.6 1.4 collective-permute-start.23
  119.9 1.5 collective-permute-start.11
  121.4 3.4 %shard_map.96 = (f32[256,256]{1,0:T(8,128)S(1)}, f32[256,256]{1,0:T(8,128)S(1)}, f32[256,256]{1,0:T(8,128)S(1)}, f32[256,256]{1,0:T(8,128)S(1)}) custom-call(bf16[512,1024]{1,0:T(8,128)(2,1)S(1)} %get-tuple-element.75.first_high, bf16[512,1024]{1,0:T(8,128)(2,1)S(1)} %get-tuple-element.76.first_low, bf16[1024,512]{1,0:T(8,128)(2,1)S(1)} %get-tuple-element.77.second_high, ...), custom_call_target="tpu_custom_call" | custom-call | flops 1610612736 | bytes 2097152 | tf_op jit(solution)/shard_map/pallas_call | solution.py:159
  124.8 20.6 %collective-permute-done.23.refs_3_ = f32[256,128]{1,0:T(8,128)S(1)} collective-permute-done((f32[256,128]{1,0:T(8,128)S(1)}, f32[256,128]{1,0:T(8,128)S(1)}, u32[]{:S(2)}, u32[]{:S(2)}) %collective-permute-start.23) | collective-permute-done | bytes 131104 | tf_op jit(solution)/shard_map/ppermute | solution.py:426
  145.5 20.5 %collective-permute-start.15 = (f32[256,128]{1,0:T(8,128)S(1)}, f32[256,128]{1,0:T(8,128)S(1)}, u32[]{:S(2)}, u32[]{:S(2)}) collective-permute-start(f32[256,128]{1,0:T(8,128)S(1)} %get-tuple-element.63.refs_9_.refs_1_), channel_id=1, source_target_pairs={{0,4},{4,0},{8,12},{12,8},{1,5},{5,1},{9,13},{13,9},{2,6},{6,2},{1... | collective-permute-start | bytes 393224 | tf_op jit(solution)/shard_map/ppermute | solution.py:426
  165.9 3.5 %shard_map.93 = (f32[256,128]{1,0:T(8,128)S(1)}, f32[256,128]{1,0:T(8,128)S(1)}, f32[256,128]{1,0:T(8,128)S(1)}, f32[256,128]{1,0:T(8,128)S(1)}) custom-call(bf16[512,1024]{1,0:T(8,128)(2,1)S(1)} %get-tuple-element.75.first_high, bf16[512,1024]{1,0:T(8,128)(2,1)S(1)} %get-tuple-element.76.first_low, bf16[1024,512]{1,0:T(8,128)(2,1)S(1)} %get-tuple-element.77.second_high, ...), custom_call_target="tpu_custom_call" | custom-call | flops 805306368 | bytes 1048576 | tf_op jit(solution)/shard_map/pallas_call | solution.py:159
  169.4 1.5 collective-permute-start.14
  171.0 2.2 collective-permute-done.14
  173.2 1.4 collective-permute-start.16
  174.6 1.5 collective-permute-start.17
  176.7 1.4 collective-permute-start.36
  178.1 7.4 %shard_map.95 = (f32[256,512]{1,0:T(8,128)S(1)}, f32[256,512]{1,0:T(8,128)S(1)}, f32[256,512]{1,0:T(8,128)S(1)}, f32[256,512]{1,0:T(8,128)S(1)}) custom-call(bf16[512,1024]{1,0:T(8,128)(2,1)S(1)} %get-tuple-element.75.first_high, bf16[512,1024]{1,0:T(8,128)(2,1)S(1)} %get-tuple-element.76.first_low, bf16[1024,512]{1,0:T(8,128)(2,1)S(1)} %get-tuple-element.77.second_high, ...), custom_call_target="tpu_custom_call" | custom-call | flops 3221225472 | bytes 4194304 | tf_op jit(solution)/shard_map/pallas_call | solution.py:159
  186.3 2.3 collective-permute-start.31
  188.6 1.5 collective-permute-start.32
  190.0 11.3 %collective-permute-done.36.refs_5_ = f32[256,256]{1,0:T(8,128)S(1)} collective-permute-done((f32[256,256]{1,0:T(8,128)S(1)}, f32[256,256]{1,0:T(8,128)S(1)}, u32[]{:S(2)}, u32[]{:S(2)}) %collective-permute-start.36) | collective-permute-done | bytes 262176 | tf_op jit(solution)/shard_map/ppermute | solution.py:426
  201.4 1.9 collective-permute-start.38
  203.3 3.5 %shard_map.91 = (f32[256,128]{1,0:T(8,128)S(1)}, f32[256,128]{1,0:T(8,128)S(1)}, f32[256,128]{1,0:T(8,128)S(1)}, f32[256,128]{1,0:T(8,128)S(1)}) custom-call(bf16[512,1024]{1,0:T(8,128)(2,1)S(1)} %get-tuple-element.75.first_high, bf16[512,1024]{1,0:T(8,128)(2,1)S(1)} %get-tuple-element.76.first_low, bf16[1024,512]{1,0:T(8,128)(2,1)S(1)} %get-tuple-element.77.second_high, ...), custom_call_target="tpu_custom_call" | custom-call | flops 805306368 | bytes 1048576 | tf_op jit(solution)/shard_map/pallas_call | solution.py:159
  207.4 45.1 %collective-permute-done.37.refs_6_ = f32[256,256]{1,0:T(8,128)S(1)} collective-permute-done((f32[256,256]{1,0:T(8,128)S(1)}, f32[256,256]{1,0:T(8,128)S(1)}, u32[]{:S(2)}, u32[]{:S(2)}) %collective-permute-start.37) | collective-permute-done | bytes 262176 | tf_op jit(solution)/shard_map/ppermute | solution.py:426
  252.6 2.8 %collective-permute-start.26 = (f32[256,128]{1,0:T(8,128)S(1)}, f32[256,128]{1,0:T(8,128)S(1)}, u32[]{:S(2)}, u32[]{:S(2)}) collective-permute-start(f32[256,128]{1,0:T(8,128)S(1)} %get-tuple-element.94), channel_id=1, source_target_pairs={{0,12},{4,8},{8,4},{12,0},{1,13},{5,9},{9,5},{13,1},{2,14},{6,10},... | collective-permute-start | bytes 393224 | tf_op jit(solution)/shard_map/ppermute | solution.py:426
  255.4 3.0 %shard_map.97.refs_10_ = f32[256,4096]{1,0:T(8,128)} custom-call(s32[5]{0:T(128)S(1)} %stack.20.at_ref, f32[256,256]{1,0:T(8,128)S(1)} %get-tuple-element.66.refs_12_.refs_0_, f32[256,256]{1,0:T(8,128)S(1)} %get-tuple-element.54.refs_0_.refs_1_, f32[256,256]{1,0:T(8,128)S(1)} %get-tuple-element.55.refs_1_.refs_2_, ...), custom_call_target="tpu_custom_call" | custom-call | flops 536870912 | bytes 3145728 | tf_op jit(solution)/shard_map/pallas_call | solution.py:375
  258.5 10.9 %collective-permute-start.18 = (f32[256,128]{1,0:T(8,128)S(1)}, f32[256,128]{1,0:T(8,128)S(1)}, u32[]{:S(2)}, u32[]{:S(2)}) collective-permute-start(f32[256,128]{1,0:T(8,128)S(1)} %get-tuple-element.84), channel_id=1, source_target_pairs={{0,4},{4,0},{8,12},{12,8},{1,5},{5,1},{9,13},{13,9},{2,6},{6,2},{1... | collective-permute-start | bytes 393224 | tf_op jit(solution)/shard_map/ppermute | solution.py:426
  269.4 2.4 collective-permute-start.20
  271.8 1.3 shard_map.94
  273.1 3.8 %shard_map.98.refs_7_ = f32[256,4096]{1,0:T(8,128)} custom-call(s32[5]{0:T(128)S(1)} %stack.20.at_ref, f32[256,512]{1,0:T(8,128)S(1)} %get-tuple-element.67.refs_13_.refs_0_, f32[256,512]{1,0:T(8,128)S(1)} %get-tuple-element.57.refs_3_.refs_1_, f32[256,512]{1,0:T(8,128)S(1)} %get-tuple-element.58.refs_4_.refs_2_, ...), custom_call_target="tpu_custom_call", output_to_operand_aliasing={{}: (11, {})} | custom-call | flops 1073741824 | bytes 6291456 | tf_op jit(solution)/shard_map/pallas_call | solution.py:375
  276.9 1.4 shard_map.99.refs_7_
  278.2 1.3 shard_map.92
  280.3 1.4 shard_map.100
  (82 shorter events, 10.0 us)
Async XLA Ops:
  0.9 10.4 %collective-permute-start = (f32[1,2,32,512]{3,2,1,0:T(8,128)S(1)}, f32[1,2,32,512]{3,2,1,0:T(8,128)S(1)}, u32[]{:S(2)}, u32[]{:S(2)}) collective-permute-start(f32[1,2,32,512]{3,2,1,0:T(8,128)S(1)} %shard_map.82), channel_id=1, source_target_pairs={{0,8},{4,12},{8,0},{12,4},{1,9},{5,13},{9,1},{13,5},{2,10},{6,14},... | collective-permute-start | bytes 393224 | tf_op jit(solution)/shard_map/ppermute | solution.py:426
  11.4 28.9 %copy-start.10 = (s32[4]{0:T(128)S(1)}, s32[4]{0:T(128)}, u32[]{:S(2)}) copy-start(s32[4]{0:T(128)} %index_ref.1) | copy-start | bytes 52
  11.4 30.2 %copy-start.3 = (s32[4096]{0:T(1024)S(1)}, s32[4096]{0:T(1024)}, u32[]{:S(2)}) copy-start(s32[4096]{0:T(1024)} %param.10) | copy-start | bytes 49156
  11.4 30.2 %copy-start.5 = (f32[4096]{0:T(1024)S(1)}, f32[4096]{0:T(1024)}, u32[]{:S(2)}) copy-start(f32[4096]{0:T(1024)} %param.11) | copy-start | bytes 49156
  11.4 30.1 %copy-start.8 = (f32[256,64]{0,1:T(8,128)S(1)}, f32[256,64]{0,1:T(8,128)}, u32[]{:S(2)}) copy-start(f32[256,64]{0,1:T(8,128)} %param.9) | copy-start | bytes 196612
  11.4 7.5 %collective-permute-start.1 = (f32[2,2,32,512]{3,2,1,0:T(8,128)S(1)}, f32[2,2,32,512]{3,2,1,0:T(8,128)S(1)}, u32[]{:S(2)}, u32[]{:S(2)}) collective-permute-start(f32[2,2,32,512]{3,2,1,0:T(8,128)S(1)} %pad_maximum_fusion.1), channel_id=1, source_target_pairs={{0,4},{4,0},{8,12},{12,8},{1,5},{5,1},{9,13},{13,9},{2,6},{6,2},{1... | collective-permute-start | bytes 786440 | tf_op jit(solution)/shard_map/ppermute | solution.py:426
  19.0 12.3 %collective-permute-start.2 = (f32[4,2,32,512]{3,2,1,0:T(8,128)S(1)}, f32[4,2,32,512]{3,2,1,0:T(8,128)S(1)}, u32[]{:S(2)}, u32[]{:S(2)}) collective-permute-start(f32[4,2,32,512]{3,2,1,0:T(8,128)S(1)} %pad_maximum_fusion), channel_id=1, source_target_pairs={{0,2},{1,3},{2,0},{3,1},{4,6},{5,7},{6,4},{7,5},{8,10},{9,11},{10,... | collective-permute-start | bytes 1572872 | tf_op jit(solution)/shard_map/ppermute | solution.py:426
  20.3 12.7 %collective-permute-start.3 = (f32[4,2,32,512]{3,2,1,0:T(8,128)S(1)}, f32[4,2,32,512]{3,2,1,0:T(8,128)S(1)}, u32[]{:S(2)}, u32[]{:S(2)}) collective-permute-start(f32[4,2,32,512]{3,2,1,0:T(8,128)S(1)} %pad_maximum_fusion), channel_id=1, source_target_pairs={{0,16},{16,0},{1,17},{17,1},{2,18},{18,2},{3,19},{19,3},{4,20},{20... | collective-permute-start | bytes 1572872 | tf_op jit(solution)/shard_map/ppermute | solution.py:426
  31.3 6.6 %collective-permute-start.4 = (f32[2,2,32,512]{3,2,1,0:T(8,128)S(1)}, f32[2,2,32,512]{3,2,1,0:T(8,128)S(1)}, u32[]{:S(2)}, u32[]{:S(2)}) collective-permute-start(f32[2,2,32,512]{3,2,1,0:T(8,128)S(1)} %slice.28), channel_id=1, source_target_pairs={{0,16},{16,0},{1,17},{17,1},{2,18},{18,2},{3,19},{19,3},{4,20},{20... | collective-permute-start | bytes 786440 | tf_op jit(solution)/shard_map/ppermute | solution.py:426
  33.0 6.4 %collective-permute-start.5 = (f32[2,2,32,512]{3,2,1,0:T(8,128)S(1)}, f32[2,2,32,512]{3,2,1,0:T(8,128)S(1)}, u32[]{:S(2)}, u32[]{:S(2)}) collective-permute-start(f32[2,2,32,512]{3,2,1,0:T(8,128)S(1)} %slice.29), channel_id=1, source_target_pairs={{0,2},{1,3},{2,0},{3,1},{4,6},{5,7},{6,4},{7,5},{8,10},{9,11},{10,... | collective-permute-start | bytes 786440 | tf_op jit(solution)/shard_map/ppermute | solution.py:426
  40.3 23.4 %collective-permute-start.6 = (f32[16,2,32,512]{3,2,1,0:T(8,128)}, f32[16,2,32,512]{3,2,1,0:T(8,128)S(1)}, u32[]{:S(2)}, u32[]{:S(2)}) collective-permute-start(f32[16,2,32,512]{3,2,1,0:T(8,128)} %get-tuple-element.107), channel_id=1, source_target_pairs={{0,1},{1,0},{2,3},{3,2},{4,5},{5,4},{6,7},{7,6},{8,9},{9,8},{10,11... | collective-permute-start | bytes 6291464 | tf_op jit(solution)/shard_map/ppermute | solution.py:426
  41.6 2.2 copy-start
  44.1 1.6 copy-start.4
  44.1 1.6 copy-start.6
  44.1 1.6 copy-start.9
  45.7 2.2 copy-start.1
  48.3 0.7 copy-start.11
  52.7 12.5 %copy-start.2 = (f32[2,512,512]{2,1,0:T(8,128)S(1)}, f32[2,512,512]{2,1,0:T(8,128)}, u32[]{:S(2)}) copy-start(f32[2,512,512]{2,1,0:T(8,128)} %mix_ref.3) | copy-start | bytes 6291460
  52.8 12.5 %copy-start.7 = (f32[2,256,512]{2,1,0:T(8,128)S(1)}, f32[2,256,512]{2,1,0:T(8,128)}, u32[]{:S(2)}) copy-start(f32[2,256,512]{2,1,0:T(8,128)} %own_ref.1) | copy-start | bytes 3145732
  52.8 2.1 collective-permute-start.7
  55.0 8.7 %collective-permute-start.8 = (f32[256,256]{1,0:T(8,128)S(1)}, f32[256,256]{1,0:T(8,128)S(1)}, u32[]{:S(2)}, u32[]{:S(2)}) collective-permute-start(f32[256,256]{1,0:T(8,128)S(1)} %slice.31), channel_id=1, source_target_pairs={{0,2},{1,3},{2,0},{3,1},{4,6},{5,7},{6,4},{7,5},{8,10},{9,11},{10,... | collective-permute-start | bytes 786440 | tf_op jit(solution)/shard_map/ppermute | solution.py:426
  72.0 13.5 %collective-permute-start.9 = (f32[512,128]{1,0:T(8,128)S(1)}, f32[512,128]{1,0:T(8,128)S(1)}, u32[]{:S(2)}, u32[]{:S(2)}) collective-permute-start(f32[512,128]{1,0:T(8,128)S(1)} %get-tuple-element.73), channel_id=1, source_target_pairs={{0,4},{4,0},{8,12},{12,8},{1,5},{5,1},{9,13},{13,9},{2,6},{6,2},{1... | collective-permute-start | bytes 786440 | tf_op jit(solution)/shard_map/ppermute | solution.py:426
  75.2 5.6 %collective-permute-start.13 = (f32[8,512]{1,0:T(8,128)S(1)}, f32[8,512]{1,0:T(8,128)S(1)}, u32[]{:S(2)}, u32[]{:S(2)}) collective-permute-start(f32[8,512]{1,0:T(8,128)S(1)} %broadcast_in_dim.8), channel_id=1, source_target_pairs={{0,1},{1,0},{2,3},{3,2},{4,5},{5,4},{6,7},{7,6},{8,9},{9,8},{10,11... | collective-permute-start | bytes 49160 | tf_op jit(solution)/shard_map/ppermute | solution.py:426
  75.2 16.6 %collective-permute-start.21 = (f32[256,128]{1,0:T(8,128)S(1)}, f32[256,128]{1,0:T(8,128)S(1)}, u32[]{:S(2)}, u32[]{:S(2)}) collective-permute-start(f32[256,128]{1,0:T(8,128)S(1)} %get-tuple-element.60.refs_6_.refs_1_), channel_id=1, source_target_pairs={{0,4},{4,0},{8,12},{12,8},{1,5},{5,1},{9,13},{13,9},{2,6},{6,2},{1... | collective-permute-start | bytes 393224 | tf_op jit(solution)/shard_map/ppermute | solution.py:426
  75.3 24.8 %collective-permute-start.22 = (f32[256,128]{1,0:T(8,128)S(1)}, f32[256,128]{1,0:T(8,128)S(1)}, u32[]{:S(2)}, u32[]{:S(2)}) collective-permute-start(f32[256,128]{1,0:T(8,128)S(1)} %get-tuple-element.61.refs_7_.refs_2_), channel_id=1, source_target_pairs={{0,8},{4,12},{8,0},{12,4},{1,9},{5,13},{9,1},{13,5},{2,10},{6,14},... | collective-permute-start | bytes 393224 | tf_op jit(solution)/shard_map/ppermute | solution.py:426
  79.4 23.4 %collective-permute-start.33 = (f32[256,256]{1,0:T(8,128)S(1)}, f32[256,256]{1,0:T(8,128)S(1)}, u32[]{:S(2)}, u32[]{:S(2)}) collective-permute-start(f32[256,256]{1,0:T(8,128)S(1)} %get-tuple-element.54.refs_0_.refs_1_), channel_id=1, source_target_pairs={{0,4},{4,0},{8,12},{12,8},{1,5},{5,1},{9,13},{13,9},{2,6},{6,2},{1... | collective-permute-start | bytes 786440 | tf_op jit(solution)/shard_map/ppermute | solution.py:426
  80.7 37.8 %collective-permute-start.34 = (f32[256,256]{1,0:T(8,128)S(1)}, f32[256,256]{1,0:T(8,128)S(1)}, u32[]{:S(2)}, u32[]{:S(2)}) collective-permute-start(f32[256,256]{1,0:T(8,128)S(1)} %get-tuple-element.55.refs_1_.refs_2_), channel_id=1, source_target_pairs={{0,8},{4,12},{8,0},{12,4},{1,9},{5,13},{9,1},{13,5},{2,10},{6,14},... | collective-permute-start | bytes 786440 | tf_op jit(solution)/shard_map/ppermute | solution.py:426
  85.5 34.4 %collective-permute-start.35 = (f32[256,256]{1,0:T(8,128)S(1)}, f32[256,256]{1,0:T(8,128)S(1)}, u32[]{:S(2)}, u32[]{:S(2)}) collective-permute-start(f32[256,256]{1,0:T(8,128)S(1)} %get-tuple-element.56.refs_2_.refs_3_), channel_id=1, source_target_pairs={{0,12},{4,8},{8,4},{12,0},{1,13},{5,9},{9,5},{13,1},{2,14},{6,10},... | collective-permute-start | bytes 786440 | tf_op jit(solution)/shard_map/ppermute | solution.py:426
  91.8 24.2 %collective-permute-start.10 = (f32[112,256]{0,1:T(8,128)S(1)}, f32[112,256]{0,1:T(8,128)S(1)}, u32[]{:S(2)}, u32[]{:S(2)}) collective-permute-start(f32[112,256]{0,1:T(8,128)S(1)} %bitcast.54), channel_id=1, source_target_pairs={{0,8},{4,12},{8,0},{12,4},{1,9},{5,13},{9,1},{13,5},{2,10},{6,14},... | collective-permute-start | bytes 344072 | tf_op jit(solution)/shard_map/ppermute | solution.py:426
  100.1 75.9 %collective-permute-start.27 = (f32[256,512]{1,0:T(8,128)S(1)}, f32[256,512]{1,0:T(8,128)S(1)}, u32[]{:S(2)}, u32[]{:S(2)}) collective-permute-start(f32[256,512]{1,0:T(8,128)S(1)} %get-tuple-element.57.refs_3_.refs_1_), channel_id=1, source_target_pairs={{0,4},{4,0},{8,12},{12,8},{1,5},{5,1},{9,13},{13,9},{2,6},{6,2},{1... | collective-permute-start | bytes 1572872 | tf_op jit(solution)/shard_map/ppermute | solution.py:426
  102.8 73.9 %collective-permute-start.28 = (f32[256,512]{1,0:T(8,128)S(1)}, f32[256,512]{1,0:T(8,128)S(1)}, u32[]{:S(2)}, u32[]{:S(2)}) collective-permute-start(f32[256,512]{1,0:T(8,128)S(1)} %get-tuple-element.58.refs_4_.refs_2_), channel_id=1, source_target_pairs={{0,8},{4,12},{8,0},{12,4},{1,9},{5,13},{9,1},{13,5},{2,10},{6,14},... | collective-permute-start | bytes 1572872 | tf_op jit(solution)/shard_map/ppermute | solution.py:426
  116.0 62.1 %collective-permute-start.29 = (f32[256,512]{1,0:T(8,128)S(1)}, f32[256,512]{1,0:T(8,128)S(1)}, u32[]{:S(2)}, u32[]{:S(2)}) collective-permute-start(f32[256,512]{1,0:T(8,128)S(1)} %get-tuple-element.59.refs_5_.refs_3_), channel_id=1, source_target_pairs={{0,12},{4,8},{8,4},{12,0},{1,13},{5,9},{9,5},{13,1},{2,14},{6,10},... | collective-permute-start | bytes 1572872 | tf_op jit(solution)/shard_map/ppermute | solution.py:426
  118.6 26.9 %collective-permute-start.23 = (f32[256,128]{1,0:T(8,128)S(1)}, f32[256,128]{1,0:T(8,128)S(1)}, u32[]{:S(2)}, u32[]{:S(2)}) collective-permute-start(f32[256,128]{1,0:T(8,128)S(1)} %get-tuple-element.62.refs_8_.refs_3_), channel_id=1, source_target_pairs={{0,12},{4,8},{8,4},{12,0},{1,13},{5,9},{9,5},{13,1},{2,14},{6,10},... | collective-permute-start | bytes 393224 | tf_op jit(solution)/shard_map/ppermute | solution.py:426
  119.9 49.4 %collective-permute-start.11 = (f32[256,128]{1,0:T(8,128)S(1)}, f32[256,128]{1,0:T(8,128)S(1)}, u32[]{:S(2)}, u32[]{:S(2)}) collective-permute-start(f32[256,128]{1,0:T(8,128)S(1)} %fusion.1), channel_id=1, source_target_pairs={{0,2},{1,3},{2,0},{3,1},{4,6},{5,7},{6,4},{7,5},{8,10},{9,11},{10,... | collective-permute-start | bytes 393224 | tf_op jit(solution)/shard_map/ppermute | solution.py:426
  145.5 29.1 %collective-permute-start.15 = (f32[256,128]{1,0:T(8,128)S(1)}, f32[256,128]{1,0:T(8,128)S(1)}, u32[]{:S(2)}, u32[]{:S(2)}) collective-permute-start(f32[256,128]{1,0:T(8,128)S(1)} %get-tuple-element.63.refs_9_.refs_1_), channel_id=1, source_target_pairs={{0,4},{4,0},{8,12},{12,8},{1,5},{5,1},{9,13},{13,9},{2,6},{6,2},{1... | collective-permute-start | bytes 393224 | tf_op jit(solution)/shard_map/ppermute | solution.py:426
  169.4 3.8 %collective-permute-start.14 = (f32[8,512]{1,0:T(8,128)S(1)}, f32[8,512]{1,0:T(8,128)S(1)}, u32[]{:S(2)}, u32[]{:S(2)}) collective-permute-start(f32[8,512]{1,0:T(8,128)S(1)} %broadcast_add_fusion), channel_id=1, source_target_pairs={{0,2},{1,3},{2,0},{3,1},{4,6},{5,7},{6,4},{7,5},{8,10},{9,11},{10,... | collective-permute-start | bytes 49160 | tf_op jit(solution)/shard_map/ppermute | solution.py:426
  173.2 12.3 %collective-permute-start.16 = (f32[256,128]{1,0:T(8,128)S(1)}, f32[256,128]{1,0:T(8,128)S(1)}, u32[]{:S(2)}, u32[]{:S(2)}) collective-permute-start(f32[256,128]{1,0:T(8,128)S(1)} %get-tuple-element.64.refs_10_.refs_2_), channel_id=1, source_target_pairs={{0,8},{4,12},{8,0},{12,4},{1,9},{5,13},{9,1},{13,5},{2,10},{6,14},... | collective-permute-start | bytes 393224 | tf_op jit(solution)/shard_map/ppermute | solution.py:426
  174.6 11.7 %collective-permute-start.17 = (f32[256,128]{1,0:T(8,128)S(1)}, f32[256,128]{1,0:T(8,128)S(1)}, u32[]{:S(2)}, u32[]{:S(2)}) collective-permute-start(f32[256,128]{1,0:T(8,128)S(1)} %get-tuple-element.65.refs_11_.refs_3_), channel_id=1, source_target_pairs={{0,12},{4,8},{8,4},{12,0},{1,13},{5,9},{9,5},{13,1},{2,14},{6,10},... | collective-permute-start | bytes 393224 | tf_op jit(solution)/shard_map/ppermute | solution.py:426
  176.0 12.5 %collective-permute-start.24 = (f32[256,128]{1,0:T(8,128)S(1)}, f32[256,128]{1,0:T(8,128)S(1)}, u32[]{:S(2)}, u32[]{:S(2)}) collective-permute-start(f32[256,128]{1,0:T(8,128)S(1)} %get-tuple-element.92), channel_id=1, source_target_pairs={{0,4},{4,0},{8,12},{12,8},{1,5},{5,1},{9,13},{13,9},{2,6},{6,2},{1... | collective-permute-start | bytes 393224 | tf_op jit(solution)/shard_map/ppermute | solution.py:426
  176.7 24.6 %collective-permute-start.36 = (f32[256,256]{1,0:T(8,128)S(1)}, f32[256,256]{1,0:T(8,128)S(1)}, u32[]{:S(2)}, u32[]{:S(2)}) collective-permute-start(f32[256,256]{1,0:T(8,128)S(1)} %get-tuple-element.100), channel_id=1, source_target_pairs={{0,4},{4,0},{8,12},{12,8},{1,5},{5,1},{9,13},{13,9},{2,6},{6,2},{1... | collective-permute-start | bytes 786440 | tf_op jit(solution)/shard_map/ppermute | solution.py:426
  178.1 23.3 %collective-permute-start.12 = (f32[256,256]{1,0:T(8,128)S(1)}, f32[256,256]{1,0:T(8,128)S(1)}, u32[]{:S(2)}, u32[]{:S(2)}) collective-permute-start(f32[256,256]{1,0:T(8,128)S(1)} %pad_maximum_fusion.2.here_ref), channel_id=1, source_target_pairs={{0,1},{1,0},{2,3},{3,2},{4,5},{5,4},{6,7},{7,6},{8,9},{9,8},{10,11... | collective-permute-start | bytes 786440 | tf_op jit(solution)/shard_map/ppermute | solution.py:426
  185.6 72.9 %collective-permute-start.30 = (f32[256,512]{1,0:T(8,128)S(1)}, f32[256,512]{1,0:T(8,128)S(1)}, u32[]{:S(2)}, u32[]{:S(2)}) collective-permute-start(f32[256,512]{1,0:T(8,128)S(1)} %get-tuple-element.96), channel_id=1, source_target_pairs={{0,4},{4,0},{8,12},{12,8},{1,5},{5,1},{9,13},{13,9},{2,6},{6,2},{1... | collective-permute-start | bytes 1572872 | tf_op jit(solution)/shard_map/ppermute | solution.py:426
  186.3 83.1 %collective-permute-start.31 = (f32[256,512]{1,0:T(8,128)S(1)}, f32[256,512]{1,0:T(8,128)S(1)}, u32[]{:S(2)}, u32[]{:S(2)}) collective-permute-start(f32[256,512]{1,0:T(8,128)S(1)} %get-tuple-element.97), channel_id=1, source_target_pairs={{0,8},{4,12},{8,0},{12,4},{1,9},{5,13},{9,1},{13,5},{2,10},{6,14},... | collective-permute-start | bytes 1572872 | tf_op jit(solution)/shard_map/ppermute | solution.py:426
  188.6 80.8 %collective-permute-start.32 = (f32[256,512]{1,0:T(8,128)S(1)}, f32[256,512]{1,0:T(8,128)S(1)}, u32[]{:S(2)}, u32[]{:S(2)}) collective-permute-start(f32[256,512]{1,0:T(8,128)S(1)} %get-tuple-element.98), channel_id=1, source_target_pairs={{0,12},{4,8},{8,4},{12,0},{1,13},{5,9},{9,5},{13,1},{2,14},{6,10},... | collective-permute-start | bytes 1572872 | tf_op jit(solution)/shard_map/ppermute | solution.py:426
  201.3 51.2 %collective-permute-start.37 = (f32[256,256]{1,0:T(8,128)S(1)}, f32[256,256]{1,0:T(8,128)S(1)}, u32[]{:S(2)}, u32[]{:S(2)}) collective-permute-start(f32[256,256]{1,0:T(8,128)S(1)} %get-tuple-element.101), channel_id=1, source_target_pairs={{0,8},{4,12},{8,0},{12,4},{1,9},{5,13},{9,1},{13,5},{2,10},{6,14},... | collective-permute-start | bytes 786440 | tf_op jit(solution)/shard_map/ppermute | solution.py:426
  201.4 51.2 %collective-permute-start.38 = (f32[256,256]{1,0:T(8,128)S(1)}, f32[256,256]{1,0:T(8,128)S(1)}, u32[]{:S(2)}, u32[]{:S(2)}) collective-permute-start(f32[256,256]{1,0:T(8,128)S(1)} %get-tuple-element.102), channel_id=1, source_target_pairs={{0,12},{4,8},{8,4},{12,0},{1,13},{5,9},{9,5},{13,1},{2,14},{6,10},... | collective-permute-start | bytes 786440 | tf_op jit(solution)/shard_map/ppermute | solution.py:426
  252.6 24.3 %collective-permute-start.25 = (f32[256,128]{1,0:T(8,128)S(1)}, f32[256,128]{1,0:T(8,128)S(1)}, u32[]{:S(2)}, u32[]{:S(2)}) collective-permute-start(f32[256,128]{1,0:T(8,128)S(1)} %get-tuple-element.93), channel_id=1, source_target_pairs={{0,8},{4,12},{8,0},{12,4},{1,9},{5,13},{9,1},{13,5},{2,10},{6,14},... | collective-permute-start | bytes 393224 | tf_op jit(solution)/shard_map/ppermute | solution.py:426
  252.6 24.3 %collective-permute-start.26 = (f32[256,128]{1,0:T(8,128)S(1)}, f32[256,128]{1,0:T(8,128)S(1)}, u32[]{:S(2)}, u32[]{:S(2)}) collective-permute-start(f32[256,128]{1,0:T(8,128)S(1)} %get-tuple-element.94), channel_id=1, source_target_pairs={{0,12},{4,8},{8,4},{12,0},{1,13},{5,9},{9,5},{13,1},{2,14},{6,10},... | collective-permute-start | bytes 393224 | tf_op jit(solution)/shard_map/ppermute | solution.py:426
  258.5 21.0 %collective-permute-start.18 = (f32[256,128]{1,0:T(8,128)S(1)}, f32[256,128]{1,0:T(8,128)S(1)}, u32[]{:S(2)}, u32[]{:S(2)}) collective-permute-start(f32[256,128]{1,0:T(8,128)S(1)} %get-tuple-element.84), channel_id=1, source_target_pairs={{0,4},{4,0},{8,12},{12,8},{1,5},{5,1},{9,13},{13,9},{2,6},{6,2},{1... | collective-permute-start | bytes 393224 | tf_op jit(solution)/shard_map/ppermute | solution.py:426
  269.4 10.9 %collective-permute-start.19 = (f32[256,128]{1,0:T(8,128)S(1)}, f32[256,128]{1,0:T(8,128)S(1)}, u32[]{:S(2)}, u32[]{:S(2)}) collective-permute-start(f32[256,128]{1,0:T(8,128)S(1)} %get-tuple-element.85), channel_id=1, source_target_pairs={{0,8},{4,12},{8,0},{12,4},{1,9},{5,13},{9,1},{13,5},{2,10},{6,14},... | collective-permute-start | bytes 393224 | tf_op jit(solution)/shard_map/ppermute | solution.py:426
  269.4 10.9 %collective-permute-start.20 = (f32[256,128]{1,0:T(8,128)S(1)}, f32[256,128]{1,0:T(8,128)S(1)}, u32[]{:S(2)}, u32[]{:S(2)}) collective-permute-start(f32[256,128]{1,0:T(8,128)S(1)} %get-tuple-element.86), channel_id=1, source_target_pairs={{0,12},{4,8},{8,4},{12,0},{1,13},{5,9},{9,5},{13,1},{2,14},{6,10},... | collective-permute-start | bytes 393224 | tf_op jit(solution)/shard_map/ppermute | solution.py:426
